TPU v7x, 512 devices: a whole 4x8x8 slice. The times are simulated.
512 devices in a mesh: grid: 64 (over y, z), col: 8 (over x, core).
Axes of the slice: x: 4, y: 8, z: 8, core: 2. Of those that a mesh axis runs over, the one named last changes fastest.
Arguments:
- density: bfloat16 [196608, 1024], P('grid', 'col'), may hold values from -0.029907227 to 0.029907227
- row_centers: float32 [3, 196608], P(None, 'grid'), may hold values from -2 to 2
- row_exps: float32 [196608], P('grid'), may hold values from 0.2 to 1
- win_centers: float32 [3, 1024], P(None, 'col'), may hold values from -2 to 2
- win_exps: float32 [1024], P('col'), may hold values from 0.2 to 1
- points: float32 [256, 3, 128], P('grid'), may hold values from -2 to 2
- weights: float32 [256, 128], P('grid'), may hold values from 0.05 to 0.5
- sig_blocks: int32 [256, 32], replicated, may hold values from 0 to 1535, as said below
- pair_target: int32 [256, 16384], P('grid', 'col'), may hold values from 0 to 1023
- pair_source: int32 [256, 16384], P('grid', 'col'), may hold values from 0 to 127
Outputs:
- fock: float32 [196608, 1024], P('grid', 'col')
Inputs may be any that keep to these rules, and one draw needn't show every extreme that they name: `sig_blocks`: each row lists 32 different blocks; block i is owned by grid index i // 24. Over the 4 rows of one grid index d (rows d * 4 to (d + 1) * 4 - 1, the batches that index holds), at most 2 different blocks of any one owner appear, and exactly 2 for some owner.
All inputs are finite; a program needn't handle non-finite values.
Results may differ from a plain program's by a relative error of at most 0.0011.
Values may be sent and summed in bfloat16 or wider, within the bound.
No kernel may reach another device: no remote copies, remote signals or barrier semaphores. Data moves between devices by JAX's collectives and lax.ppermute only.
A program may use at most 64 MiB of HBM per device.

v0:
```python
import math

import jax
import jax.numpy as jnp
from jax import lax
from jax.sharding import PartitionSpec as P

BLK = 128
CAPB = 2


quad_nodes = 8


def from_everyone(value, axis):
    devices = lax.axis_size(axis)
    return lax.all_to_all(
        jnp.broadcast_to(value[None], (devices, *value.shape)), axis, 0, 0, tiled=True
    )


def in_order(tiles, dim):
    dims = list(tiles.shape[1:])
    dims[dim] *= tiles.shape[0]
    return jnp.moveaxis(tiles, 0, dim).reshape(dims)


def gather_directly(value, axis, dim):
    tiles = from_everyone(value, axis)
    return in_order(tiles, dim)


def split_up(value, dim, devices):
    dims = value.shape
    tiles = value.reshape(*dims[:dim], devices, dims[dim] // devices, *dims[dim + 1 :])
    return jnp.moveaxis(tiles, dim, 0)


def sum_at_owner(value, axis, dim):
    devices = lax.axis_size(axis)
    tiles = lax.all_to_all(split_up(value, dim, devices), axis, 0, 0, tiled=True)
    return jnp.sum(tiles, axis=0)


def boys_zero(argument):
    summed = jnp.zeros_like(argument)
    for quad_node in range(quad_nodes):
        node_spot = (quad_node + 0.5) / quad_nodes
        summed = summed + jnp.exp(-argument * (node_spot * node_spot))
    return summed / quad_nodes


def basis_values(centers, exponents, coordinates):
    squared = None
    for axis_id in range(3):
        deltas = coordinates[..., axis_id, :, None] - centers[..., axis_id, None, :]
        squared = deltas * deltas if squared is None else squared + deltas * deltas
    return jnp.exp(-exponents[..., None, :] * squared)


def pair_values(target_par, source_par, coordinates):
    target_exp = target_par[..., 3, :]
    source_exp = source_par[..., 3, :]
    joined = target_exp + source_exp
    separation = jnp.zeros_like(joined)
    spread = None
    for axis_id in range(3):
        offset = target_par[..., axis_id, :] - source_par[..., axis_id, :]
        separation = separation + offset * offset
        centre = (
            target_exp * target_par[..., axis_id, :] + source_exp * source_par[..., axis_id, :]
        ) / joined
        deltas = coordinates[..., axis_id, :, None] - centre[..., None, :]
        spread = deltas * deltas if spread is None else spread + deltas * deltas
    prefactor = 2.0 * math.pi / joined * jnp.exp(-target_exp * source_exp / joined * separation)
    return prefactor[..., None, :] * boys_zero(joined[..., None, :] * spread)


def on_device(
    density,
    row_centers,
    row_exps,
    win_centers,
    win_exps,
    points,
    weights,
    sig_blocks,
    pair_target,
    pair_source,
):
    owners = lax.axis_size("grid")
    my_index = lax.axis_index("grid")
    held_blocks = row_exps.shape[0] // BLK
    local_width = density.shape[1]
    batches_here = points.shape[0]
    listed_count = sig_blocks.shape[1]
    own_ids = my_index * held_blocks + jnp.arange(held_blocks, dtype=jnp.int32)
    every_list = sig_blocks.reshape(owners, batches_here * listed_count)
    wanted = jnp.any(every_list[:, :, None] == own_ids[None, None, :], axis=1)
    wanted_rank = jnp.cumsum(wanted.astype(jnp.int32), axis=1)
    slot_ids = jnp.arange(CAPB, dtype=jnp.int32)
    selector = wanted[:, None, :] & (wanted_rank[:, None, :] == slot_ids[None, :, None] + 1)
    own_params = jnp.concatenate([row_centers, row_exps[None, :]], axis=0).reshape(
        4, held_blocks, BLK
    )
    own_tiles = density.reshape(held_blocks, BLK, local_width)
    tile_slots = jnp.einsum(
        "dck,krw->dcrw",
        selector.astype(jnp.bfloat16),
        own_tiles,
        preferred_element_type=jnp.float32,
    ).astype(jnp.bfloat16)
    param_slots = jnp.einsum(
        "dck,xkr->dcxr", selector.astype(jnp.float32), own_params, precision=lax.Precision.HIGHEST
    )
    got_tiles = lax.all_to_all(tile_slots, "grid", split_axis=0, concat_axis=0, tiled=True)
    got_params = lax.all_to_all(param_slots, "grid", split_axis=0, concat_axis=0, tiled=True)
    my_lists = lax.dynamic_slice_in_dim(sig_blocks, my_index * batches_here, batches_here, 0)
    block_ids = jnp.arange(owners * held_blocks, dtype=jnp.int32)
    needed = jnp.any(my_lists.reshape(-1)[:, None] == block_ids[None, :], axis=0)
    needed_rank = jnp.cumsum(needed.reshape(owners, held_blocks).astype(jnp.int32), axis=1).reshape(
        -1
    )
    slot_index = my_lists // held_blocks * CAPB + jnp.take(needed_rank, my_lists) - 1
    row_tiles = got_tiles.reshape(owners * CAPB, BLK, local_width)[slot_index]
    row_tiles = row_tiles.reshape(batches_here, listed_count * BLK, local_width)
    row_params = got_params.reshape(owners * CAPB, 4, BLK)[slot_index]
    row_params = row_params.transpose(0, 2, 1, 3).reshape(batches_here, 4, listed_count * BLK)
    basis_rows = basis_values(row_params[:, 0:3], row_params[:, 3], points).astype(jnp.bfloat16)
    field_values = jnp.einsum(
        "bgf,bfw->bgw", basis_rows, row_tiles, preferred_element_type=jnp.float32
    ).astype(jnp.bfloat16)
    local_window = jnp.concatenate([win_centers, win_exps[None, :]], axis=0)
    whole_window = gather_directly(local_window, "col", 1)
    window_count = whole_window.shape[1]
    target_par = jnp.take(whole_window, pair_target, axis=1).transpose(1, 0, 2)
    source_par = jnp.take(local_window, pair_source, axis=1).transpose(1, 0, 2)
    source_pick = (
        pair_source[:, :, None] == jnp.arange(local_width, dtype=jnp.int32)[None, None, :]
    ).astype(jnp.bfloat16)
    target_pick = (
        pair_target[:, :, None] == jnp.arange(window_count, dtype=jnp.int32)[None, None, :]
    ).astype(jnp.bfloat16)
    field_source = jnp.einsum(
        "bgw,bnw->bgn", field_values, source_pick, preferred_element_type=jnp.float32
    )
    product = (pair_values(target_par, source_par, points) * field_source).astype(jnp.bfloat16)
    partial_sum = jnp.einsum(
        "bgn,bnw->bgw", product, target_pick, preferred_element_type=jnp.float32
    )
    potential = sum_at_owner(partial_sum, "col", 2)
    weighted = (weights[:, :, None] * potential).astype(jnp.bfloat16)
    contribution_rows = jnp.einsum(
        "bgf,bgw->bfw", basis_rows, weighted, preferred_element_type=jnp.float32
    )
    contribution_rows = contribution_rows.reshape(batches_here * listed_count, BLK, local_width)
    fock_slots = (
        jnp.zeros((owners * CAPB, BLK, local_width), jnp.float32)
        .at[slot_index.reshape(-1)]
        .add(contribution_rows)
    )
    returned = lax.all_to_all(
        fock_slots.reshape(owners, CAPB, BLK, local_width),
        "grid",
        split_axis=0,
        concat_axis=0,
        tiled=True,
    )
    fock_rows = jnp.einsum(
        "dck,dcrw->krw", selector.astype(jnp.float32), returned, precision=lax.Precision.HIGHEST
    )
    return fock_rows.reshape(held_blocks * BLK, local_width)


def solution(mesh):
    return jax.shard_map(
        on_device,
        mesh=mesh,
        in_specs=(
            P("grid", "col"),
            P(None, "grid"),
            P("grid"),
            P(None, "col"),
            P("col"),
            P("grid", None, None),
            P("grid", None),
            P(),
            P("grid", "col"),
            P("grid", "col"),
        ),
        out_specs=P("grid", "col"),
        check_vma=False,
    )
```

profile of v0, /device:TPU:36, one launch (start us, length us, event | category | flops | bytes accessed | tf_op | source)
XLA Modules:
  0.0 557.8 jit_solution(12876178380273454578)
XLA Ops:
  1.3 4.8 all-to-all-start.1
  6.1 0.9 copy.66
  7.1 1.2 compare_reduce_fusion
  8.4 0.8 copy.114
  9.5 1.1 fusion.17
  10.6 0.9 copy.70
  11.5 16.3 %all-to-all-start = ((f32[64,2,4,128]{3,2,1,0:T(4,128)}), f32[64,2,4,128]{3,2,1,0:T(4,128)S(1)}, u32[]{:S(2)}, u32[]{:S(2)}) async-start(f32[64,2,4,128]{3,2,1,0:T(4,128)} %copy.70), calls=%async_computation | async-start | bytes 524288 | tf_op jit(solution)/shard_map/all_to_all | solution.py:117
  27.8 2.5 convolution_convert_fusion
  30.3 4.7 copy.79
  35.0 4.1 all-to-all-done
  39.1 9.6 %all-to-all-start.2 = ((bf16[64,2,128,128]{3,2,1,0:T(8,128)(2,1)}), bf16[64,2,128,128]{3,2,1,0:T(8,128)(2,1)}, u32[]{:S(2)}, u32[]{:S(2)}) async-start(bf16[64,2,128,128]{3,2,1,0:T(8,128)(2,1)} %copy.79), calls=%async_computation.2 | async-start | bytes 8388608 | tf_op jit(solution)/shard_map/all_to_all | solution.py:116
  49.6 1.1 gather_fusion
  51.0 27.7 %gather_fusion.3 = f32[8192,4]{1,0:T(8,128)} fusion(f32[4,128]{0,1:T(8,128)S(1)} %copy.76, s32[8192]{0:T(1024)S(1)} %broadcast_clamp_fusion), kind=kCustom, calls=%fused_computation.3 | custom fusion | bytes 294912 | tf_op jit(solution)/shard_map/jit(_take)/gather | solution.py:137
  78.6 2.9 copy.77
  81.9 27.7 %gather_fusion.2 = f32[8192,4]{1,0:T(8,128)} fusion(f32[4,1024]{0,1:T(8,128)S(1)} %bitcast.96, s32[8192]{0:T(1024)S(1)} %broadcast_clamp_fusion.1), kind=kCustom, calls=%fused_computation.2 | custom fusion | bytes 294912 | tf_op jit(solution)/shard_map/jit(_take)/gather | solution.py:136
  109.5 2.9 copy.75
  112.6 0.8 gather_fusion.1
  113.9 46.4 %all-to-all-done.2 = bf16[64,2,128,128]{3,2,1,0:T(8,128)(2,1)} async-done(((bf16[64,2,128,128]{3,2,1,0:T(8,128)(2,1)}), bf16[64,2,128,128]{3,2,1,0:T(8,128)(2,1)}, u32[]{:S(2)}, u32[]{:S(2)}) %all-to-all-start.2) | async-done | bytes 4194336 | tf_op jit(solution)/shard_map/all_to_all | solution.py:116
  160.3 5.2 gather_fusion.4
  165.6 13.2 %fusion.12 = bf16[4,128,128]{2,1,0:T(8,128)(2,1)S(1)} fusion(bf16[4,4096,128]{2,1,0:T(8,128)(2,1)} %bitcast.99, f32[4,4096]{1,0:T(4,128)S(1)} %get-tuple-element.21, f32[4,128]{1,0:T(4,128)S(1)} %get-tuple-element.19, f32[4,4096]{1,0:T(4,128)S(1)} %get-tuple-element.22, f32[4,128]{1,0:T(4,128)S(1)} %get-tuple-element.20, ...), kind=kOutput, calls=%fused_computation.22 | convolution fusion | flops 557907968 | bytes 4593664 | tf_op jit(solution)/shard_map/bgf,bfw->bgw/dot_general | solution.py:130
  178.7 7.6 %multiply_convert_fusion.9 = bf16[4,128,2048]{2,1,0:T(8,128)(2,1)S(1)} fusion(f32[4,2048]{1,0:T(4,128)S(1)} %get-tuple-element.13, f32[4,2048]{1,0:T(4,128)S(1)} %get-tuple-element.12, f32[4,128]{1,0:T(4,128)S(1)} %get-tuple-element.19, f32[4,2048]{1,0:T(4,128)S(1)} %get-tuple-element.11, f32[4,128]{1,0:T(4,128)S(1)} %get-tuple-element.20, ...), kind=kOutput, calls=%fused_computation.12.clone.clone.clone.clone.2 | convolution fusion | flops 298844160 | bytes 2430976 | tf_op jit(solution)/shard_map/bgw,bnw->bgn/dot_general | solution.py:144
  186.4 7.0 %fusion.8 = f32[4,16,8,8,128]{4,3,2,1,0:T(8,128)S(1)} fusion(s32[4,2048]{1,0:T(4,128)S(1)} %copy-done.1, bf16[4,128,2048]{2,1,0:T(8,128)(2,1)S(1)} %multiply_convert_fusion.9), kind=kOutput, calls=%fused_computation.20 | convolution fusion | flops 2155872256 | bytes 4227072 | tf_op jit(solution)/shard_map/bgn,bnw->bgw/dot_general | solution.py:148
  193.4 1.6 copy.112
  195.0 12.8 %all-to-all-start.3 = ((f32[8,4,128,128]{3,2,1,0:T(8,128)}), f32[8,4,128,128]{3,2,1,0:T(8,128)S(1)}, u32[]{:S(2)}, u32[]{:S(2)}) async-start(f32[8,4,128,128]{3,2,1,0:T(8,128)} %bitcast.95), calls=%async_computation.3 | async-start | bytes 4194304 | tf_op jit(solution)/shard_map/all_to_all | solution.py:41
  207.9 23.9 %all-to-all-done.3 = f32[8,4,128,128]{3,2,1,0:T(8,128)S(1)} async-done(((f32[8,4,128,128]{3,2,1,0:T(8,128)}), f32[8,4,128,128]{3,2,1,0:T(8,128)S(1)}, u32[]{:S(2)}, u32[]{:S(2)}) %all-to-all-start.3) | async-done | bytes 2097184 | tf_op jit(solution)/shard_map/all_to_all | solution.py:41
  231.9 11.1 %fusion.5 = f32[4,4096,128]{2,1,0:T(8,128)} fusion(f32[4,4096]{1,0:T(4,128)S(1)} %get-tuple-element.21, f32[4,128]{1,0:T(4,128)S(1)} %get-tuple-element.19, f32[4,4096]{1,0:T(4,128)S(1)} %get-tuple-element.22, f32[4,128]{1,0:T(4,128)S(1)} %get-tuple-element.20, f32[4,4096]{1,0:T(4,128)S(1)} %get-tuple-element.23, f32[4,128]{1,0:T(4,128)S(1)} %get-tuple-element.18, ...), kind=kOutput, calls=%fused_computation.16 | convolution fusion | flops 557973504 | bytes 8921088 | tf_op jit(solution)/shard_map/bgf,bgw->bfw/dot_general | solution.py:153
  243.0 4.3 broadcast_in_dim.38
  247.2 26.8 %scatter_fusion = f32[128,128,128]{2,1,0:T(8,128)} fusion(f32[128,128,128]{2,1,0:T(8,128)} %broadcast_in_dim.38, s32[128]{0:T(128)S(1)} %fusion.38, f32[128,128,128]{2,1,0:T(8,128)} %bitcast.94), kind=kCustom, calls=%fused_computation.5 | custom fusion | flops 2097152 | bytes 25166336 | tf_op jit(solution)/shard_map/scatter-add | solution.py:160
  274.1 14.3 %copy.82 = f32[64,2,128,128]{3,1,2,0:T(2,128)S(1)} copy(f32[64,2,128,128]{3,2,1,0:T(8,128)} %bitcast.93) | data formatting | bytes 16777216 | tf_op jit(solution)/shard_map/reshape | solution.py:163
  288.4 260.2 %all_to_all.25 = f32[64,2,128,128]{3,1,2,0:T(2,128)S(1)} all-to-all(f32[64,2,128,128]{3,1,2,0:T(2,128)S(1)} %copy.82), channel_id=1, replica_groups=mesh['grid'=64,'col'=8] {'grid'}, dimensions={0} | all-to-all | bytes 16777216 | tf_op jit(solution)/shard_map/all_to_all | solution.py:162
  548.6 7.7 %fusion.9 = f32[24,128,128]{2,0,1:T(8,128)S(1)} fusion(f32[64,2,128,128]{3,1,2,0:T(2,128)S(1)} %all_to_all.25, s32[64,24]{0,1:T(8,128)S(1)} %copy.68, s32[2]{0:T(128)S(1)} %iota_add_fusion, pred[64,24]{0,1:T(8,128)(4,1)S(1)} %copy.67), kind=kOutput, calls=%fused_computation.21 | convolution fusion | flops 603985920 | bytes 9969160 | tf_op jit(solution)/shard_map/dck,dcrw->krw/dot_general | solution.py:169
  556.3 1.4 copy.84
  (54 shorter events, 4.0 us)
Async XLA Ops:
  1.3 10.1 %all-to-all-start.1 = ((f32[8,4,128]{2,1,0:T(4,128)}), f32[8,4,128]{2,1,0:T(4,128)S(1)}, u32[]{:S(2)}, u32[]{:S(2)}) async-start(f32[8,4,128]{2,1,0:T(4,128)} %broadcast_in_dim.69), calls=%async_computation.1 | async-start | bytes 32768 | tf_op jit(solution)/shard_map/all_to_all | solution.py:17
  11.5 27.6 %all-to-all-start = ((f32[64,2,4,128]{3,2,1,0:T(4,128)}), f32[64,2,4,128]{3,2,1,0:T(4,128)S(1)}, u32[]{:S(2)}, u32[]{:S(2)}) async-start(f32[64,2,4,128]{3,2,1,0:T(4,128)} %copy.70), calls=%async_computation | async-start | bytes 524288 | tf_op jit(solution)/shard_map/all_to_all | solution.py:117
  35.0 13.8 %copy-start.1 = (s32[4,2048]{1,0:T(4,128)S(1)}, s32[4,2048]{1,0:T(4,128)}, u32[]{:S(2)}) copy-start(s32[4,2048]{1,0:T(4,128)} %param.18) | copy-start | bytes 98308
  35.0 13.8 %copy-start = (s32[4,2048]{1,0:T(4,128)S(1)}, s32[4,2048]{1,0:T(4,128)}, u32[]{:S(2)}) copy-start(s32[4,2048]{1,0:T(4,128)} %param.19) | copy-start | bytes 98308
  39.1 121.2 %all-to-all-start.2 = ((bf16[64,2,128,128]{3,2,1,0:T(8,128)(2,1)}), bf16[64,2,128,128]{3,2,1,0:T(8,128)(2,1)}, u32[]{:S(2)}, u32[]{:S(2)}) async-start(bf16[64,2,128,128]{3,2,1,0:T(8,128)(2,1)} %copy.79), calls=%async_computation.2 | async-start | bytes 8388608 | tf_op jit(solution)/shard_map/all_to_all | solution.py:116
  48.6 32.9 %copy-start.2 = (f32[4,3,128]{2,0,1:T(4,128)S(1)}, f32[4,3,128]{2,0,1:T(4,128)}, u32[]{:S(2)}) copy-start(f32[4,3,128]{2,0,1:T(4,128)} %param.15) | copy-start | bytes 18436
  195.0 36.9 %copy-start.3 = (f32[4,128]{1,0:T(4,128)S(1)}, f32[4,128]{1,0:T(4,128)}, u32[]{:S(2)}) copy-start(f32[4,128]{1,0:T(4,128)} %param.16) | copy-start | bytes 6148
  195.0 36.8 %all-to-all-start.3 = ((f32[8,4,128,128]{3,2,1,0:T(8,128)}), f32[8,4,128,128]{3,2,1,0:T(8,128)S(1)}, u32[]{:S(2)}, u32[]{:S(2)}) async-start(f32[8,4,128,128]{3,2,1,0:T(8,128)} %bitcast.95), calls=%async_computation.3 | async-start | bytes 4194304 | tf_op jit(solution)/shard_map/all_to_all | solution.py:41
where the time goes:
time: 559 us; the launch traced here: 558 us
  blocking collectives  260 us (47%)
  local copies, waits for them, and re-layouts  99.1 us (18%)
  waiting for transfers between devices  74.4 us (13%)
  matrix products  50.2 us (9%)
  starting transfers between devices  43.5 us (8%)
  other arithmetic  30 us (5%)
    all_to_all x1, blocking collectives, on_device(): lax.all_to_all(fock_slots.reshape(owners, CAPB, BLK, local_width), 'grid'...  260 us
    all_to_all x1, waiting for transfers between devices, on_device(): lax.all_to_all(tile_slots, 'grid', split_axis=0, concat_axis=0, tiled=True)  46.4 us
    gather x2, local copies, waits for them, and re-layouts, on_device(): source_par = jnp.take(local_window, pair_source, axis=1).transpose(1, 0, 2)  30.5 us
    gather x2, local copies, waits for them, and re-layouts, on_device(): target_par = jnp.take(whole_window, pair_target, axis=1).transpose(1, 0, 2)  30.5 us
    scatter-add x1, other arithmetic, on_device(): fock_slots = jnp.zeros((owners * CAPB, BLK, local_width), jnp.float32).at...  26.8 us
    all_to_all x1, waiting for transfers between devices, sum_at_owner(): lax.all_to_all(split_up(value, dim, devices), axis, 0, 0, tiled=True)  23.9 us
    all_to_all x1, starting transfers between devices, on_device(): lax.all_to_all(param_slots, 'grid', split_axis=0, concat_axis=0, tiled=True)  16.3 us
    reshape x1, local copies, waits for them, and re-layouts, on_device(): fock_slots.reshape(owners, CAPB, BLK, local_width)  14.3 us
  transfers between devices with their start and end apart: 4, of which 3 were waited for; matrix products, arithmetic and copies ran while one was open for 14% of the time, Pallas kernels for 0%

commit v1 on v0

v1 whole, which is shorter than its diff:
```python
import functools
import math

import jax
import jax.numpy as jnp
from jax import lax
from jax.experimental import pallas as pl
from jax.experimental.pallas import tpu as pltpu
from jax.sharding import PartitionSpec as P

BLK = 128
CAPB = 2
PARAMS = 4
CHUNK = 512
STEP_OWNERS = 4
SCALE_ROWS = 16
quad_nodes = 8
F32 = jnp.float32
BF16 = jnp.bfloat16


def call(kernel, name, flops=0, **kwargs):
    return pl.pallas_call(
        kernel,
        name=name,
        compiler_params=pltpu.CompilerParams(dimension_semantics=("arbitrary",) * len(kwargs["grid_spec"].grid)),
        cost_estimate=pl.CostEstimate(flops=flops, transcendentals=0, bytes_accessed=0),
        **kwargs,
    )


def pack_kernel(pick, tiles, params, tiles_out, params_out, *, owners_here):
    base = pl.program_id(0) * owners_here
    for owner in range(owners_here):
        for slot in range(CAPB):
            block = pick[(base + owner) * CAPB + slot]
            tiles_out[owner, slot * BLK : (slot + 1) * BLK, :] = tiles[block]
            params_out[owner, slot * PARAMS : (slot + 1) * PARAMS, :] = params[block]


def pack_slots(pick, tiles, params, owners):
    held, _, width = tiles.shape
    owners_here = min(8, owners)
    return call(
        functools.partial(pack_kernel, owners_here=owners_here),
        "pack_slots",
        grid_spec=pltpu.PrefetchScalarGridSpec(
            num_scalar_prefetch=1,
            grid=(owners // owners_here,),
            in_specs=[
                pl.BlockSpec((held, BLK, width), lambda i, *_: (0, 0, 0)),
                pl.BlockSpec((held, PARAMS, BLK), lambda i, *_: (0, 0, 0)),
            ],
            out_specs=[
                pl.BlockSpec((owners_here, CAPB * BLK, width), lambda i, *_: (i, 0, 0)),
                pl.BlockSpec((owners_here, CAPB * PARAMS, BLK), lambda i, *_: (i, 0, 0)),
            ],
        ),
        out_shape=[
            jax.ShapeDtypeStruct((owners, CAPB * BLK, width), BF16),
            jax.ShapeDtypeStruct((owners, CAPB * PARAMS, BLK), F32),
        ],
    )(pick, tiles, params)


def basis_kernel(slots, params, points, out, spots, *, listed):
    batch = pl.program_id(0)
    for axis in range(3):
        spots[axis] = jnp.broadcast_to(points[0, :, axis : axis + 1], spots.shape[1:])

    def one_block(entry, carry):
        row = slots[batch * listed + entry] * PARAMS
        squared = None
        for axis in range(3):
            delta = spots[axis] - params[pl.ds(row + axis, 1), :]
            squared = delta * delta if squared is None else squared + delta * delta
        value = jnp.exp(-params[pl.ds(row + 3, 1), :] * squared)
        out[0, :, pl.ds(pl.multiple_of(entry * BLK, BLK), BLK)] = value.astype(BF16)
        return carry

    lax.fori_loop(0, listed, one_block, 0, unroll=2)


def basis_for_field(slots, params, points_t, listed):
    batches, pts, _ = points_t.shape
    return call(
        functools.partial(basis_kernel, listed=listed),
        "basis_for_field",
        flops=batches * pts * listed * BLK * 100,
        grid_spec=pltpu.PrefetchScalarGridSpec(
            num_scalar_prefetch=1,
            grid=(batches,),
            in_specs=[
                pl.BlockSpec(params.shape, lambda b, *_: (0, 0)),
                pl.BlockSpec((1, pts, 3), lambda b, *_: (b, 0, 0)),
            ],
            out_specs=pl.BlockSpec((1, pts, listed * BLK), lambda b, *_: (b, 0, 0)),
            scratch_shapes=[pltpu.VMEM((3, pts, BLK), F32)],
        ),
        out_shape=jax.ShapeDtypeStruct((batches, pts, listed * BLK), BF16),
    )(slots, params, points_t)


def one_hot(columns, rows):
    spot = lax.broadcasted_iota(jnp.int32, (rows, columns.shape[1]), 0)
    return jnp.where(spot == columns, 1.0, 0.0).astype(BF16)


def rejoin(picked):
    return picked[0:4] + picked[4:8] + picked[8:12]


def pair_kernel(target, source, window, local, points, out, spots):
    @pl.when(pl.program_id(1) == 0)
    def _():
        for axis in range(3):
            spots[axis] = jnp.broadcast_to(points[0, :, axis : axis + 1], spots.shape[1:])

    target_par = rejoin(
        jnp.dot(window[...], one_hot(target[0], window.shape[1]), preferred_element_type=F32)
    )
    source_par = rejoin(
        jnp.dot(local[...], one_hot(source[0], local.shape[1]), preferred_element_type=F32)
    )
    target_exp, source_exp = target_par[3:4], source_par[3:4]
    joined = target_exp + source_exp
    separation = jnp.zeros_like(joined)
    centres = []
    for axis in range(3):
        here, there = target_par[axis : axis + 1], source_par[axis : axis + 1]
        offset = here - there
        separation = separation + offset * offset
        centres.append((target_exp * here + source_exp * there) / joined)
    prefactor = 2.0 * math.pi / joined * jnp.exp(-target_exp * source_exp / joined * separation)
    lanes = spots.shape[2]
    for first in range(0, joined.shape[1], lanes):
        part = slice(first, first + lanes)
        spread = None
        for axis in range(3):
            delta = spots[axis] - centres[axis][:, part]
            spread = delta * delta if spread is None else spread + delta * delta
        argument = joined[:, part] * spread
        summed = jnp.zeros_like(argument)
        for quad_node in range(quad_nodes):
            node_spot = (quad_node + 0.5) / quad_nodes
            summed = summed + jnp.exp(-argument * (node_spot * node_spot))
        out[0, :, part] = prefactor[:, part] * (summed / quad_nodes)


def pair_values(target, source, window, local, points_t):
    batches, _, pairs = target.shape
    pts = points_t.shape[1]
    return call(
        pair_kernel,
        "pair_values",
        flops=batches * pairs * pts * 400,
        grid_spec=pltpu.PrefetchScalarGridSpec(
            num_scalar_prefetch=0,
            grid=(batches, pairs // CHUNK),
            in_specs=[
                pl.BlockSpec((1, 1, CHUNK), lambda b, n: (b, 0, n)),
                pl.BlockSpec((1, 1, CHUNK), lambda b, n: (b, 0, n)),
                pl.BlockSpec(window.shape, lambda b, n: (0, 0)),
                pl.BlockSpec(local.shape, lambda b, n: (0, 0)),
                pl.BlockSpec((1, pts, 3), lambda b, n: (b, 0, 0)),
            ],
            out_specs=pl.BlockSpec((1, pts, CHUNK), lambda b, n: (b, 0, n)),
            scratch_shapes=[pltpu.VMEM((3, pts, BLK), F32)],
        ),
        out_shape=jax.ShapeDtypeStruct((batches, pts, pairs), F32),
    )(target, source, window, local, points_t)


def potential_kernel(slots, tiles, basis, values, target, source, out, rows, *, listed):
    batch = pl.program_id(0)
    for entry in range(listed):
        first = pl.multiple_of(slots[batch * listed + entry] * BLK, BLK)
        rows[entry * BLK : (entry + 1) * BLK, :] = tiles[pl.ds(first, BLK), :]
    field = jnp.dot(basis[0], rows[...], preferred_element_type=F32).astype(BF16)
    columns, width = out.shape[0], out.shape[3]
    window_count = columns * width
    potential = jnp.zeros((field.shape[0], window_count), F32)
    for first in range(0, values.shape[2], CHUNK):
        part = slice(first, first + CHUNK)
        picked = jnp.dot(field, one_hot(source[0, :, part], width), preferred_element_type=F32)
        product = (values[0, :, part] * picked).astype(BF16)
        potential += lax.dot_general(
            product,
            one_hot(target[0, :, part], window_count),
            (((1,), (1,)), ((), ())),
            preferred_element_type=F32,
        )
    for column in range(columns):
        out[column, 0] = potential[:, column * width : (column + 1) * width]


def potential_parts(slots, tiles, basis, values, target, source, columns):
    batches, pts, functions = basis.shape
    pairs = values.shape[2]
    width = tiles.shape[1]
    return call(
        functools.partial(potential_kernel, listed=functions // BLK),
        "potential_parts",
        grid_spec=pltpu.PrefetchScalarGridSpec(
            num_scalar_prefetch=1,
            grid=(batches,),
            in_specs=[
                pl.BlockSpec(tiles.shape, lambda b, *_: (0, 0)),
                pl.BlockSpec((1, pts, functions), lambda b, *_: (b, 0, 0)),
                pl.BlockSpec((1, pts, pairs), lambda b, *_: (b, 0, 0)),
                pl.BlockSpec((1, 1, pairs), lambda b, *_: (b, 0, 0)),
                pl.BlockSpec((1, 1, pairs), lambda b, *_: (b, 0, 0)),
            ],
            out_specs=pl.BlockSpec((columns, 1, pts, width), lambda b, *_: (0, b, 0, 0)),
            scratch_shapes=[pltpu.VMEM((functions, width), BF16)],
        ),
        out_shape=jax.ShapeDtypeStruct((columns, batches, pts, width), F32),
    )(slots, tiles, basis, values, target, source)


def owner_basis_kernel(pick, listed, params, points, out, spread_params, *, batches):
    @pl.when(pl.program_id(0) == 0)
    def _():
        for block in range(spread_params.shape[0]):
            for which in range(PARAMS):
                spread_params[block, which] = jnp.broadcast_to(
                    params[block * BLK : (block + 1) * BLK, which : which + 1], (BLK, BLK)
                )

    def one_owner(owner, carry):
        place = pl.program_id(0) * STEP_OWNERS + owner
        for slot in range(CAPB):
            block = pick[place * CAPB + slot]
            for batch in range(batches):
                squared = None
                for axis in range(3):
                    row = axis * batches + batch
                    delta = points[owner, row : row + 1, :] - spread_params[block, axis]
                    squared = delta * delta if squared is None else squared + delta * delta
                value = jnp.exp(-spread_params[block, 3] * squared)
                keep = listed[(place * CAPB + slot) * batches + batch]
                value = jnp.where(keep > 0, value, 0.0)
                out[owner, slot * BLK : (slot + 1) * BLK, batch * BLK : (batch + 1) * BLK] = (
                    value.astype(BF16)
                )
        return carry

    lax.fori_loop(0, STEP_OWNERS, one_owner, 0)


def basis_at_owner(pick, listed, params_t, points_all, batches):
    owners, rows, pts = points_all.shape
    held = params_t.shape[0] // BLK
    return call(
        functools.partial(owner_basis_kernel, batches=batches),
        "basis_at_owner",
        flops=owners * CAPB * BLK * batches * pts * 100,
        grid_spec=pltpu.PrefetchScalarGridSpec(
            num_scalar_prefetch=2,
            grid=(owners // STEP_OWNERS,),
            in_specs=[
                pl.BlockSpec(params_t.shape, lambda i, *_: (0, 0)),
                pl.BlockSpec((STEP_OWNERS, rows, pts), lambda i, *_: (i, 0, 0)),
            ],
            out_specs=pl.BlockSpec((STEP_OWNERS, CAPB * BLK, batches * pts), lambda i, *_: (i, 0, 0)),
            scratch_shapes=[pltpu.VMEM((held, PARAMS, BLK, BLK), F32)],
        ),
        out_shape=jax.ShapeDtypeStruct((owners, CAPB * BLK, batches * pts), BF16),
    )(pick, listed, params_t, points_all)


def fock_kernel(pick, basis, weighted, out):
    @pl.when(pl.program_id(0) == 0)
    def _():
        out[...] = jnp.zeros_like(out)

    for owner in range(STEP_OWNERS):
        place = pl.program_id(0) * STEP_OWNERS + owner
        rows = jnp.dot(basis[owner], weighted[owner], preferred_element_type=F32)
        for slot in range(CAPB):
            block = pick[place * CAPB + slot]
            out[block] = out[block] + rows[slot * BLK : (slot + 1) * BLK]


def fock_at_owner(pick, basis, weighted, held):
    owners, rows, points = basis.shape
    width = weighted.shape[2]
    return call(
        fock_kernel,
        "fock_at_owner",
        flops=2 * owners * rows * points * width,
        grid_spec=pltpu.PrefetchScalarGridSpec(
            num_scalar_prefetch=1,
            grid=(owners // STEP_OWNERS,),
            in_specs=[
                pl.BlockSpec((STEP_OWNERS, rows, points), lambda i, *_: (i, 0, 0)),
                pl.BlockSpec((STEP_OWNERS, points, width), lambda i, *_: (i, 0, 0)),
            ],
            out_specs=pl.BlockSpec((held, BLK, width), lambda i, *_: (0, 0, 0)),
        ),
        out_shape=jax.ShapeDtypeStruct((held, BLK, width), F32),
    )(pick, basis, weighted)


def to_everyone(value, axis):
    devices = lax.axis_size(axis)
    return lax.all_to_all(
        jnp.broadcast_to(value[None], (devices, *value.shape)), axis, 0, 0, tiled=True
    )


def in_parts(values):
    high = lax.reduce_precision(values, 8, 7)
    middle = lax.reduce_precision(values - high, 8, 7)
    low = values - high - middle
    parts = jnp.concatenate([high, middle, low, jnp.zeros_like(low)], axis=0)
    return parts.astype(BF16)


def sum_at_column(parts):
    columns, batches, pts, width = parts.shape
    largest = jnp.max(jnp.abs(parts), axis=(0, 2, 3))
    power = jnp.clip(13.0 - jnp.ceil(jnp.log2(largest)), -100.0, 100.0)
    scaled = (parts * jnp.exp2(power)[None, :, None, None]).astype(jnp.float16)
    tail = jnp.broadcast_to(
        power[None, :, None, None], (columns, batches, SCALE_ROWS, width)
    ).astype(jnp.float16)
    got = lax.all_to_all(
        jnp.concatenate([scaled, tail], axis=2), "col", split_axis=0, concat_axis=0, tiled=True
    )
    factor = jnp.exp2(-got[:, :, pts : pts + 1, 0:1].astype(F32))
    return jnp.sum(got[:, :, :pts].astype(F32) * factor, axis=0)


def on_device(
    density,
    row_centers,
    row_exps,
    win_centers,
    win_exps,
    points,
    weights,
    sig_blocks,
    pair_target,
    pair_source,
):
    owners = lax.axis_size("grid")
    columns = lax.axis_size("col")
    my_index = lax.axis_index("grid")
    held = row_exps.shape[0] // BLK
    width = density.shape[1]
    batches, _, pts = points.shape
    listed = sig_blocks.shape[1]

    lists = sig_blocks.reshape(owners, batches * listed)
    spot = lists - my_index * held
    owned = (spot >= 0) & (spot < held)
    lowest = jnp.min(jnp.where(owned, spot, held), axis=1)
    highest = jnp.max(jnp.where(owned, spot, -1), axis=1)
    found = highest >= 0
    ends = jnp.stack([lowest, highest], axis=1)
    pick = jnp.where(found[:, None], ends, 0).reshape(-1).astype(jnp.int32)
    at_end = owned[:, None, :] & (spot[:, None, :] == ends[:, :, None])
    at_end = at_end & ((ends[:, 1:] != ends[:, :1]) | (jnp.arange(CAPB) == 0))[:, :, None]
    in_batch = jnp.any(at_end.reshape(owners, CAPB, batches, listed), axis=3)
    in_batch = in_batch.reshape(-1).astype(jnp.int32)

    mine = lax.dynamic_slice_in_dim(lists, my_index, 1, 0)[0]
    owner_of = mine // held
    second = jnp.any(
        (owner_of[:, None] == owner_of[None, :]) & (mine[None, :] < mine[:, None]), axis=1
    )
    slots = (owner_of * CAPB + second).astype(jnp.int32)

    own_params = jnp.concatenate([row_centers, row_exps[None, :]], axis=0)
    own_blocks = own_params.reshape(PARAMS, held, BLK).transpose(1, 0, 2)
    tile_slots, param_slots = pack_slots(
        pick, density.reshape(held, BLK, width), own_blocks, owners
    )
    got_params = lax.all_to_all(param_slots, "grid", split_axis=0, concat_axis=0, tiled=True)
    got_tiles = lax.all_to_all(tile_slots, "grid", split_axis=0, concat_axis=0, tiled=True)

    points_t = points.transpose(0, 2, 1)
    basis = basis_for_field(
        slots, got_params.reshape(owners * CAPB * PARAMS, BLK), points_t, listed
    )
    local_window = jnp.concatenate([win_centers, win_exps[None, :]], axis=0)
    whole_window = to_everyone(local_window, "col").transpose(1, 0, 2).reshape(PARAMS, -1)
    target = pair_target[:, None, :]
    source = pair_source[:, None, :]
    values = pair_values(target, source, in_parts(whole_window), in_parts(local_window), points_t)
    parts = potential_parts(
        slots,
        got_tiles.reshape(owners * CAPB * BLK, width),
        basis,
        values,
        target,
        source,
        columns,
    )
    potential = sum_at_column(parts)
    weighted = (weights[:, :, None] * potential).astype(BF16).reshape(batches * pts, width)

    all_weighted = lax.all_gather(weighted, "grid", axis=0, tiled=True)
    points_all = to_everyone(points.transpose(1, 0, 2).reshape(3 * batches, pts), "grid")
    own_basis = basis_at_owner(pick, in_batch, own_params.T, points_all, batches)
    fock = fock_at_owner(
        pick, own_basis, all_weighted.reshape(owners, batches * pts, width), held
    )
    return fock.reshape(held * BLK, width)


def solution(mesh):
    return jax.shard_map(
        on_device,
        mesh=mesh,
        in_specs=(
            P("grid", "col"),
            P(None, "grid"),
            P("grid"),
            P(None, "col"),
            P("col"),
            P("grid", None, None),
            P("grid", None),
            P(),
            P("grid", "col"),
            P("grid", "col"),
        ),
        out_specs=P("grid", "col"),
        check_vma=False,
    )
```

time: 559 us -> 358 us (0.64)
  the two profiles are of different devices: /device:TPU:36 before, /device:TPU:1 now
where the time goes in v1:
time: 358 us; the launch traced here: 357 us
  waiting for transfers between devices  157 us (44%)
  Pallas kernels  79.6 us (22%)
  blocking collectives  46.5 us (13%)
  starting transfers between devices  42.1 us (12%)
  between operations  13.6 us (4%)
  other arithmetic  9.33 us (3%)
  local copies, waits for them, and re-layouts  8.95 us (2%)
    all_to_all x1, waiting for transfers between devices, on_device(): lax.all_to_all(tile_slots, 'grid', split_axis=0, concat_axis=0, tiled=True)  91.9 us
    all_gather x1, waiting for transfers between devices, on_device(): all_weighted = lax.all_gather(weighted, 'grid', axis=0, tiled=True)  50.8 us
    all_to_all x2, starting transfers between devices, to_everyone(): lax.all_to_all(jnp.broadcast_to(value[None], (devices, *value.shape)), ax...  36.2 us
    all_to_all x1, blocking collectives, on_device(): lax.all_to_all(param_slots, 'grid', split_axis=0, concat_axis=0, tiled=True)  25.6 us
    pallas_call x1, Pallas kernels, basis_at_owner(): call(functools.partial(owner_basis_kernel, batches=batches), 'basis_at_ow...  21 us
    all_to_all x1, blocking collectives, sum_at_column(): lax.all_to_all(jnp.concatenate([scaled, tail], axis=2), 'col', split_axis...  20.9 us
    pallas_call x1, Pallas kernels, fock_at_owner(): call(fock_kernel, 'fock_at_owner', flops=2 * owners * rows * points * wid...  17.5 us
    pallas_call x1, Pallas kernels, pair_values(): call(pair_kernel, 'pair_values', flops=batches * pairs * pts * 400, grid_...  14.4 us
  transfers between devices with their start and end apart: 4, of which 3 were waited for; matrix products, arithmetic and copies ran while one was open for 3% of the time, Pallas kernels for 13%

profile of v1, /device:TPU:1, one launch (start us, length us, event | category | flops | bytes accessed | tf_op | source)
XLA Modules:
  0.0 357.1 jit_solution(4211385840803173752)
XLA Ops:
  6.5 0.7 reduce-precision_convert_fusion.3
  7.2 0.6 broadcast_in_dim.76
  7.8 10.1 %all-to-all-start.3 = ((f32[8,4,128]{2,1,0:T(4,128)}), f32[8,4,128]{2,1,0:T(4,128)S(1)}, u32[]{:S(2)}, u32[]{:S(2)}) async-start(f32[8,4,128]{2,1,0:T(4,128)} %broadcast_in_dim.76), calls=%async_computation.3 | async-start | bytes 32768 | tf_op jit(solution)/shard_map/all_to_all | solution.py:307
  17.9 0.8 select_reduce_fusion
  19.2 1.5 maximum_bitcast_fusion.params
  20.7 0.7 select_n.35.pick
  21.5 5.4 %pack_slots.1 = (bf16[64,256,128]{2,1,0:T(8,128)(2,1)}, f32[64,8,128]{2,1,0:T(8,128)}) custom-call(s32[128]{0:T(128)} %select_n.35.pick, bf16[24,128,128]{2,1,0:T(8,128)(2,1)} %bitcast.42, f32[24,4,128]{2,1,0:T(4,128)} %maximum_bitcast_fusion.params), custom_call_target="tpu_custom_call" | custom-call | tf_op jit(solution)/shard_map/pack_slots/pallas_call | solution.py:44
  26.8 25.6 %all_to_all.25 = f32[64,8,128]{2,1,0:T(8,128)} all-to-all(f32[64,8,128]{2,1,0:T(8,128)} %get-tuple-element.8), channel_id=1, replica_groups=mesh['grid'=64,'col'=8] {'grid'}, dimensions={0} | all-to-all | bytes 524288 | tf_op jit(solution)/shard_map/all_to_all | solution.py:380
  52.5 5.8 %all-to-all-start.1 = ((bf16[64,256,128]{2,1,0:T(8,128)(2,1)}), bf16[64,256,128]{2,1,0:T(8,128)(2,1)}, u32[]{:S(2)}, u32[]{:S(2)}) async-start(bf16[64,256,128]{2,1,0:T(8,128)(2,1)} %get-tuple-element.7), calls=%async_computation.1 | async-start | bytes 8388608 | tf_op jit(solution)/shard_map/all_to_all | solution.py:381
  58.4 0.6 broadcast_in_dim.73.target
  59.1 0.6 broadcast_in_dim.74.source
  59.8 0.9 copy.54
  61.0 0.5 convert_add_fusion.slots
  61.5 0.7 maximum_maximum_fusion.1.local
  62.2 0.7 maximum_maximum_fusion.window
  62.9 14.4 %pair_values.1.values = f32[4,128,2048]{2,1,0:T(8,128)} custom-call(s32[4,1,2048]{2,1,0:T(1,128)} %broadcast_in_dim.73.target, s32[4,1,2048]{2,1,0:T(1,128)} %broadcast_in_dim.74.source, bf16[16,1024]{1,0:T(8,128)(2,1)} %maximum_maximum_fusion.window, bf16[16,128]{1,0:T(8,128)(2,1)} %maximum_maximum_fusion.1.local, f32[4,128,3]{2,1,0:T(8,128)} %bitcast.39), custom_call_target="tpu_custom_call" | custom-call | flops 419430400 | tf_op jit(solution)/shard_map/pair_values/pallas_call | solution.py:153
  77.3 7.4 %basis_for_field.1.basis = bf16[4,128,4096]{2,1,0:T(8,128)(2,1)} custom-call(s32[128]{0:T(128)} %convert_add_fusion.slots, f32[512,128]{1,0:T(8,128)} %bitcast.41, f32[4,128,3]{2,1,0:T(8,128)} %bitcast.40), custom_call_target="tpu_custom_call" | custom-call | flops 209715200 | tf_op jit(solution)/shard_map/basis_for_field/pallas_call | solution.py:86
  84.7 91.9 %all-to-all-done.1 = bf16[64,256,128]{2,1,0:T(8,128)(2,1)} async-done(((bf16[64,256,128]{2,1,0:T(8,128)(2,1)}), bf16[64,256,128]{2,1,0:T(8,128)(2,1)}, u32[]{:S(2)}, u32[]{:S(2)}) %all-to-all-start.1) | async-done | bytes 4194336 | tf_op jit(solution)/shard_map/all_to_all | solution.py:381
  176.5 14.0 %potential_parts.1 = f32[8,4,128,128]{3,2,1,0:T(8,128)} custom-call(s32[128]{0:T(128)} %convert_add_fusion.slots, bf16[16384,128]{1,0:T(8,128)(2,1)} %bitcast.13.tiles, bf16[4,128,4096]{2,1,0:T(8,128)(2,1)} %basis_for_field.1.basis, f32[4,128,2048]{2,1,0:T(8,128)} %pair_values.1.values, s32[4,1,2048]{2,1,0:T(1,128)} %broadcast_in_dim.73.target, ...), custom_call_target="tpu_custom_call" | custom-call | tf_op jit(solution)/shard_map/potential_parts/pallas_call | solution.py:201
  190.5 1.9 abs_reduce_fusion
  193.6 20.9 %all_to_all.26 = f16[8,4,144,128]{3,2,1,0:T(8,128)(2,1)S(1)} all-to-all(f16[8,4,144,128]{3,2,1,0:T(8,128)(2,1)S(1)} %pad_maximum_fusion), channel_id=1, replica_groups=mesh['grid'=64,'col'=8] {'col'}, dimensions={0} | all-to-all | bytes 2359296 | tf_op jit(solution)/shard_map/all_to_all | solution.py:328
  214.7 0.4 multiply_reduce_fusion
  215.1 0.8 fusion
  215.9 0.8 broadcast_in_dim.71
  216.7 26.2 %all-to-all-start = ((f32[64,12,128]{2,1,0:T(8,128)}), f32[64,12,128]{2,1,0:T(8,128)S(1)}, u32[]{:S(2)}, u32[]{:S(2)}) async-start(f32[64,12,128]{2,1,0:T(8,128)} %broadcast_in_dim.71), calls=%async_computation | async-start | bytes 1048576 | tf_op jit(solution)/shard_map/all_to_all | solution.py:307
  243.4 0.7 reshape.138.listed
  244.2 1.7 copy.52
  245.8 14.4 %all-to-all-done.points = f32[64,12,128]{2,1,0:T(8,128)S(1)} async-done(((f32[64,12,128]{2,1,0:T(8,128)}), f32[64,12,128]{2,1,0:T(8,128)S(1)}, u32[]{:S(2)}, u32[]{:S(2)}) %all-to-all-start) | async-done | bytes 393248 | tf_op jit(solution)/shard_map/all_to_all | solution.py:307
  260.2 0.8 copy-done.1
  261.0 21.0 %basis_at_owner.1.basis = bf16[64,256,512]{2,1,0:T(8,128)(2,1)} custom-call(s32[128]{0:T(128)} %select_n.35.pick, s32[512]{0:T(512)} %reshape.138.listed, f32[3072,4]{1,0:T(8,128)} %bitcast.38, f32[64,12,128]{2,1,0:T(8,128)} %copy-done.1), custom_call_target="tpu_custom_call" | custom-call | flops 838860800 | tf_op jit(solution)/shard_map/basis_at_owner/pallas_call | solution.py:254
  282.1 50.8 %all-gather.2.cloned.1.call-done = bf16[32768,128]{1,0:T(8,128)(2,1)} async-done(((bf16[512,128]{1,0:T(8,128)(2,1)}), bf16[32768,128]{1,0:T(8,128)(2,1)}) %all-gather.2.cloned.1.call-update) | async-done | bytes 8388624 | tf_op jit(solution)/shard_map/all_gather | solution.py:404
  332.8 17.5 %fock_at_owner.1 = f32[24,128,128]{2,1,0:T(8,128)} custom-call(s32[128]{0:T(128)} %select_n.35.pick, bf16[64,256,512]{2,1,0:T(8,128)(2,1)} %basis_at_owner.1.basis, bf16[64,512,128]{2,1,0:T(8,128)(2,1)} %bitcast.37), custom_call_target="tpu_custom_call" | custom-call | flops 2147483648 | tf_op jit(solution)/shard_map/fock_at_owner/pallas_call | solution.py:288
  (53 shorter events, 2.9 us)
Async XLA Ops:
  7.8 19.0 %all-to-all-start.3 = ((f32[8,4,128]{2,1,0:T(4,128)}), f32[8,4,128]{2,1,0:T(4,128)S(1)}, u32[]{:S(2)}, u32[]{:S(2)}) async-start(f32[8,4,128]{2,1,0:T(4,128)} %broadcast_in_dim.76), calls=%async_computation.3 | async-start | bytes 32768 | tf_op jit(solution)/shard_map/all_to_all | solution.py:307
  52.4 5.9 %copy-start.3 = (s32[256,32]{0,1:T(8,128)S(1)}, s32[256,32]{0,1:T(8,128)}, u32[]{:S(2)}) copy-start(s32[256,32]{0,1:T(8,128)} %param.17) | copy-start | bytes 98308
  52.4 6.0 %copy-start.5 = (s32[4,2048]{1,0:T(4,128)S(1)}, s32[4,2048]{1,0:T(4,128)}, u32[]{:S(2)}) copy-start(s32[4,2048]{1,0:T(4,128)} %param.18) | copy-start | bytes 98308
  52.4 6.6 %copy-start.6 = (s32[4,2048]{1,0:T(4,128)S(1)}, s32[4,2048]{1,0:T(4,128)}, u32[]{:S(2)}) copy-start(s32[4,2048]{1,0:T(4,128)} %param.19) | copy-start | bytes 98308
  52.4 7.3 %copy-start.7 = (f32[4,3,128]{2,0,1:T(4,128)S(1)}, f32[4,3,128]{2,0,1:T(4,128)}, u32[]{:S(2)}) copy-start(f32[4,3,128]{2,0,1:T(4,128)} %param.15) | copy-start | bytes 18436
  52.5 124.1 %all-to-all-start.1 = ((bf16[64,256,128]{2,1,0:T(8,128)(2,1)}), bf16[64,256,128]{2,1,0:T(8,128)(2,1)}, u32[]{:S(2)}, u32[]{:S(2)}) async-start(bf16[64,256,128]{2,1,0:T(8,128)(2,1)} %get-tuple-element.7), calls=%async_computation.1 | async-start | bytes 8388608 | tf_op jit(solution)/shard_map/all_to_all | solution.py:381
  58.3 274.6 %all-gather.2.cloned.1.call-start = ((), (), s32[]{:S(2)}) async-start(), calls=%async_computation.5 | async-start | bytes 8519680 | tf_op jit(solution)/shard_map/all_gather | solution.py:404
  190.5 2.2 copy-start
  193.6 21.5 %copy-start.8 = (f32[4,128]{1,0:T(4,128)S(1)}, f32[4,128]{1,0:T(4,128)}, u32[]{:S(2)}) copy-start(f32[4,128]{1,0:T(4,128)} %param.16) | copy-start | bytes 6148
  214.5 29.7 %copy-start.2 = (f32[3,3072]{1,0:T(4,128)S(1)}, f32[3,3072]{1,0:T(4,128)}, u32[]{:S(2)}) copy-start(f32[3,3072]{1,0:T(4,128)} %param.11) | copy-start | bytes 110596
  214.5 29.7 %copy-start.4 = (f32[3072]{0:T(1024)S(1)}, f32[3072]{0:T(1024)}, u32[]{:S(2)}) copy-start(f32[3072]{0:T(1024)} %param.12) | copy-start | bytes 36868
  216.7 43.5 %all-to-all-start = ((f32[64,12,128]{2,1,0:T(8,128)}), f32[64,12,128]{2,1,0:T(8,128)S(1)}, u32[]{:S(2)}, u32[]{:S(2)}) async-start(f32[64,12,128]{2,1,0:T(8,128)} %broadcast_in_dim.71), calls=%async_computation | async-start | bytes 1048576 | tf_op jit(solution)/shard_map/all_to_all | solution.py:307
  260.2 0.8 copy-start.1
Sparse Core Ops, SparseCore 0:
  216.0 116.7 all-gather.1

commit v2 on v1

--- a/solution.py
+++ b/solution.py
@@ -6,6 +6,7 @@
 from jax import lax
 from jax.experimental import pallas as pl
 from jax.experimental.pallas import tpu as pltpu
+from jax.sharding import Mesh
 from jax.sharding import PartitionSpec as P
 
 BLK = 128
@@ -14,6 +15,8 @@
 CHUNK = 512
 STEP_OWNERS = 4
 SCALE_ROWS = 16
+POINT_ROWS = 16
+GRID = ("y", "z")
 quad_nodes = 8
 F32 = jnp.float32
 BF16 = jnp.bfloat16
@@ -23,53 +26,44 @@
     return pl.pallas_call(
         kernel,
         name=name,
-        compiler_params=pltpu.CompilerParams(dimension_semantics=("arbitrary",) * len(kwargs["grid_spec"].grid)),
+        compiler_params=pltpu.CompilerParams(
+            dimension_semantics=("arbitrary",) * len(kwargs["grid_spec"].grid),
+        ),
         cost_estimate=pl.CostEstimate(flops=flops, transcendentals=0, bytes_accessed=0),
         **kwargs,
     )
 
 
-def pack_kernel(pick, tiles, params, tiles_out, params_out, *, owners_here):
-    base = pl.program_id(0) * owners_here
-    for owner in range(owners_here):
+def pack_kernel(pick, tiles, out):
+    first = pl.program_id(0) * out.shape[0]
+    for owner in range(out.shape[0]):
         for slot in range(CAPB):
-            block = pick[(base + owner) * CAPB + slot]
-            tiles_out[owner, slot * BLK : (slot + 1) * BLK, :] = tiles[block]
-            params_out[owner, slot * PARAMS : (slot + 1) * PARAMS, :] = params[block]
-
-
-def pack_slots(pick, tiles, params, owners):
+            out[owner, slot * BLK : (slot + 1) * BLK, :] = tiles[pick[(first + owner) * CAPB + slot]]
+
+
+def pack_slots(pick, tiles, owners):
     held, _, width = tiles.shape
     owners_here = min(8, owners)
     return call(
-        functools.partial(pack_kernel, owners_here=owners_here),
+        pack_kernel,
         "pack_slots",
         grid_spec=pltpu.PrefetchScalarGridSpec(
             num_scalar_prefetch=1,
             grid=(owners // owners_here,),
-            in_specs=[
-                pl.BlockSpec((held, BLK, width), lambda i, *_: (0, 0, 0)),
-                pl.BlockSpec((held, PARAMS, BLK), lambda i, *_: (0, 0, 0)),
-            ],
-            out_specs=[
-                pl.BlockSpec((owners_here, CAPB * BLK, width), lambda i, *_: (i, 0, 0)),
-                pl.BlockSpec((owners_here, CAPB * PARAMS, BLK), lambda i, *_: (i, 0, 0)),
-            ],
-        ),
-        out_shape=[
-            jax.ShapeDtypeStruct((owners, CAPB * BLK, width), BF16),
-            jax.ShapeDtypeStruct((owners, CAPB * PARAMS, BLK), F32),
-        ],
-    )(pick, tiles, params)
-
-
-def basis_kernel(slots, params, points, out, spots, *, listed):
+            in_specs=[pl.BlockSpec((held, BLK, width), lambda i, *_: (0, 0, 0))],
+            out_specs=pl.BlockSpec((owners_here, CAPB * BLK, width), lambda i, *_: (i, 0, 0)),
+        ),
+        out_shape=jax.ShapeDtypeStruct((owners, CAPB * BLK, width), BF16),
+    )(pick, tiles)
+
+
+def basis_kernel(rows_at, params, points, out, spots, *, listed):
     batch = pl.program_id(0)
     for axis in range(3):
         spots[axis] = jnp.broadcast_to(points[0, :, axis : axis + 1], spots.shape[1:])
 
     def one_block(entry, carry):
-        row = slots[batch * listed + entry] * PARAMS
+        row = rows_at[batch * listed + entry]
         squared = None
         for axis in range(3):
             delta = spots[axis] - params[pl.ds(row + axis, 1), :]
@@ -81,7 +75,7 @@
     lax.fori_loop(0, listed, one_block, 0, unroll=2)
 
 
-def basis_for_field(slots, params, points_t, listed):
+def basis_for_field(rows_at, params, points_t, listed):
     batches, pts, _ = points_t.shape
     return call(
         functools.partial(basis_kernel, listed=listed),
@@ -97,8 +91,8 @@
             out_specs=pl.BlockSpec((1, pts, listed * BLK), lambda b, *_: (b, 0, 0)),
             scratch_shapes=[pltpu.VMEM((3, pts, BLK), F32)],
         ),
-        out_shape=jax.ShapeDtypeStruct((batches, pts, listed * BLK), BF16),
-    )(slots, params, points_t)
+        out_shape=pltpu.HBM((batches, pts, listed * BLK), BF16),
+    )(rows_at, params, points_t)
 
 
 def one_hot(columns, rows):
@@ -167,7 +161,7 @@
             out_specs=pl.BlockSpec((1, pts, CHUNK), lambda b, n: (b, 0, n)),
             scratch_shapes=[pltpu.VMEM((3, pts, BLK), F32)],
         ),
-        out_shape=jax.ShapeDtypeStruct((batches, pts, pairs), F32),
+        out_shape=pltpu.HBM((batches, pts, pairs), F32),
     )(target, source, window, local, points_t)
 
 
@@ -232,24 +226,29 @@
         for slot in range(CAPB):
             block = pick[place * CAPB + slot]
             for batch in range(batches):
-                squared = None
-                for axis in range(3):
-                    row = axis * batches + batch
-                    delta = points[owner, row : row + 1, :] - spread_params[block, axis]
-                    squared = delta * delta if squared is None else squared + delta * delta
-                value = jnp.exp(-spread_params[block, 3] * squared)
+                here = (owner, slice(slot * BLK, (slot + 1) * BLK), slice(batch * BLK, (batch + 1) * BLK))
                 keep = listed[(place * CAPB + slot) * batches + batch]
-                value = jnp.where(keep > 0, value, 0.0)
-                out[owner, slot * BLK : (slot + 1) * BLK, batch * BLK : (batch + 1) * BLK] = (
-                    value.astype(BF16)
-                )
+
+                @pl.when(keep > 0)
+                def _():
+                    squared = None
+                    for axis in range(3):
+                        row = axis * batches + batch
+                        delta = points[owner, row : row + 1, :] - spread_params[block, axis]
+                        squared = delta * delta if squared is None else squared + delta * delta
+                    out[here] = jnp.exp(-spread_params[block, 3] * squared).astype(BF16)
+
+                @pl.when(keep == 0)
+                def _():
+                    out[here] = jnp.zeros((BLK, BLK), BF16)
+
         return carry
 
     lax.fori_loop(0, STEP_OWNERS, one_owner, 0)
 
 
-def basis_at_owner(pick, listed, params_t, points_all, batches):
-    owners, rows, pts = points_all.shape
+def basis_at_owner(pick, listed, params_t, gathered, batches, pts):
+    owners, rows, _ = gathered.shape
     held = params_t.shape[0] // BLK
     return call(
         functools.partial(owner_basis_kernel, batches=batches),
@@ -260,34 +259,39 @@
             grid=(owners // STEP_OWNERS,),
             in_specs=[
                 pl.BlockSpec(params_t.shape, lambda i, *_: (0, 0)),
-                pl.BlockSpec((STEP_OWNERS, rows, pts), lambda i, *_: (i, 0, 0)),
+                pl.BlockSpec(
+                    (STEP_OWNERS, POINT_ROWS, BLK), lambda i, *_: (i, rows // POINT_ROWS - 1, 0)
+                ),
             ],
             out_specs=pl.BlockSpec((STEP_OWNERS, CAPB * BLK, batches * pts), lambda i, *_: (i, 0, 0)),
             scratch_shapes=[pltpu.VMEM((held, PARAMS, BLK, BLK), F32)],
         ),
-        out_shape=jax.ShapeDtypeStruct((owners, CAPB * BLK, batches * pts), BF16),
-    )(pick, listed, params_t, points_all)
-
-
-def fock_kernel(pick, basis, weighted, out):
+        out_shape=pltpu.HBM((owners, CAPB * BLK, batches * pts), BF16),
+    )(pick, listed, params_t, gathered)
+
+
+def add_rows(out, pick, place, rows):
+    for slot in range(CAPB):
+        block = pick[place * CAPB + slot]
+        out[block] = out[block] + rows[slot * BLK : (slot + 1) * BLK]
+
+
+def fock_kernel(pick, basis, weighted, before, out):
     @pl.when(pl.program_id(0) == 0)
     def _():
-        out[...] = jnp.zeros_like(out)
+        out[...] = before[...]
 
     for owner in range(STEP_OWNERS):
         place = pl.program_id(0) * STEP_OWNERS + owner
-        rows = jnp.dot(basis[owner], weighted[owner], preferred_element_type=F32)
-        for slot in range(CAPB):
-            block = pick[place * CAPB + slot]
-            out[block] = out[block] + rows[slot * BLK : (slot + 1) * BLK]
-
-
-def fock_at_owner(pick, basis, weighted, held):
-    owners, rows, points = basis.shape
-    width = weighted.shape[2]
+        add_rows(out, pick, place, jnp.dot(basis[owner], weighted[owner], preferred_element_type=F32))
+
+
+def fock_from_gather(pick, basis, weighted, before):
+    owners, rows, _ = basis.shape
+    _, points, width = weighted.shape
     return call(
         fock_kernel,
-        "fock_at_owner",
+        "fock_from_gather",
         flops=2 * owners * rows * points * width,
         grid_spec=pltpu.PrefetchScalarGridSpec(
             num_scalar_prefetch=1,
@@ -295,11 +299,55 @@
             in_specs=[
                 pl.BlockSpec((STEP_OWNERS, rows, points), lambda i, *_: (i, 0, 0)),
                 pl.BlockSpec((STEP_OWNERS, points, width), lambda i, *_: (i, 0, 0)),
+                pl.BlockSpec(before.shape, lambda i, *_: (0, 0, 0)),
             ],
-            out_specs=pl.BlockSpec((held, BLK, width), lambda i, *_: (0, 0, 0)),
+            out_specs=pl.BlockSpec(before.shape, lambda i, *_: (0, 0, 0)),
+        ),
+        out_shape=jax.ShapeDtypeStruct(before.shape, F32),
+        input_output_aliases={3: 0},
+    )(pick, basis, weighted, before)
+
+
+def fock_line_kernel(pick, lines, *refs, first, count, side, fresh):
+    basis, weighted, out = refs[:count], refs[count : 2 * count], refs[-1]
+
+    @pl.when(pl.program_id(0) == 0)
+    def _():
+        out[...] = jnp.zeros_like(out) if fresh else refs[2 * count][...]
+
+    for line in range(count):
+        place = pl.program_id(0) * side + lines[first + line]
+        rows = jnp.dot(basis[line][0, 0], weighted[line][0], preferred_element_type=F32)
+        add_rows(out, pick, place, rows)
+
+
+def fock_from_lines(pick, lines, first, basis, weighted, before, held):
+    side, _, rows, _ = basis.shape
+    count = len(weighted)
+    _, points, width = weighted[0].shape
+    last = basis.shape[3] // points - 1
+    whole = pl.BlockSpec((held, BLK, width), lambda i, *_: (0, 0, 0))
+
+    def line_spec(line):
+        return pl.BlockSpec((1, 1, rows, points), lambda i, _, lines: (i, lines[first + line], 0, last))
+
+    return call(
+        functools.partial(
+            fock_line_kernel, first=first, count=count, side=side, fresh=before is None
+        ),
+        "fock_from_lines",
+        flops=2 * count * side * rows * points * width,
+        grid_spec=pltpu.PrefetchScalarGridSpec(
+            num_scalar_prefetch=2,
+            grid=(side,),
+            in_specs=[line_spec(line) for line in range(count)]
+            + [pl.BlockSpec((1, points, width), lambda i, *_: (i, 0, 0))] * count
+            + ([] if before is None else [whole]),
+            out_specs=whole,
         ),
         out_shape=jax.ShapeDtypeStruct((held, BLK, width), F32),
-    )(pick, basis, weighted)
+        input_output_aliases={} if before is None else {2 + 2 * count: 0},
+    )(pick, lines, *[basis] * count, *weighted, *([] if before is None else [before]))
 
 
 def to_everyone(value, axis):
@@ -344,9 +392,9 @@
     pair_target,
     pair_source,
 ):
-    owners = lax.axis_size("grid")
+    owners = lax.axis_size(GRID)
     columns = lax.axis_size("col")
-    my_index = lax.axis_index("grid")
+    my_index = lax.axis_index(GRID)
     held = row_exps.shape[0] // BLK
     width = density.shape[1]
     batches, _, pts = points.shape
@@ -373,22 +421,28 @@
     slots = (owner_of * CAPB + second).astype(jnp.int32)
 
     own_params = jnp.concatenate([row_centers, row_exps[None, :]], axis=0)
-    own_blocks = own_params.reshape(PARAMS, held, BLK).transpose(1, 0, 2)
-    tile_slots, param_slots = pack_slots(
-        pick, density.reshape(held, BLK, width), own_blocks, owners
-    )
-    got_params = lax.all_to_all(param_slots, "grid", split_axis=0, concat_axis=0, tiled=True)
-    got_tiles = lax.all_to_all(tile_slots, "grid", split_axis=0, concat_axis=0, tiled=True)
+    own_blocks = own_params.reshape(PARAMS, held, BLK).transpose(1, 0, 2).reshape(-1, BLK)
+    own_points = points.transpose(1, 0, 2).reshape(3 * batches, pts)
+    spare = jnp.zeros((POINT_ROWS - own_points.shape[0], BLK), F32)
+    sent = jnp.concatenate([own_blocks, own_points, spare], axis=0)
+    gathered = lax.all_gather(sent, GRID, axis=0, tiled=True)
+    rows_each = sent.shape[0]
+    rows_at = (owner_of * rows_each + (mine - owner_of * held) * PARAMS).astype(jnp.int32)
+
+    tile_slots = pack_slots(pick, density.reshape(held, BLK, width), owners)
+    got_tiles = lax.all_to_all(tile_slots, GRID, split_axis=0, concat_axis=0, tiled=True)
 
     points_t = points.transpose(0, 2, 1)
-    basis = basis_for_field(
-        slots, got_params.reshape(owners * CAPB * PARAMS, BLK), points_t, listed
-    )
     local_window = jnp.concatenate([win_centers, win_exps[None, :]], axis=0)
     whole_window = to_everyone(local_window, "col").transpose(1, 0, 2).reshape(PARAMS, -1)
     target = pair_target[:, None, :]
     source = pair_source[:, None, :]
     values = pair_values(target, source, in_parts(whole_window), in_parts(local_window), points_t)
+    basis = basis_for_field(rows_at, gathered, points_t, listed)
+    own_basis = basis_at_owner(
+        pick, in_batch, own_params.T, gathered.reshape(owners, rows_each, BLK), batches, pts
+    )
+    basis, values, own_basis = lax.optimization_barrier((basis, values, own_basis))
     parts = potential_parts(
         slots,
         got_tiles.reshape(owners * CAPB * BLK, width),
@@ -401,31 +455,55 @@
     potential = sum_at_column(parts)
     weighted = (weights[:, :, None] * potential).astype(BF16).reshape(batches * pts, width)
 
-    all_weighted = lax.all_gather(weighted, "grid", axis=0, tiled=True)
-    points_all = to_everyone(points.transpose(1, 0, 2).reshape(3 * batches, pts), "grid")
-    own_basis = basis_at_owner(pick, in_batch, own_params.T, points_all, batches)
-    fock = fock_at_owner(
-        pick, own_basis, all_weighted.reshape(owners, batches * pts, width), held
-    )
+    half = batches * pts // 2
+    side = lax.axis_size("z")
+    all_weighted = lax.all_gather(weighted[:half], GRID, axis=0, tiled=True)
+    line = to_everyone(weighted[half:], "y")
+    lined_basis = own_basis.reshape(lax.axis_size("y"), side, CAPB * BLK, batches * pts)
+    offsets = [0]
+    for step in range(1, side // 2 + 1):
+        offsets += [side - step, step]
+    lines = (lax.axis_index("z") + jnp.array(offsets[:side], jnp.int32)) & (side - 1)
+    ahead = [(i, (i + 1) % side) for i in range(side)]
+    behind = [(i, (i - 1) % side) for i in range(side)]
+    up = down = line
+    came = [line]
+    fock = None
+    for step in range(1, side // 2 + 1):
+        up = lax.ppermute(up, "z", ahead)
+        if step < side - step:
+            down = lax.ppermute(down, "z", behind)
+        fock = fock_from_lines(pick, lines, max(0, 2 * step - 3), lined_basis, came, fock, held)
+        if step < side - step:
+            up, down, fock = lax.optimization_barrier((up, down, fock))
+            came = [up, down]
+        else:
+            fock = fock_from_gather(
+                pick, own_basis, all_weighted.reshape(owners, half, width), fock
+            )
+            fock = fock_from_lines(pick, lines, 2 * step - 1, lined_basis, [up], fock, held)
     return fock.reshape(held * BLK, width)
 
 
 def solution(mesh):
+    columns = mesh.shape["col"]
+    side = math.isqrt(mesh.shape["grid"])
+    planes = Mesh(mesh.devices.reshape(-1, side, columns), (*GRID, "col"))
     return jax.shard_map(
         on_device,
-        mesh=mesh,
+        mesh=planes,
         in_specs=(
-            P("grid", "col"),
-            P(None, "grid"),
-            P("grid"),
+            P(GRID, "col"),
+            P(None, GRID),
+            P(GRID),
             P(None, "col"),
             P("col"),
-            P("grid", None, None),
-            P("grid", None),
+            P(GRID, None, None),
+            P(GRID, None),
             P(),
-            P("grid", "col"),
-            P("grid", "col"),
-        ),
-        out_specs=P("grid", "col"),
+            P(GRID, "col"),
+            P(GRID, "col"),
+        ),
+        out_specs=P(GRID, "col"),
         check_vma=False,
     )

time: 358 us -> 410 us (1.15)
  the two profiles are of different devices: /device:TPU:1 before, /device:TPU:64 now
where the time goes in v2:
time: 410 us; the launch traced here: 408 us
  waiting for transfers between devices  176 us (43%)
  Pallas kernels  114 us (28%)
  blocking collectives  44.8 us (11%)
  starting transfers between devices  41.6 us (10%)
  between operations  13.8 us (3%)
  other arithmetic  9 us (2%)
  local copies, waits for them, and re-layouts  8.9 us (2%)
    all_gather x1, waiting for transfers between devices, on_device(): gathered = lax.all_gather(sent, GRID, axis=0, tiled=True)  152 us
    pallas_call x5, Pallas kernels, fock_from_lines(): call(functools.partial(fock_line_kernel, first=first, count=count, side=s...  37.5 us
    all_to_all x1, blocking collectives, to_everyone(): lax.all_to_all(jnp.broadcast_to(value[None], (devices, *value.shape)), ax...  23.3 us
    all_to_all x1, blocking collectives, sum_at_column(): lax.all_to_all(jnp.concatenate([scaled, tail], axis=2), 'col', split_axis...  21.4 us
    pallas_call x1, Pallas kernels, basis_at_owner(): call(functools.partial(owner_basis_kernel, batches=batches), 'basis_at_ow...  19.3 us
    all_to_all x1, starting transfers between devices, on_device(): lax.all_to_all(tile_slots, GRID, split_axis=0, concat_axis=0, tiled=True)  16.1 us
    pallas_call x1, Pallas kernels, fock_from_gather(): call(fock_kernel, 'fock_from_gather', flops=2 * owners * rows * points *...  14.7 us
    pallas_call x1, Pallas kernels, pair_values(): call(pair_kernel, 'pair_values', flops=batches * pairs * pts * 400, grid_...  14.4 us
  transfers between devices with their start and end apart: 11, of which 7 were waited for; matrix products, arithmetic and copies ran while one was open for 3% of the time, Pallas kernels for 23%

profile of v2, /device:TPU:64, one launch (start us, length us, event | category | flops | bytes accessed | tf_op | source)
XLA Modules:
  0.0 407.7 jit_solution(2356675740468359139)
XLA Ops:
  7.9 4.3 %all-to-all-start = ((f32[8,4,128]{2,1,0:T(4,128)}), f32[8,4,128]{2,1,0:T(4,128)S(1)}, u32[]{:S(2)}, u32[]{:S(2)}) async-start(f32[8,4,128]{2,1,0:T(4,128)} %broadcast_in_dim.71), calls=%async_computation | async-start | bytes 32768 | tf_op jit(solution)/shard_map/all_to_all | solution.py:355
  14.2 5.4 %pack_slots.1 = bf16[64,256,128]{2,1,0:T(8,128)(2,1)} custom-call(s32[128]{0:T(128)} %select_n.35.pick, bf16[24,128,128]{2,1,0:T(8,128)(2,1)} %bitcast.49), custom_call_target="tpu_custom_call" | custom-call | tf_op jit(solution)/shard_map/pack_slots/pallas_call | solution.py:47
  19.7 16.1 %all-to-all-start.1 = ((bf16[64,256,128]{2,1,0:T(8,128)(2,1)}), bf16[64,256,128]{2,1,0:T(8,128)(2,1)}, u32[]{:S(2)}, u32[]{:S(2)}) async-start(bf16[64,256,128]{2,1,0:T(8,128)(2,1)} %pack_slots.1), calls=%async_computation.1 | async-start | bytes 8388608 | tf_op jit(solution)/shard_map/all_to_all | solution.py:433
  36.9 0.9 copy.59
  39.0 1.7 copy.65
  44.8 14.4 %pair_values.1.values = f32[4,128,2048]{2,1,0:T(8,128)} custom-call(s32[4,1,2048]{2,1,0:T(1,128)} %broadcast_in_dim.68.target, s32[4,1,2048]{2,1,0:T(1,128)} %broadcast_in_dim.69.source, bf16[16,1024]{1,0:T(8,128)(2,1)} %maximum_maximum_fusion.1.window, bf16[16,128]{1,0:T(8,128)(2,1)} %maximum_maximum_fusion.2.local, f32[4,128,3]{2,1,0:T(8,128)} %bitcast.47), custom_call_target="tpu_custom_call" | custom-call | flops 419430400 | tf_op jit(solution)/shard_map/pair_values/pallas_call | solution.py:147
  59.2 152.3 %all-gather.3.cloned.1.call-done.params = f32[7168,128]{1,0:T(8,128)} async-done(((f32[112,128]{1,0:T(8,128)}), f32[7168,128]{1,0:T(8,128)}) %all-gather.3.cloned.1.call-update) | async-done | bytes 3670032 | tf_op jit(solution)/shard_map/all_gather | solution.py:428
  211.5 8.5 %basis_for_field.1.basis = bf16[4,128,4096]{2,1,0:T(8,128)(2,1)} custom-call(s32[128]{0:T(128)} %get-tuple-element.33.rows_at, f32[7168,128]{1,0:T(8,128)} %all-gather.3.cloned.1.call-done.params, f32[4,128,3]{2,1,0:T(8,128)} %bitcast.48), custom_call_target="tpu_custom_call" | custom-call | flops 209715200 | tf_op jit(solution)/shard_map/basis_for_field/pallas_call | solution.py:80
  220.0 19.3 %basis_at_owner.1.basis = bf16[64,256,512]{2,1,0:T(8,128)(2,1)} custom-call(s32[128]{0:T(128)} %select_n.35.pick, s32[512]{0:T(512)} %reshape.150.listed, f32[3072,4]{1,0:T(8,128)} %bitcast.45, f32[64,112,128]{2,1,0:T(8,128)} %bitcast.44), custom_call_target="tpu_custom_call" | custom-call | flops 838860800 | tf_op jit(solution)/shard_map/basis_at_owner/pallas_call | solution.py:253
  239.3 14.0 %potential_parts.1 = f32[8,4,128,128]{3,2,1,0:T(8,128)} custom-call(s32[128]{0:T(128)} %convert_add_fusion.slots, bf16[16384,128]{1,0:T(8,128)(2,1)} %bitcast.20.tiles, bf16[4,128,4096]{2,1,0:T(8,128)(2,1)} %basis_for_field.1.basis, f32[4,128,2048]{2,1,0:T(8,128)} %pair_values.1.values, s32[4,1,2048]{2,1,0:T(1,128)} %broadcast_in_dim.68.target, ...), custom_call_target="tpu_custom_call" | custom-call | tf_op jit(solution)/shard_map/potential_parts/pallas_call | solution.py:195
  253.3 1.9 abs_reduce_fusion
  256.3 21.4 %all_to_all.20 = f16[8,4,144,128]{3,2,1,0:T(8,128)(2,1)S(1)} all-to-all(f16[8,4,144,128]{3,2,1,0:T(8,128)(2,1)S(1)} %pad_maximum_fusion), channel_id=1, replica_groups=mesh['y'=8,'z'=8,'col'=8] {'col'}, dimensions={0} | all-to-all | bytes 2359296 | tf_op jit(solution)/shard_map/all_to_all | solution.py:376
  279.2 23.3 %all_to_all.21.refs_1_ = bf16[8,256,128]{2,1,0:T(8,128)(2,1)S(1)} all-to-all(bf16[8,256,128]{2,1,0:T(8,128)(2,1)S(1)} %broadcast_in_dim.76), channel_id=1, replica_groups=mesh['y'=8,'z'=8,'col'=8] {'y'}, dimensions={0} | all-to-all | bytes 1048576 | tf_op jit(solution)/shard_map/all_to_all | solution.py:355
  302.6 2.8 collective-permute-start
  305.4 3.0 collective-permute-start.1
  308.9 6.6 %fock_from_lines.5.refs_4_ = f32[24,128,128]{2,1,0:T(8,128)} custom-call(s32[128]{0:T(128)} %select_n.35.pick, s32[8]{0:T(128)} %add_and_fusion.lines, bf16[8,8,256,512]{3,2,1,0:T(8,128)(2,1)} %bitcast.36, bf16[8,256,128]{2,1,0:T(8,128)(2,1)} %copy-done.1), custom_call_target="tpu_custom_call" | custom-call | flops 134217728 | tf_op jit(solution)/shard_map/fock_from_lines/pallas_call | solution.py:334
  315.5 1.7 collective-permute-done.refs_2_
  317.3 2.4 collective-permute-done.1.refs_3_
  319.6 3.5 collective-permute-start.2
  323.1 2.3 collective-permute-start.3
  325.5 7.9 %fock_from_lines.6.refs_4_ = f32[24,128,128]{2,1,0:T(8,128)} custom-call(s32[128]{0:T(128)} %select_n.35.pick, s32[8]{0:T(128)} %add_and_fusion.lines, bf16[8,8,256,512]{3,2,1,0:T(8,128)(2,1)} %bitcast.37, bf16[8,8,256,512]{3,2,1,0:T(8,128)(2,1)} %bitcast.38, bf16[8,256,128]{2,1,0:T(8,128)(2,1)} %copy-done.3, ...), custom_call_target="tpu_custom_call", output_to_operand_aliasing={{}: (6, {})} | custom-call | flops 268435456 | tf_op jit(solution)/shard_map/fock_from_lines/pallas_call | solution.py:334
  333.4 2.3 collective-permute-done.2.refs_2_
  335.7 9.1 %collective-permute-done.3.refs_3_ = bf16[8,256,128]{2,1,0:T(8,128)(2,1)S(1)} collective-permute-done((bf16[8,256,128]{2,1,0:T(8,128)(2,1)S(1)}, bf16[8,256,128]{2,1,0:T(8,128)(2,1)S(1)}, u32[]{:S(2)}, u32[]{:S(2)}) %collective-permute-start.3) | collective-permute-done | bytes 524320 | tf_op jit(solution)/shard_map/ppermute | solution.py:475
  344.8 1.9 collective-permute-start.4
  346.7 3.9 collective-permute-start.5
  350.7 8.0 %fock_from_lines.7.refs_4_ = f32[24,128,128]{2,1,0:T(8,128)} custom-call(s32[128]{0:T(128)} %select_n.35.pick, s32[8]{0:T(128)} %add_and_fusion.lines, bf16[8,8,256,512]{3,2,1,0:T(8,128)(2,1)} %bitcast.39, bf16[8,8,256,512]{3,2,1,0:T(8,128)(2,1)} %bitcast.40, bf16[8,256,128]{2,1,0:T(8,128)(2,1)} %copy-done.5, ...), custom_call_target="tpu_custom_call", output_to_operand_aliasing={{}: (6, {})} | custom-call | flops 268435456 | tf_op jit(solution)/shard_map/fock_from_lines/pallas_call | solution.py:334
  358.6 6.6 %collective-permute-done.4.refs_2_ = bf16[8,256,128]{2,1,0:T(8,128)(2,1)S(1)} collective-permute-done((bf16[8,256,128]{2,1,0:T(8,128)(2,1)S(1)}, bf16[8,256,128]{2,1,0:T(8,128)(2,1)S(1)}, u32[]{:S(2)}, u32[]{:S(2)}) %collective-permute-start.4) | collective-permute-done | bytes 524320 | tf_op jit(solution)/shard_map/ppermute | solution.py:473
  365.3 1.3 collective-permute-done.5.refs_3_
  366.6 3.6 collective-permute-start.6
  370.2 7.9 %fock_from_lines.8.before = f32[24,128,128]{2,1,0:T(8,128)} custom-call(s32[128]{0:T(128)} %select_n.35.pick, s32[8]{0:T(128)} %add_and_fusion.lines, bf16[8,8,256,512]{3,2,1,0:T(8,128)(2,1)} %bitcast.41, bf16[8,8,256,512]{3,2,1,0:T(8,128)(2,1)} %bitcast.42, bf16[8,256,128]{2,1,0:T(8,128)(2,1)} %copy-done.2, ...), custom_call_target="tpu_custom_call", output_to_operand_aliasing={{}: (6, {})} | custom-call | flops 268435456 | tf_op jit(solution)/shard_map/fock_from_lines/pallas_call | solution.py:334
  378.1 14.7 %fock_from_gather.1.refs_2_ = f32[24,128,128]{2,1,0:T(8,128)} custom-call(s32[128]{0:T(128)} %select_n.35.pick, bf16[64,256,512]{2,1,0:T(8,128)(2,1)} %basis_at_owner.1.basis, bf16[64,256,128]{2,1,0:T(8,128)(2,1)} %bitcast.46, f32[24,128,128]{2,1,0:T(8,128)} %fock_from_lines.8.before), custom_call_target="tpu_custom_call", output_to_operand_aliasing={{}: (3, {})} | custom-call | flops 1073741824 | tf_op jit(solution)/shard_map/fock_from_gather/pallas_call | solution.py:292
  393.6 7.2 %fock_from_lines.9 = f32[24,128,128]{2,1,0:T(8,128)} custom-call(s32[128]{0:T(128)} %select_n.35.pick, s32[8]{0:T(128)} %add_and_fusion.lines, bf16[8,8,256,512]{3,2,1,0:T(8,128)(2,1)} %bitcast.43, bf16[8,256,128]{2,1,0:T(8,128)(2,1)} %copy-done.8, f32[24,128,128]{2,1,0:T(8,128)} %fock_from_gather.1.refs_2_), custom_call_target="tpu_custom_call", output_to_operand_aliasing={{}: (4, {})} | custom-call | flops 134217728 | tf_op jit(solution)/shard_map/fock_from_lines/pallas_call | solution.py:334
  (94 shorter events, 13.6 us)
Async XLA Ops:
  7.9 11.8 %all-to-all-start = ((f32[8,4,128]{2,1,0:T(4,128)}), f32[8,4,128]{2,1,0:T(4,128)S(1)}, u32[]{:S(2)}, u32[]{:S(2)}) async-start(f32[8,4,128]{2,1,0:T(4,128)} %broadcast_in_dim.71), calls=%async_computation | async-start | bytes 32768 | tf_op jit(solution)/shard_map/all_to_all | solution.py:355
  19.6 16.2 %copy-start.14 = (f32[4,3,128]{2,0,1:T(4,128)S(1)}, f32[4,3,128]{2,0,1:T(4,128)}, u32[]{:S(2)}) copy-start(f32[4,3,128]{2,0,1:T(4,128)} %param.16) | copy-start | bytes 18436
  19.6 16.3 %copy-start.9 = (f32[3,3072]{1,0:T(4,128)S(1)}, f32[3,3072]{1,0:T(4,128)}, u32[]{:S(2)}) copy-start(f32[3,3072]{1,0:T(4,128)} %param.12) | copy-start | bytes 110596
  19.6 16.3 %copy-start.11 = (f32[3072]{0:T(1024)S(1)}, f32[3072]{0:T(1024)}, u32[]{:S(2)}) copy-start(f32[3072]{0:T(1024)} %param.13) | copy-start | bytes 36868
  19.6 17.1 %copy-start.10 = (s32[256,32]{0,1:T(8,128)S(1)}, s32[256,32]{0,1:T(8,128)}, u32[]{:S(2)}) copy-start(s32[256,32]{0,1:T(8,128)} %param.18) | copy-start | bytes 98308
  19.7 219.6 %all-to-all-start.1 = ((bf16[64,256,128]{2,1,0:T(8,128)(2,1)}), bf16[64,256,128]{2,1,0:T(8,128)(2,1)}, u32[]{:S(2)}, u32[]{:S(2)}) async-start(bf16[64,256,128]{2,1,0:T(8,128)(2,1)} %pack_slots.1), calls=%async_computation.1 | async-start | bytes 8388608 | tf_op jit(solution)/shard_map/all_to_all | solution.py:433
  35.8 5.0 %copy-start.12 = (s32[4,2048]{1,0:T(4,128)S(1)}, s32[4,2048]{1,0:T(4,128)}, u32[]{:S(2)}) copy-start(s32[4,2048]{1,0:T(4,128)} %param.19) | copy-start | bytes 98308
  35.8 5.6 %copy-start.13 = (s32[4,2048]{1,0:T(4,128)S(1)}, s32[4,2048]{1,0:T(4,128)}, u32[]{:S(2)}) copy-start(s32[4,2048]{1,0:T(4,128)} %param.20) | copy-start | bytes 98308
  35.8 175.7 %all-gather.3.cloned.1.call-start = ((), (), s32[]{:S(2)}) async-start(), calls=%async_computation.4 | async-start | bytes 3727360 | tf_op jit(solution)/shard_map/all_gather | solution.py:428
  36.7 341.4 %all-gather.5.cloned.1.call-start = ((), (), s32[]{:S(2)}) async-start(), calls=%async_computation.5 | async-start | bytes 4259840 | tf_op jit(solution)/shard_map/all_gather | solution.py:460
  253.3 2.2 copy-start
  256.3 22.0 %copy-start.15 = (f32[4,128]{1,0:T(4,128)S(1)}, f32[4,128]{1,0:T(4,128)}, u32[]{:S(2)}) copy-start(f32[4,128]{1,0:T(4,128)} %param.17) | copy-start | bytes 6148
  277.8 30.6 %copy-start.16 = (s32[8]{0:T(128)S(1)}, s32[8]{0:T(128)}, u32[]{:S(2)}) copy-start(s32[8]{0:T(128)} %constant.66.clone) | copy-start | bytes 100
  302.6 6.4 %copy-start.1 = (bf16[8,256,128]{2,1,0:T(8,128)(2,1)}, bf16[8,256,128]{2,1,0:T(8,128)(2,1)S(1)}, u32[]{:S(2)}) copy-start(bf16[8,256,128]{2,1,0:T(8,128)(2,1)S(1)} %all_to_all.21.refs_1_) | copy-start | bytes 1572868
  302.6 14.7 %collective-permute-start = (bf16[8,256,128]{2,1,0:T(8,128)(2,1)S(1)}, bf16[8,256,128]{2,1,0:T(8,128)(2,1)S(1)}, u32[]{:S(2)}, u32[]{:S(2)}) collective-permute-start(bf16[8,256,128]{2,1,0:T(8,128)(2,1)S(1)} %all_to_all.21.refs_1_), channel_id=1, source_target_pairs={{0,8},{8,16},{16,24},{24,32},{32,40},{40,48},{48,56},{56,0},{1,9},... | collective-permute-start | bytes 1572872 | tf_op jit(solution)/shard_map/ppermute | solution.py:473
  305.4 14.2 %collective-permute-start.1 = (bf16[8,256,128]{2,1,0:T(8,128)(2,1)S(1)}, bf16[8,256,128]{2,1,0:T(8,128)(2,1)S(1)}, u32[]{:S(2)}, u32[]{:S(2)}) collective-permute-start(bf16[8,256,128]{2,1,0:T(8,128)(2,1)S(1)} %all_to_all.21.refs_1_), channel_id=1, source_target_pairs={{0,56},{8,0},{16,8},{24,16},{32,24},{40,32},{48,40},{56,48},{1,57}... | collective-permute-start | bytes 1572872 | tf_op jit(solution)/shard_map/ppermute | solution.py:475
  317.2 8.2 %copy-start.3 = (bf16[8,256,128]{2,1,0:T(8,128)(2,1)}, bf16[8,256,128]{2,1,0:T(8,128)(2,1)S(1)}, u32[]{:S(2)}) copy-start(bf16[8,256,128]{2,1,0:T(8,128)(2,1)S(1)} %collective-permute-done.refs_2_) | copy-start | bytes 1572868
  319.6 5.9 %copy-start.4 = (bf16[8,256,128]{2,1,0:T(8,128)(2,1)}, bf16[8,256,128]{2,1,0:T(8,128)(2,1)S(1)}, u32[]{:S(2)}) copy-start(bf16[8,256,128]{2,1,0:T(8,128)(2,1)S(1)} %collective-permute-done.1.refs_3_) | copy-start | bytes 1572868
  319.6 16.1 %collective-permute-start.2 = (bf16[8,256,128]{2,1,0:T(8,128)(2,1)S(1)}, bf16[8,256,128]{2,1,0:T(8,128)(2,1)S(1)}, u32[]{:S(2)}, u32[]{:S(2)}) collective-permute-start(bf16[8,256,128]{2,1,0:T(8,128)(2,1)S(1)} %collective-permute-done.refs_2_), channel_id=1, source_target_pairs={{0,8},{8,16},{16,24},{24,32},{32,40},{40,48},{48,56},{56,0},{1,9},... | collective-permute-start | bytes 1572872 | tf_op jit(solution)/shard_map/ppermute | solution.py:473
  323.1 21.7 %collective-permute-start.3 = (bf16[8,256,128]{2,1,0:T(8,128)(2,1)S(1)}, bf16[8,256,128]{2,1,0:T(8,128)(2,1)S(1)}, u32[]{:S(2)}, u32[]{:S(2)}) collective-permute-start(bf16[8,256,128]{2,1,0:T(8,128)(2,1)S(1)} %collective-permute-done.1.refs_3_), channel_id=1, source_target_pairs={{0,56},{8,0},{16,8},{24,16},{32,24},{40,32},{48,40},{56,48},{1,57}... | collective-permute-start | bytes 1572872 | tf_op jit(solution)/shard_map/ppermute | solution.py:475
  335.7 15.0 %copy-start.5 = (bf16[8,256,128]{2,1,0:T(8,128)(2,1)}, bf16[8,256,128]{2,1,0:T(8,128)(2,1)S(1)}, u32[]{:S(2)}) copy-start(bf16[8,256,128]{2,1,0:T(8,128)(2,1)S(1)} %collective-permute-done.2.refs_2_) | copy-start | bytes 1572868
  344.8 5.9 %copy-start.6 = (bf16[8,256,128]{2,1,0:T(8,128)(2,1)}, bf16[8,256,128]{2,1,0:T(8,128)(2,1)S(1)}, u32[]{:S(2)}) copy-start(bf16[8,256,128]{2,1,0:T(8,128)(2,1)S(1)} %collective-permute-done.3.refs_3_) | copy-start | bytes 1572868
  344.8 20.5 %collective-permute-start.4 = (bf16[8,256,128]{2,1,0:T(8,128)(2,1)S(1)}, bf16[8,256,128]{2,1,0:T(8,128)(2,1)S(1)}, u32[]{:S(2)}, u32[]{:S(2)}) collective-permute-start(bf16[8,256,128]{2,1,0:T(8,128)(2,1)S(1)} %collective-permute-done.2.refs_2_), channel_id=1, source_target_pairs={{0,8},{8,16},{16,24},{24,32},{32,40},{40,48},{48,56},{56,0},{1,9},... | collective-permute-start | bytes 1572872 | tf_op jit(solution)/shard_map/ppermute | solution.py:473
  346.7 19.8 %collective-permute-start.5 = (bf16[8,256,128]{2,1,0:T(8,128)(2,1)S(1)}, bf16[8,256,128]{2,1,0:T(8,128)(2,1)S(1)}, u32[]{:S(2)}, u32[]{:S(2)}) collective-permute-start(bf16[8,256,128]{2,1,0:T(8,128)(2,1)S(1)} %collective-permute-done.3.refs_3_), channel_id=1, source_target_pairs={{0,56},{8,0},{16,8},{24,16},{32,24},{40,32},{48,40},{56,48},{1,57}... | collective-permute-start | bytes 1572872 | tf_op jit(solution)/shard_map/ppermute | solution.py:475
  365.3 4.9 %copy-start.2 = (bf16[8,256,128]{2,1,0:T(8,128)(2,1)}, bf16[8,256,128]{2,1,0:T(8,128)(2,1)S(1)}, u32[]{:S(2)}) copy-start(bf16[8,256,128]{2,1,0:T(8,128)(2,1)S(1)} %collective-permute-done.4.refs_2_) | copy-start | bytes 1572868
  366.6 3.7 copy-start.7
  366.6 26.2 %collective-permute-start.6 = (bf16[8,256,128]{2,1,0:T(8,128)(2,1)S(1)}, bf16[8,256,128]{2,1,0:T(8,128)(2,1)S(1)}, u32[]{:S(2)}, u32[]{:S(2)}) collective-permute-start(bf16[8,256,128]{2,1,0:T(8,128)(2,1)S(1)} %collective-permute-done.4.refs_2_), channel_id=1, source_target_pairs={{0,8},{8,16},{16,24},{24,32},{32,40},{40,48},{48,56},{56,0},{1,9},... | collective-permute-start | bytes 1572872 | tf_op jit(solution)/shard_map/ppermute | solution.py:473
  392.8 0.8 copy-start.8
Sparse Core Ops, SparseCore 0:
  39.7 171.7 all-gather.2
  279.3 87.5 all-gather.4

commit v3 on v2

v3 whole, which is shorter than its diff:
```python
import functools
import math

import jax
import jax.numpy as jnp
from jax import lax
from jax.experimental import pallas as pl
from jax.experimental.pallas import tpu as pltpu
from jax.sharding import Mesh
from jax.sharding import PartitionSpec as P

BLK = 128
CAPB = 2
PARAMS = 4
CHUNK = 512
STEP_OWNERS = 4
SCALE_ROWS = 16
PARTS = 2
GRID = ("y", "z")
quad_nodes = 8
F32 = jnp.float32
BF16 = jnp.bfloat16


def call(kernel, name, flops=0, **kwargs):
    return pl.pallas_call(
        kernel,
        name=name,
        compiler_params=pltpu.CompilerParams(
            dimension_semantics=("arbitrary",) * len(kwargs["grid_spec"].grid),
        ),
        cost_estimate=pl.CostEstimate(flops=flops, transcendentals=0, bytes_accessed=0),
        **kwargs,
    )


def line_basis_kernel(rows_at, listed, gathered, points, out, spots, *, batches, slots):
    place = pl.program_id(0)
    for row in range(3 * batches):
        spots[row] = jnp.broadcast_to(points[0, :, row : row + 1], spots.shape[1:])

    def one_slot(slot, carry):
        row = rows_at[place * slots + slot]
        lanes = pl.ds(pl.multiple_of(slot * BLK, BLK), BLK)
        for batch in range(batches):
            keep = listed[(place * slots + slot) * batches + batch]
            here = (0, slice(batch * BLK, (batch + 1) * BLK), lanes)

            @pl.when(keep > 0)
            def _():
                squared = None
                for axis in range(3):
                    delta = spots[axis * batches + batch] - gathered[pl.ds(row + axis, 1), :]
                    squared = delta * delta if squared is None else squared + delta * delta
                out[here] = jnp.exp(-gathered[pl.ds(row + 3, 1), :] * squared).astype(BF16)

            @pl.when(keep == 0)
            def _():
                out[here] = jnp.zeros((BLK, BLK), BF16)

        return carry

    lax.fori_loop(0, slots, one_slot, 0)


def line_basis(rows_at, listed, gathered, points_t, batches):
    places, pts, rows = points_t.shape
    slots = rows_at.shape[0] // places
    return call(
        functools.partial(line_basis_kernel, batches=batches, slots=slots),
        "line_basis",
        flops=places * batches * pts * slots * BLK * 50,
        grid_spec=pltpu.PrefetchScalarGridSpec(
            num_scalar_prefetch=2,
            grid=(places,),
            in_specs=[
                pl.BlockSpec(gathered.shape, lambda i, *_: (0, 0)),
                pl.BlockSpec((1, pts, rows), lambda i, *_: (i, 0, 0)),
            ],
            out_specs=pl.BlockSpec((1, batches * pts, slots * BLK), lambda i, *_: (i, 0, 0)),
            scratch_shapes=[pltpu.VMEM((rows, pts, BLK), F32)],
        ),
        out_shape=jax.ShapeDtypeStruct((places, batches * pts, slots * BLK), BF16),
    )(rows_at, listed, gathered, points_t)


def line_field_kernel(tiles_at, tiles, basis, out, rows, *, slots):
    place = pl.program_id(0)
    for slot in range(slots):
        rows[slot * BLK : (slot + 1) * BLK, :] = tiles[tiles_at[place * slots + slot]]
    out[0] = jnp.dot(basis[0], rows[...], preferred_element_type=F32)


def line_field(tiles_at, tiles, basis, part, parts):
    places, points, functions = basis.shape
    count, _, width = tiles.shape
    points //= parts
    return call(
        functools.partial(line_field_kernel, slots=functions // BLK),
        "line_field",
        flops=2 * places * points * functions * width,
        grid_spec=pltpu.PrefetchScalarGridSpec(
            num_scalar_prefetch=1,
            grid=(places,),
            in_specs=[
                pl.BlockSpec((count, BLK, width), lambda i, *_: (0, 0, 0)),
                pl.BlockSpec((1, points, functions), lambda i, *_: (i, part, 0)),
            ],
            out_specs=pl.BlockSpec((1, points, width), lambda i, *_: (i, 0, 0)),
            scratch_shapes=[pltpu.VMEM((functions, width), BF16)],
        ),
        out_shape=jax.ShapeDtypeStruct((places, points, width), F32),
    )(tiles_at, tiles, basis)


def one_hot(columns, rows):
    spot = lax.broadcasted_iota(jnp.int32, (rows, columns.shape[1]), 0)
    return jnp.where(spot == columns, 1.0, 0.0).astype(BF16)


def rejoin(picked):
    return picked[0:4] + picked[4:8] + picked[8:12]


def pair_kernel(target, source, window, local, points, out, spots):
    @pl.when(pl.program_id(1) == 0)
    def _():
        for axis in range(3):
            spots[axis] = jnp.broadcast_to(points[0, :, axis : axis + 1], spots.shape[1:])

    target_par = rejoin(
        jnp.dot(window[...], one_hot(target[0], window.shape[1]), preferred_element_type=F32)
    )
    source_par = rejoin(
        jnp.dot(local[...], one_hot(source[0], local.shape[1]), preferred_element_type=F32)
    )
    target_exp, source_exp = target_par[3:4], source_par[3:4]
    joined = target_exp + source_exp
    separation = jnp.zeros_like(joined)
    centres = []
    for axis in range(3):
        here, there = target_par[axis : axis + 1], source_par[axis : axis + 1]
        offset = here - there
        separation = separation + offset * offset
        centres.append((target_exp * here + source_exp * there) / joined)
    prefactor = 2.0 * math.pi / joined * jnp.exp(-target_exp * source_exp / joined * separation)
    lanes = spots.shape[2]
    for first in range(0, joined.shape[1], lanes):
        part = slice(first, first + lanes)
        spread = None
        for axis in range(3):
            delta = spots[axis] - centres[axis][:, part]
            spread = delta * delta if spread is None else spread + delta * delta
        argument = joined[:, part] * spread
        summed = jnp.zeros_like(argument)
        for quad_node in range(quad_nodes):
            node_spot = (quad_node + 0.5) / quad_nodes
            summed = summed + jnp.exp(-argument * (node_spot * node_spot))
        out[0, :, part] = prefactor[:, part] * (summed / quad_nodes)


def pair_values(target, source, window, local, points_t):
    batches, _, pairs = target.shape
    pts = points_t.shape[1]
    return call(
        pair_kernel,
        "pair_values",
        flops=batches * pairs * pts * 400,
        grid_spec=pltpu.PrefetchScalarGridSpec(
            num_scalar_prefetch=0,
            grid=(batches, pairs // CHUNK),
            in_specs=[
                pl.BlockSpec((1, 1, CHUNK), lambda b, n: (b, 0, n)),
                pl.BlockSpec((1, 1, CHUNK), lambda b, n: (b, 0, n)),
                pl.BlockSpec(window.shape, lambda b, n: (0, 0)),
                pl.BlockSpec(local.shape, lambda b, n: (0, 0)),
                pl.BlockSpec((1, pts, 3), lambda b, n: (b, 0, 0)),
            ],
            out_specs=pl.BlockSpec((1, pts, CHUNK), lambda b, n: (b, 0, n)),
            scratch_shapes=[pltpu.VMEM((3, pts, BLK), F32)],
        ),
        out_shape=jax.ShapeDtypeStruct((batches, pts, pairs), F32),
    )(target, source, window, local, points_t)


def potential_kernel(field, values, target, source, out):
    columns, width = out.shape[0], out.shape[3]
    window_count = columns * width
    potential = jnp.zeros((field.shape[1], window_count), F32)
    for first in range(0, values.shape[2], CHUNK):
        part = slice(first, first + CHUNK)
        picked = jnp.dot(field[0], one_hot(source[0, :, part], width), preferred_element_type=F32)
        product = (values[0, :, part] * picked).astype(BF16)
        potential += lax.dot_general(
            product,
            one_hot(target[0, :, part], window_count),
            (((1,), (1,)), ((), ())),
            preferred_element_type=F32,
        )
    for column in range(columns):
        out[column, 0] = potential[:, column * width : (column + 1) * width]


def potential_parts(field, values, target, source, first, columns):
    batches, pts, width = field.shape
    pairs = values.shape[2]
    return call(
        potential_kernel,
        "potential_parts",
        flops=2 * batches * pts * pairs * columns * width,
        grid_spec=pltpu.PrefetchScalarGridSpec(
            num_scalar_prefetch=0,
            grid=(batches,),
            in_specs=[
                pl.BlockSpec((1, pts, width), lambda b: (b, 0, 0)),
                pl.BlockSpec((1, pts, pairs), lambda b: (first + b, 0, 0)),
                pl.BlockSpec((1, 1, pairs), lambda b: (first + b, 0, 0)),
                pl.BlockSpec((1, 1, pairs), lambda b: (first + b, 0, 0)),
            ],
            out_specs=pl.BlockSpec((columns, 1, pts, width), lambda b: (0, b, 0, 0)),
        ),
        out_shape=jax.ShapeDtypeStruct((columns, batches, pts, width), F32),
    )(field, values, target, source)


def owner_basis_kernel(pick, listed, points_at, params, gathered, out, spread_params, *, batches):
    @pl.when(pl.program_id(0) == 0)
    def _():
        for block in range(spread_params.shape[0]):
            for which in range(PARAMS):
                spread_params[block, which] = jnp.broadcast_to(
                    params[block * BLK : (block + 1) * BLK, which : which + 1], (BLK, BLK)
                )

    def one_owner(owner, carry):
        place = pl.program_id(0) * STEP_OWNERS + owner
        for slot in range(CAPB):
            block = pick[place * CAPB + slot]
            for batch in range(batches):
                here = (owner, slice(slot * BLK, (slot + 1) * BLK), slice(batch * BLK, (batch + 1) * BLK))
                keep = listed[(place * CAPB + slot) * batches + batch]

                @pl.when(keep > 0)
                def _():
                    squared = None
                    for axis in range(3):
                        row = points_at[place] + axis * batches + batch
                        delta = gathered[pl.ds(row, 1), :] - spread_params[block, axis]
                        squared = delta * delta if squared is None else squared + delta * delta
                    out[here] = jnp.exp(-spread_params[block, 3] * squared).astype(BF16)

                @pl.when(keep == 0)
                def _():
                    out[here] = jnp.zeros((BLK, BLK), BF16)

        return carry

    lax.fori_loop(0, STEP_OWNERS, one_owner, 0)


def basis_at_owner(pick, listed, points_at, params_t, gathered, batches, pts):
    owners = points_at.shape[0]
    held = params_t.shape[0] // BLK
    return call(
        functools.partial(owner_basis_kernel, batches=batches),
        "basis_at_owner",
        flops=owners * CAPB * BLK * batches * pts * 50,
        grid_spec=pltpu.PrefetchScalarGridSpec(
            num_scalar_prefetch=3,
            grid=(owners // STEP_OWNERS,),
            in_specs=[
                pl.BlockSpec(params_t.shape, lambda i, *_: (0, 0)),
                pl.BlockSpec(gathered.shape, lambda i, *_: (0, 0)),
            ],
            out_specs=pl.BlockSpec((STEP_OWNERS, CAPB * BLK, batches * pts), lambda i, *_: (i, 0, 0)),
            scratch_shapes=[pltpu.VMEM((held, PARAMS, BLK, BLK), F32)],
        ),
        out_shape=jax.ShapeDtypeStruct((owners, CAPB * BLK, batches * pts), BF16),
    )(pick, listed, points_at, params_t, gathered)


def add_rows(out, pick, place, rows):
    for slot in range(CAPB):
        block = pick[place * CAPB + slot]
        out[block] = out[block] + rows[slot * BLK : (slot + 1) * BLK]


def fock_kernel(pick, basis, weighted, *refs):
    out = refs[-1]

    @pl.when(pl.program_id(0) == 0)
    def _():
        out[...] = refs[0][...] if len(refs) > 1 else jnp.zeros_like(out)

    for owner in range(STEP_OWNERS):
        place = pl.program_id(0) * STEP_OWNERS + owner
        add_rows(out, pick, place, jnp.dot(basis[owner], weighted[owner], preferred_element_type=F32))


def fock_at_owner(pick, basis, weighted, part, before, held):
    owners, rows, _ = basis.shape
    _, points, width = weighted.shape
    whole = pl.BlockSpec((held, BLK, width), lambda i, *_: (0, 0, 0))
    return call(
        fock_kernel,
        "fock_at_owner",
        flops=2 * owners * rows * points * width,
        grid_spec=pltpu.PrefetchScalarGridSpec(
            num_scalar_prefetch=1,
            grid=(owners // STEP_OWNERS,),
            in_specs=[
                pl.BlockSpec((STEP_OWNERS, rows, points), lambda i, *_: (i, 0, part)),
                pl.BlockSpec((STEP_OWNERS, points, width), lambda i, *_: (i, 0, 0)),
            ]
            + ([] if before is None else [whole]),
            out_specs=whole,
        ),
        out_shape=jax.ShapeDtypeStruct((held, BLK, width), F32),
        input_output_aliases={} if before is None else {3: 0},
    )(pick, basis, weighted, *([] if before is None else [before]))


def to_everyone(value, axis):
    devices = lax.axis_size(axis)
    return lax.all_to_all(
        jnp.broadcast_to(value[None], (devices, *value.shape)), axis, 0, 0, tiled=True
    )


def in_parts(values):
    high = lax.reduce_precision(values, 8, 7)
    middle = lax.reduce_precision(values - high, 8, 7)
    low = values - high - middle
    parts = jnp.concatenate([high, middle, low, jnp.zeros_like(low)], axis=0)
    return parts.astype(BF16)


def sum_at_column(parts):
    columns, batches, pts, width = parts.shape
    largest = jnp.max(jnp.abs(parts), axis=(0, 2, 3))
    power = jnp.clip(13.0 - jnp.ceil(jnp.log2(largest)), -100.0, 100.0)
    scaled = (parts * jnp.exp2(power)[None, :, None, None]).astype(jnp.float16)
    tail = jnp.broadcast_to(
        power[None, :, None, None], (columns, batches, SCALE_ROWS, width)
    ).astype(jnp.float16)
    got = lax.all_to_all(
        jnp.concatenate([scaled, tail], axis=2), "col", split_axis=0, concat_axis=0, tiled=True
    )
    factor = jnp.exp2(-got[:, :, pts : pts + 1, 0:1].astype(F32))
    return jnp.sum(got[:, :, :pts].astype(F32) * factor, axis=0)


def slots_of(lists, base, held, batches):
    spot = lists - base
    owned = (spot >= 0) & (spot < held)
    lowest = jnp.min(jnp.where(owned, spot, held), axis=-1)
    highest = jnp.max(jnp.where(owned, spot, -1), axis=-1)
    ends = jnp.stack([lowest, highest], axis=-1)
    pick = jnp.where((highest >= 0)[..., None], ends, 0).astype(jnp.int32)
    hit = owned[..., None, :] & (spot[..., None, :] == ends[..., None])
    hit = hit & ((lowest != highest)[..., None] | (jnp.arange(CAPB) == 0))[..., None]
    listed = jnp.any(hit.reshape(*hit.shape[:-1], batches, -1), axis=-1)
    return pick, listed.astype(jnp.int32)


def on_device(
    density,
    row_centers,
    row_exps,
    win_centers,
    win_exps,
    points,
    weights,
    sig_blocks,
    pair_target,
    pair_source,
):
    lines, side = lax.axis_size("y"), lax.axis_size("z")
    owners = lines * side
    columns = lax.axis_size("col")
    line, place, column = lax.axis_index("y"), lax.axis_index("z"), lax.axis_index("col")
    held = row_exps.shape[0] // BLK
    width = density.shape[1]
    batches, _, pts = points.shape

    tiles = lax.all_gather(density, "z", axis=0, tiled=True).reshape(side * held, BLK, width)

    own_params = jnp.concatenate([row_centers, row_exps[None, :]], axis=0)
    own_blocks = own_params.reshape(PARAMS, held, BLK).transpose(1, 0, 2).reshape(columns, -1, BLK)
    block_rows = own_blocks.shape[1]
    own_points = points.transpose(1, 0, 2).reshape(3 * batches, pts)
    line_points = to_everyone(own_points, "y")
    point_rows = own_points.shape[0]
    shared = jnp.concatenate(
        [
            lax.dynamic_index_in_dim(own_blocks, column, 0, keepdims=False),
            lax.dynamic_index_in_dim(line_points, column, 0, keepdims=False),
        ],
        axis=0,
    )
    shared = to_everyone(shared, "z").reshape(-1, BLK)
    local_window = jnp.concatenate([win_centers, win_exps[None, :]], axis=0)
    spare = jnp.zeros_like(local_window)
    gathered = to_everyone(jnp.concatenate([shared, local_window, spare], axis=0), "col")
    rows_each = gathered.shape[1]
    whole_window = gathered[:, shared.shape[0] : shared.shape[0] + PARAMS]
    whole_window = whole_window.transpose(1, 0, 2).reshape(PARAMS, -1)
    gathered = gathered.reshape(-1, BLK)

    lists = sig_blocks.reshape(lines, side, -1)
    rows_of_place = block_rows + point_rows
    line_lists = lax.dynamic_index_in_dim(lists, place, 1, keepdims=True)
    base = (line * side + jnp.arange(side, dtype=jnp.int32)) * held
    line_pick, line_listed = slots_of(line_lists, base[None, :, None], held, batches)
    tiles_at = line_pick + (jnp.arange(side, dtype=jnp.int32) * held)[None, :, None]
    blocks_each = held // columns
    rows_at = (
        line_pick // blocks_each * rows_each
        + (jnp.arange(side, dtype=jnp.int32) * rows_of_place)[None, :, None]
        + line_pick % blocks_each * PARAMS
    )
    my_base = (line * side + place) * held
    pick, listed = slots_of(lists.reshape(owners, -1), my_base, held, batches)
    pick, listed = pick.reshape(-1), listed.reshape(-1)
    points_at = (
        jnp.arange(lines, dtype=jnp.int32)[:, None] * rows_each
        + jnp.arange(side, dtype=jnp.int32)[None, :] * rows_of_place
        + block_rows
    ).reshape(-1)

    points_t = points.transpose(0, 2, 1)
    target = pair_target[:, None, :]
    source = pair_source[:, None, :]
    basis = line_basis(
        rows_at.reshape(-1),
        line_listed.reshape(-1),
        gathered,
        line_points.transpose(0, 2, 1),
        batches,
    )
    values = pair_values(target, source, in_parts(whole_window), in_parts(local_window), points_t)
    basis, values = lax.optimization_barrier((basis, values))

    together = batches // PARTS
    weighted = []
    for part in range(PARTS):
        share = line_field(tiles_at.reshape(-1), tiles, basis, part, PARTS)
        field = lax.psum_scatter(
            share.reshape(-1, width), "y", scatter_dimension=0, tiled=True
        ).astype(BF16)
        parts = potential_parts(
            field.reshape(together, pts, width), values, target, source, part * together, columns
        )
        potential = sum_at_column(parts)
        scale = weights[part * together : (part + 1) * together, :, None]
        weighted.append((scale * potential).astype(BF16).reshape(together * pts, width))

    everyone = [lax.all_gather(value, GRID, axis=0, tiled=True) for value in weighted]
    gathered, weighted = lax.optimization_barrier((gathered, weighted[-1]))
    own_basis = basis_at_owner(pick, listed, points_at, own_params.T, gathered, batches, pts)
    fock = None
    for part, value in enumerate(everyone):
        value = value.reshape(owners, together * pts, width)
        fock = fock_at_owner(pick, own_basis, value, part, fock, held)
    return fock.reshape(held * BLK, width)


def solution(mesh):
    columns = mesh.shape["col"]
    side = math.isqrt(mesh.shape["grid"])
    planes = Mesh(mesh.devices.reshape(-1, side, columns), (*GRID, "col"))
    return jax.shard_map(
        on_device,
        mesh=planes,
        in_specs=(
            P(GRID, "col"),
            P(None, GRID),
            P(GRID),
            P(None, "col"),
            P("col"),
            P(GRID, None, None),
            P(GRID, None),
            P(),
            P(GRID, "col"),
            P(GRID, "col"),
        ),
        out_specs=P(GRID, "col"),
        check_vma=False,
    )
```

time: 410 us -> 386 us (0.941)
  the two profiles are of different devices: /device:TPU:64 before, /device:TPU:1 now
where the time goes in v3:
time: 386 us; the launch traced here: 381 us
  waiting for transfers between devices  162 us (42%)
  Pallas kernels  114 us (30%)
  starting transfers between devices  35.6 us (9%)
  blocking collectives  19.2 us (5%)
  other arithmetic  18.5 us (5%)
  local copies, waits for them, and re-layouts  17.8 us (5%)
  between operations  13.4 us (3%)
    all_gather x2, waiting for transfers between devices, on_device(): lax.all_gather(value, GRID, axis=0, tiled=True)  106 us
    reduce_scatter x2, waiting for transfers between devices, on_device(): lax.psum_scatter(share.reshape(-1, width), 'y', scatter_dimension=0, tile...  30.2 us
    pallas_call x2, Pallas kernels, fock_at_owner(): call(fock_kernel, 'fock_at_owner', flops=2 * owners * rows * points * wid...  28.6 us
    all_to_all x3, starting transfers between devices, to_everyone(): lax.all_to_all(jnp.broadcast_to(value[None], (devices, *value.shape)), ax...  25.5 us
    pallas_call x2, Pallas kernels, line_field(): call(functools.partial(line_field_kernel, slots=functions // BLK), 'line_...  21.8 us
    pallas_call x1, Pallas kernels, basis_at_owner(): call(functools.partial(owner_basis_kernel, batches=batches), 'basis_at_ow...  19.5 us
    all_to_all x1, blocking collectives, sum_at_column(): lax.all_to_all(jnp.concatenate([scaled, tail], axis=2), 'col', split_axis...  19.2 us
    pallas_call x1, Pallas kernels, line_basis(): call(functools.partial(line_basis_kernel, batches=batches, slots=slots),...  18.2 us
  transfers between devices with their start and end apart: 9, of which 8 were waited for; matrix products, arithmetic and copies ran while one was open for 9% of the time, Pallas kernels for 23%

profile of v3, /device:TPU:1, one launch (start us, length us, event | category | flops | bytes accessed | tf_op | source)
XLA Modules:
  0.0 380.6 jit_solution(11034186061652004281)
XLA Ops:
  8.6 7.6 %all-to-all-start = ((f32[8,12,128]{2,1,0:T(8,128)}), f32[8,12,128]{2,1,0:T(8,128)S(1)}, u32[]{:S(2)}, u32[]{:S(2)}) async-start(f32[8,12,128]{2,1,0:T(8,128)} %broadcast_in_dim.63), calls=%async_computation | async-start | bytes 131072 | tf_op jit(solution)/shard_map/all_to_all | solution.py:325
  20.2 3.3 all-to-all-done
  24.1 10.0 %all-to-all-start.1 = ((f32[8,24,128]{2,1,0:T(8,128)}), f32[8,24,128]{2,1,0:T(8,128)S(1)}, u32[]{:S(2)}, u32[]{:S(2)}) async-start(f32[8,24,128]{2,1,0:T(8,128)} %broadcast_in_dim.64), calls=%async_computation.1 | async-start | bytes 196608 | tf_op jit(solution)/shard_map/all_to_all | solution.py:325
  34.2 1.6 copy.86
  36.0 1.4 broadcast_in_dim.118.target
  37.3 1.4 broadcast_in_dim.119.source
  40.3 2.6 all-to-all-done.1
  44.7 7.8 %all-to-all-start.2 = ((f32[8,200,128]{2,1,0:T(8,128)}), f32[8,200,128]{2,1,0:T(8,128)S(1)}, u32[]{:S(2)}, u32[]{:S(2)}) async-start(f32[8,200,128]{2,1,0:T(8,128)} %broadcast_in_dim.66), calls=%async_computation.2 | async-start | bytes 1638400 | tf_op jit(solution)/shard_map/all_to_all | solution.py:325
  55.7 9.3 %all-to-all-done.2 = f32[8,200,128]{2,1,0:T(8,128)S(1)} async-done(((f32[8,200,128]{2,1,0:T(8,128)}), f32[8,200,128]{2,1,0:T(8,128)S(1)}, u32[]{:S(2)}, u32[]{:S(2)}) %all-to-all-start.2) | async-done | bytes 819232 | tf_op jit(solution)/shard_map/all_to_all | solution.py:325
  65.9 18.2 %line_basis.1.basis = bf16[8,512,2048]{2,1,0:T(8,128)(2,1)} custom-call(s32[128]{0:T(128)} %get-tuple-element.30.rows_at, s32[512]{0:T(512)} %reshape.228.listed, f32[1600,128]{1,0:T(8,128)} %bitcast.58, f32[8,128,12]{2,1,0:T(8,128)} %bitcast.65), custom_call_target="tpu_custom_call" | custom-call | flops 419430400 | tf_op jit(solution)/shard_map/line_basis/pallas_call | solution.py:69
  85.6 14.4 %pair_values.1.values = f32[4,128,2048]{2,1,0:T(8,128)} custom-call(s32[4,1,2048]{2,1,0:T(1,128)} %broadcast_in_dim.118.target, s32[4,1,2048]{2,1,0:T(1,128)} %broadcast_in_dim.119.source, bf16[16,1024]{1,0:T(8,128)(2,1)} %maximum_maximum_fusion.1.window, bf16[16,128]{1,0:T(8,128)(2,1)} %maximum_maximum_fusion.2.local, f32[4,128,3]{2,1,0:T(8,128)} %bitcast.66), custom_call_target="tpu_custom_call" | custom-call | flops 419430400 | tf_op jit(solution)/shard_map/pair_values/pallas_call | solution.py:165
  100.0 10.9 %line_field.3 = f32[8,256,128]{2,1,0:T(8,128)} custom-call(s32[128]{0:T(128)} %get-tuple-element.31.tiles_at, bf16[192,128,128]{2,1,0:T(8,128)(2,1)} %bitcast.56, bf16[8,512,2048]{2,1,0:T(8,128)(2,1)} %line_basis.1.basis), custom_call_target="tpu_custom_call" | custom-call | flops 1073741824 | tf_op jit(solution)/shard_map/line_field/pallas_call | solution.py:98
  111.0 10.9 %line_field.2 = f32[8,256,128]{2,1,0:T(8,128)} custom-call(s32[128]{0:T(128)} %get-tuple-element.31.tiles_at, bf16[192,128,128]{2,1,0:T(8,128)(2,1)} %bitcast.57, bf16[8,512,2048]{2,1,0:T(8,128)(2,1)} %line_basis.1.basis), custom_call_target="tpu_custom_call" | custom-call | flops 1073741824 | tf_op jit(solution)/shard_map/line_field/pallas_call | solution.py:98
  122.0 18.4 %reduce-scatter.5.cloned.1.call-done = f32[256,128]{1,0:T(8,128)} async-done(((f32[2048,128]{1,0:T(8,128)}), f32[256,128]{1,0:T(8,128)}) %reduce-scatter.5.cloned.1.call-update) | async-done | bytes 131088 | tf_op jit(solution)/shard_map/reduce_scatter | solution.py:448
  140.4 1.5 convert_element_type.66
  141.9 5.7 %potential_parts.3 = f32[8,2,128,128]{3,2,1,0:T(8,128)} custom-call(bf16[2,128,128]{2,1,0:T(8,128)(2,1)} %bitcast.70, f32[4,128,2048]{2,1,0:T(8,128)} %pair_values.1.values, s32[4,1,2048]{2,1,0:T(1,128)} %broadcast_in_dim.118.target, s32[4,1,2048]{2,1,0:T(1,128)} %broadcast_in_dim.119.source), custom_call_target="tpu_custom_call" | custom-call | flops 1073741824 | tf_op jit(solution)/shard_map/potential_parts/pallas_call | solution.py:207
  147.6 1.4 abs_reduce_fusion
  149.0 1.4 multiply_convert_fusion
  151.5 10.0 %all-to-all-start.4 = ((f16[8,2,144,128]{3,2,1,0:T(8,128)(2,1)}), f16[8,2,144,128]{3,2,1,0:T(8,128)(2,1)S(1)}, u32[]{:S(2)}, u32[]{:S(2)}) async-start(f16[8,2,144,128]{3,2,1,0:T(8,128)(2,1)} %pad_maximum_fusion.1), calls=%async_computation.6 | async-start | bytes 1179648 | tf_op jit(solution)/shard_map/all_to_all | solution.py:346
  161.4 10.0 %all-to-all-done.4 = f16[8,2,144,128]{3,2,1,0:T(8,128)(2,1)S(1)} async-done(((f16[8,2,144,128]{3,2,1,0:T(8,128)(2,1)}), f16[8,2,144,128]{3,2,1,0:T(8,128)(2,1)S(1)}, u32[]{:S(2)}, u32[]{:S(2)}) %all-to-all-start.4) | async-done | bytes 589856 | tf_op jit(solution)/shard_map/all_to_all | solution.py:346
  172.7 11.8 %reduce-scatter.3.cloned.1.call-done = f32[256,128]{1,0:T(8,128)} async-done(((f32[2048,128]{1,0:T(8,128)}), f32[256,128]{1,0:T(8,128)}) %reduce-scatter.3.cloned.1.call-update) | async-done | bytes 131088 | tf_op jit(solution)/shard_map/reduce_scatter | solution.py:448
  184.5 1.5 convert_element_type.60
  186.0 5.7 %potential_parts.2 = f32[8,2,128,128]{3,2,1,0:T(8,128)} custom-call(bf16[2,128,128]{2,1,0:T(8,128)(2,1)} %bitcast.69, f32[4,128,2048]{2,1,0:T(8,128)} %pair_values.1.values, s32[4,1,2048]{2,1,0:T(1,128)} %broadcast_in_dim.118.target, s32[4,1,2048]{2,1,0:T(1,128)} %broadcast_in_dim.119.source), custom_call_target="tpu_custom_call" | custom-call | flops 1073741824 | tf_op jit(solution)/shard_map/potential_parts/pallas_call | solution.py:207
  191.7 1.4 abs_reduce_fusion.1
  193.1 1.4 multiply_convert_fusion.1
  194.8 19.2 %all_to_all.25 = f16[8,2,144,128]{3,2,1,0:T(8,128)(2,1)S(1)} all-to-all(f16[8,2,144,128]{3,2,1,0:T(8,128)(2,1)S(1)} %pad_maximum_fusion), channel_id=1, replica_groups=mesh['y'=8,'z'=8,'col'=8] {'col'}, dimensions={0} | all-to-all | bytes 1179648 | tf_op jit(solution)/shard_map/all_to_all | solution.py:346
  218.4 1.7 copy.78
  220.0 19.5 %basis_at_owner.1.basis = bf16[64,256,512]{2,1,0:T(8,128)(2,1)} custom-call(s32[128]{0:T(128)} %select_n.59.pick, s32[512]{0:T(512)} %reshape.227.listed, s32[64]{0:T(128)} %add.92.points_at, f32[3072,4]{1,0:T(8,128)} %bitcast.60, f32[1600,128]{1,0:T(8,128)} %bitcast.59), custom_call_target="tpu_custom_call" | custom-call | flops 419430400 | tf_op jit(solution)/shard_map/basis_at_owner/pallas_call | solution.py:264
  239.5 33.9 %all-gather.8.cloned.1.call-done = bf16[16384,128]{1,0:T(8,128)(2,1)} async-done(((bf16[256,128]{1,0:T(8,128)(2,1)}), bf16[16384,128]{1,0:T(8,128)(2,1)}) %all-gather.8.cloned.1.call-update) | async-done | bytes 4194320 | tf_op jit(solution)/shard_map/all_gather | solution.py:458
  273.4 13.9 %fock_at_owner.2.refs_0_ = f32[24,128,128]{2,1,0:T(8,128)} custom-call(s32[128]{0:T(128)} %select_n.59.pick, bf16[64,256,512]{2,1,0:T(8,128)(2,1)} %basis_at_owner.1.basis, bf16[64,256,128]{2,1,0:T(8,128)(2,1)} %bitcast.61), custom_call_target="tpu_custom_call" | custom-call | flops 1073741824 | tf_op jit(solution)/shard_map/fock_at_owner/pallas_call | solution.py:304
  287.3 72.1 %all-gather.6.cloned.1.call-done = bf16[16384,128]{1,0:T(8,128)(2,1)} async-done(((bf16[256,128]{1,0:T(8,128)(2,1)}), bf16[16384,128]{1,0:T(8,128)(2,1)}) %all-gather.6.cloned.1.call-update) | async-done | bytes 4194320 | tf_op jit(solution)/shard_map/all_gather | solution.py:458
  359.4 14.7 %fock_at_owner.3 = f32[24,128,128]{2,1,0:T(8,128)} custom-call(s32[128]{0:T(128)} %select_n.59.pick, bf16[64,256,512]{2,1,0:T(8,128)(2,1)} %basis_at_owner.1.basis, bf16[64,256,128]{2,1,0:T(8,128)(2,1)} %bitcast.62, f32[24,128,128]{2,1,0:T(8,128)} %fock_at_owner.2.refs_0_), custom_call_target="tpu_custom_call", output_to_operand_aliasing={{}: (3, {})} | custom-call | flops 1073741824 | tf_op jit(solution)/shard_map/fock_at_owner/pallas_call | solution.py:304
  (105 shorter events, 22.6 us)
Async XLA Ops:
  6.5 46.9 %copy-start.4 = (f32[3,128]{1,0:T(4,128)S(1)}, f32[3,128]{1,0:T(4,128)}, u32[]{:S(2)}) copy-start(f32[3,128]{1,0:T(4,128)} %param.13) | copy-start | bytes 4612
  6.5 46.9 %copy-start.5 = (f32[128]{0:T(128)S(1)}, f32[128]{0:T(128)}, u32[]{:S(2)}) copy-start(f32[128]{0:T(128)} %param.14) | copy-start | bytes 1540
  6.5 93.5 %all-gather.4.cloned.1.call-start = ((), (), s32[]{:S(2)}) async-start(), calls=%async_computation.7 | async-start | bytes 7077888 | tf_op jit(solution)/shard_map/all_gather | solution.py:386
  8.6 14.9 %all-to-all-start = ((f32[8,12,128]{2,1,0:T(8,128)}), f32[8,12,128]{2,1,0:T(8,128)S(1)}, u32[]{:S(2)}, u32[]{:S(2)}) async-start(f32[8,12,128]{2,1,0:T(8,128)} %broadcast_in_dim.63), calls=%async_computation | async-start | bytes 131072 | tf_op jit(solution)/shard_map/all_to_all | solution.py:325
  24.1 18.8 %all-to-all-start.1 = ((f32[8,24,128]{2,1,0:T(8,128)}), f32[8,24,128]{2,1,0:T(8,128)S(1)}, u32[]{:S(2)}, u32[]{:S(2)}) async-start(f32[8,24,128]{2,1,0:T(8,128)} %broadcast_in_dim.64), calls=%async_computation.1 | async-start | bytes 196608 | tf_op jit(solution)/shard_map/all_to_all | solution.py:325
  44.7 20.3 %all-to-all-start.2 = ((f32[8,200,128]{2,1,0:T(8,128)}), f32[8,200,128]{2,1,0:T(8,128)S(1)}, u32[]{:S(2)}, u32[]{:S(2)}) async-start(f32[8,200,128]{2,1,0:T(8,128)} %broadcast_in_dim.66), calls=%async_computation.2 | async-start | bytes 1638400 | tf_op jit(solution)/shard_map/all_to_all | solution.py:325
  52.5 87.9 %reduce-scatter.5.cloned.1.call-start = ((), (), s32[]{:S(2)}) async-start(), calls=%async_computation.10 | async-start | bytes 1179648 | tf_op jit(solution)/shard_map/reduce_scatter | solution.py:448
  65.0 0.9 copy-start
  110.9 73.6 %reduce-scatter.3.cloned.1.call-start = ((), (), s32[]{:S(2)}) async-start(), calls=%async_computation.8 | async-start | bytes 1179648 | tf_op jit(solution)/shard_map/reduce_scatter | solution.py:448
  141.9 19.5 %copy-start.6 = (f32[4,128]{1,0:T(4,128)S(1)}, f32[4,128]{1,0:T(4,128)}, u32[]{:S(2)}) copy-start(f32[4,128]{1,0:T(4,128)} %param.16) | copy-start | bytes 6148
  151.5 20.0 %all-to-all-start.4 = ((f16[8,2,144,128]{3,2,1,0:T(8,128)(2,1)}), f16[8,2,144,128]{3,2,1,0:T(8,128)(2,1)S(1)}, u32[]{:S(2)}, u32[]{:S(2)}) async-start(f16[8,2,144,128]{3,2,1,0:T(8,128)(2,1)} %pad_maximum_fusion.1), calls=%async_computation.6 | async-start | bytes 1179648 | tf_op jit(solution)/shard_map/all_to_all | solution.py:346
  161.4 111.9 %all-gather.8.cloned.1.call-start = ((), (), s32[]{:S(2)}) async-start(), calls=%async_computation.11 | async-start | bytes 4259840 | tf_op jit(solution)/shard_map/all_gather | solution.py:458
  172.6 186.8 %all-gather.6.cloned.1.call-start = ((), (), s32[]{:S(2)}) async-start(), calls=%async_computation.9 | async-start | bytes 4259840 | tf_op jit(solution)/shard_map/all_gather | solution.py:458
  191.7 24.2 %copy-start.2 = (s32[256,32]{0,1:T(8,128)S(1)}, s32[256,32]{0,1:T(8,128)}, u32[]{:S(2)}) copy-start(s32[256,32]{0,1:T(8,128)} %param.17) | copy-start | bytes 98308
  191.7 26.6 %copy-start.1 = (f32[3,3072]{1,0:T(4,128)S(1)}, f32[3,3072]{1,0:T(4,128)}, u32[]{:S(2)}) copy-start(f32[3,3072]{1,0:T(4,128)} %param.11) | copy-start | bytes 110596
  191.7 26.6 %copy-start.3 = (f32[3072]{0:T(1024)S(1)}, f32[3072]{0:T(1024)}, u32[]{:S(2)}) copy-start(f32[3072]{0:T(1024)} %param.12) | copy-start | bytes 36868
Sparse Core Ops, SparseCore 0:
  9.4 85.2 all-gather.3
  111.1 29.2 reduce-scatter.4
  143.2 41.2 reduce-scatter.2
  187.4 85.9 all-gather.7
  276.2 83.1 all-gather.5

commit v4 on v3

--- a/solution.py
+++ b/solution.py
@@ -15,7 +15,8 @@
 CHUNK = 512
 STEP_OWNERS = 4
 SCALE_ROWS = 16
-PARTS = 2
+STEP_GATHERED = 16
+STEP_PLACES = 2
 GRID = ("y", "z")
 quad_nodes = 8
 F32 = jnp.float32
@@ -85,29 +86,30 @@
 
 
 def line_field_kernel(tiles_at, tiles, basis, out, rows, *, slots):
-    place = pl.program_id(0)
-    for slot in range(slots):
-        rows[slot * BLK : (slot + 1) * BLK, :] = tiles[tiles_at[place * slots + slot]]
-    out[0] = jnp.dot(basis[0], rows[...], preferred_element_type=F32)
-
-
-def line_field(tiles_at, tiles, basis, part, parts):
+    for place in range(out.shape[0]):
+        first = (pl.program_id(0) * out.shape[0] + place) * slots
+        for slot in range(slots):
+            rows[place, slot * BLK : (slot + 1) * BLK, :] = tiles[tiles_at[first + slot]]
+        out[place] = jnp.dot(basis[place], rows[place], preferred_element_type=F32)
+
+
+def line_field(tiles_at, tiles, basis):
     places, points, functions = basis.shape
     count, _, width = tiles.shape
-    points //= parts
+    step = min(STEP_PLACES, places)
     return call(
         functools.partial(line_field_kernel, slots=functions // BLK),
         "line_field",
         flops=2 * places * points * functions * width,
         grid_spec=pltpu.PrefetchScalarGridSpec(
             num_scalar_prefetch=1,
-            grid=(places,),
+            grid=(places // step,),
             in_specs=[
                 pl.BlockSpec((count, BLK, width), lambda i, *_: (0, 0, 0)),
-                pl.BlockSpec((1, points, functions), lambda i, *_: (i, part, 0)),
-            ],
-            out_specs=pl.BlockSpec((1, points, width), lambda i, *_: (i, 0, 0)),
-            scratch_shapes=[pltpu.VMEM((functions, width), BF16)],
+                pl.BlockSpec((step, points, functions), lambda i, *_: (i, 0, 0)),
+            ],
+            out_specs=pl.BlockSpec((step, points, width), lambda i, *_: (i, 0, 0)),
+            scratch_shapes=[pltpu.VMEM((step, functions, width), BF16)],
         ),
         out_shape=jax.ShapeDtypeStruct((places, points, width), F32),
     )(tiles_at, tiles, basis)
@@ -183,13 +185,14 @@
     )(target, source, window, local, points_t)
 
 
-def potential_kernel(field, values, target, source, out):
+def potential_kernel(field, values, target, source, out, largest):
     columns, width = out.shape[0], out.shape[3]
     window_count = columns * width
+    rounded = field[0].astype(BF16)
     potential = jnp.zeros((field.shape[1], window_count), F32)
     for first in range(0, values.shape[2], CHUNK):
         part = slice(first, first + CHUNK)
-        picked = jnp.dot(field[0], one_hot(source[0, :, part], width), preferred_element_type=F32)
+        picked = jnp.dot(rounded, one_hot(source[0, :, part], width), preferred_element_type=F32)
         product = (values[0, :, part] * picked).astype(BF16)
         potential += lax.dot_general(
             product,
@@ -199,9 +202,10 @@
         )
     for column in range(columns):
         out[column, 0] = potential[:, column * width : (column + 1) * width]
-
-
-def potential_parts(field, values, target, source, first, columns):
+    largest[0] = jnp.broadcast_to(jnp.max(jnp.abs(potential), keepdims=True), largest.shape[1:])
+
+
+def potential_parts(field, values, target, source, columns):
     batches, pts, width = field.shape
     pairs = values.shape[2]
     return call(
@@ -213,13 +217,19 @@
             grid=(batches,),
             in_specs=[
                 pl.BlockSpec((1, pts, width), lambda b: (b, 0, 0)),
-                pl.BlockSpec((1, pts, pairs), lambda b: (first + b, 0, 0)),
-                pl.BlockSpec((1, 1, pairs), lambda b: (first + b, 0, 0)),
-                pl.BlockSpec((1, 1, pairs), lambda b: (first + b, 0, 0)),
-            ],
-            out_specs=pl.BlockSpec((columns, 1, pts, width), lambda b: (0, b, 0, 0)),
-        ),
-        out_shape=jax.ShapeDtypeStruct((columns, batches, pts, width), F32),
+                pl.BlockSpec((1, pts, pairs), lambda b: (b, 0, 0)),
+                pl.BlockSpec((1, 1, pairs), lambda b: (b, 0, 0)),
+                pl.BlockSpec((1, 1, pairs), lambda b: (b, 0, 0)),
+            ],
+            out_specs=[
+                pl.BlockSpec((columns, 1, pts, width), lambda b: (0, b, 0, 0)),
+                pl.BlockSpec((1, 8, BLK), lambda b: (b, 0, 0)),
+            ],
+        ),
+        out_shape=[
+            jax.ShapeDtypeStruct((columns, batches, pts, width), F32),
+            jax.ShapeDtypeStruct((batches, 8, BLK), F32),
+        ],
     )(field, values, target, source)
 
 
@@ -285,39 +295,35 @@
         out[block] = out[block] + rows[slot * BLK : (slot + 1) * BLK]
 
 
-def fock_kernel(pick, basis, weighted, *refs):
-    out = refs[-1]
-
+def fock_kernel(pick, basis, weighted, out):
     @pl.when(pl.program_id(0) == 0)
     def _():
-        out[...] = refs[0][...] if len(refs) > 1 else jnp.zeros_like(out)
-
-    for owner in range(STEP_OWNERS):
-        place = pl.program_id(0) * STEP_OWNERS + owner
+        out[...] = jnp.zeros_like(out)
+
+    for owner in range(basis.shape[0]):
+        place = pl.program_id(0) * basis.shape[0] + owner
         add_rows(out, pick, place, jnp.dot(basis[owner], weighted[owner], preferred_element_type=F32))
 
 
-def fock_at_owner(pick, basis, weighted, part, before, held):
-    owners, rows, _ = basis.shape
-    _, points, width = weighted.shape
-    whole = pl.BlockSpec((held, BLK, width), lambda i, *_: (0, 0, 0))
+def fock_at_owner(pick, basis, weighted, held):
+    owners, rows, points = basis.shape
+    width = weighted.shape[2]
+    step = min(STEP_GATHERED, owners)
     return call(
         fock_kernel,
         "fock_at_owner",
         flops=2 * owners * rows * points * width,
         grid_spec=pltpu.PrefetchScalarGridSpec(
             num_scalar_prefetch=1,
-            grid=(owners // STEP_OWNERS,),
-            in_specs=[
-                pl.BlockSpec((STEP_OWNERS, rows, points), lambda i, *_: (i, 0, part)),
-                pl.BlockSpec((STEP_OWNERS, points, width), lambda i, *_: (i, 0, 0)),
-            ]
-            + ([] if before is None else [whole]),
-            out_specs=whole,
+            grid=(owners // step,),
+            in_specs=[
+                pl.BlockSpec((step, rows, points), lambda i, *_: (i, 0, 0)),
+                pl.BlockSpec((step, points, width), lambda i, *_: (i, 0, 0)),
+            ],
+            out_specs=pl.BlockSpec((held, BLK, width), lambda i, *_: (0, 0, 0)),
         ),
         out_shape=jax.ShapeDtypeStruct((held, BLK, width), F32),
-        input_output_aliases={} if before is None else {3: 0},
-    )(pick, basis, weighted, *([] if before is None else [before]))
+    )(pick, basis, weighted)
 
 
 def to_everyone(value, axis):
@@ -335,9 +341,8 @@
     return parts.astype(BF16)
 
 
-def sum_at_column(parts):
+def sum_at_column(parts, largest):
     columns, batches, pts, width = parts.shape
-    largest = jnp.max(jnp.abs(parts), axis=(0, 2, 3))
     power = jnp.clip(13.0 - jnp.ceil(jnp.log2(largest)), -100.0, 100.0)
     scaled = (parts * jnp.exp2(power)[None, :, None, None]).astype(jnp.float16)
     tail = jnp.broadcast_to(
@@ -438,30 +443,24 @@
         line_points.transpose(0, 2, 1),
         batches,
     )
+    share = line_field(tiles_at.reshape(-1), tiles, basis)
+    share, local_window, whole_window = lax.optimization_barrier(
+        (share, local_window, whole_window)
+    )
+    field = lax.psum_scatter(share.reshape(-1, width), "y", scatter_dimension=0, tiled=True)
     values = pair_values(target, source, in_parts(whole_window), in_parts(local_window), points_t)
-    basis, values = lax.optimization_barrier((basis, values))
-
-    together = batches // PARTS
-    weighted = []
-    for part in range(PARTS):
-        share = line_field(tiles_at.reshape(-1), tiles, basis, part, PARTS)
-        field = lax.psum_scatter(
-            share.reshape(-1, width), "y", scatter_dimension=0, tiled=True
-        ).astype(BF16)
-        parts = potential_parts(
-            field.reshape(together, pts, width), values, target, source, part * together, columns
-        )
-        potential = sum_at_column(parts)
-        scale = weights[part * together : (part + 1) * together, :, None]
-        weighted.append((scale * potential).astype(BF16).reshape(together * pts, width))
-
-    everyone = [lax.all_gather(value, GRID, axis=0, tiled=True) for value in weighted]
-    gathered, weighted = lax.optimization_barrier((gathered, weighted[-1]))
+    parts, largest = potential_parts(
+        field.reshape(batches, pts, width), values, target, source, columns
+    )
+    potential = sum_at_column(parts, largest[:, 0, 0])
+    weighted = (weights[:, :, None] * potential).astype(BF16).reshape(batches * pts, width)
+
+    all_weighted = lax.all_gather(weighted, GRID, axis=0, tiled=True)
+    gathered, weighted = lax.optimization_barrier((gathered, weighted))
     own_basis = basis_at_owner(pick, listed, points_at, own_params.T, gathered, batches, pts)
-    fock = None
-    for part, value in enumerate(everyone):
-        value = value.reshape(owners, together * pts, width)
-        fock = fock_at_owner(pick, own_basis, value, part, fock, held)
+    fock = fock_at_owner(
+        pick, own_basis, all_weighted.reshape(owners, batches * pts, width), held
+    )
     return fock.reshape(held * BLK, width)
 
 

time: 386 us -> 303 us (0.78); the launches traced: 381 us -> 302 us
  waiting for transfers between devices: 162 us -> 123 us
  Pallas kernels: 114 us -> 86.6 us
  starting transfers between devices: 35.6 us -> 25.6 us
  other arithmetic: 18.5 us -> 9.85 us
  blocking collectives: 19.2 us -> 25.9 us
    all_gather x2 -> x1, waiting for transfers between devices: 106 us -> 72 us  [on_device(): all_weighted = lax.all_gather(weighted, GRID, axis=0, tiled=True)]
    pallas_call x2 -> x1, Pallas kernels: 28.6 us -> 12.1 us  [fock_at_owner(): call(fock_kernel, 'fock_at_owner', flops=2 * owners * rows * points * wid...]
    all_gather x1, waiting for transfers between devices: 0.01 us -> 10.2 us  [on_device(): lax.all_gather(density, 'z', axis=0, tiled=True)]
    all_to_all x1 -> x0, waiting for transfers between devices: 10 us -> none  [sum_at_column(): lax.all_to_all(jnp.concatenate([scaled, tail], axis=2), 'col', split_axis...]
    all_to_all x1 -> x0, starting transfers between devices: 9.96 us -> none  [sum_at_column(): lax.all_to_all(jnp.concatenate([scaled, tail], axis=2), 'col', split_axis...]
    reduce_scatter x2 -> x1, waiting for transfers between devices: 30.2 us -> 20.3 us  [on_device(): lax.psum_scatter(share.reshape(-1, width), 'y', scatter_dimension=0, tile...]
    pallas_call x2 -> x1, Pallas kernels: 21.8 us -> 12.3 us  [line_field(): call(functools.partial(line_field_kernel, slots=functions // BLK), 'line_...]
    all_to_all x1, blocking collectives: 19.2 us -> 25.9 us  [sum_at_column(): lax.all_to_all(jnp.concatenate([scaled, tail], axis=2), 'col', split_axis...]
  transfers between devices with their start and end apart: 9 -> 6, of which waited for: 8 -> 6; matrix products, arithmetic and copies ran while one was open for 9% -> 7% of each run, Pallas kernels for 23% -> 17%
where the time goes in v4:
time: 303 us; the launch traced here: 302 us
  waiting for transfers between devices  123 us (41%)
  Pallas kernels  86.6 us (29%)
  blocking collectives  25.9 us (9%)
  starting transfers between devices  25.6 us (8%)
  local copies, waits for them, and re-layouts  16.9 us (6%)
  between operations  13.4 us (4%)
  other arithmetic  9.85 us (3%)
    all_gather x1, waiting for transfers between devices, on_device(): all_weighted = lax.all_gather(weighted, GRID, axis=0, tiled=True)  72 us
    all_to_all x1, blocking collectives, sum_at_column(): lax.all_to_all(jnp.concatenate([scaled, tail], axis=2), 'col', split_axis...  25.9 us
    all_to_all x3, starting transfers between devices, to_everyone(): lax.all_to_all(jnp.broadcast_to(value[None], (devices, *value.shape)), ax...  25.5 us
    reduce_scatter x1, waiting for transfers between devices, on_device(): lax.psum_scatter(share.reshape(-1, width), 'y', scatter_dimension=0, tile...  20.3 us
    all_to_all x3, waiting for transfers between devices, to_everyone(): lax.all_to_all(jnp.broadcast_to(value[None], (devices, *value.shape)), ax...  20.1 us
    pallas_call x1, Pallas kernels, basis_at_owner(): call(functools.partial(owner_basis_kernel, batches=batches), 'basis_at_ow...  19.5 us
    pallas_call x1, Pallas kernels, line_basis(): call(functools.partial(line_basis_kernel, batches=batches, slots=slots),...  18.5 us
    pallas_call x1, Pallas kernels, pair_values(): call(pair_kernel, 'pair_values', flops=batches * pairs * pts * 400, grid_...  14.4 us
  transfers between devices with their start and end apart: 6, of which 6 were waited for; matrix products, arithmetic and copies ran while one was open for 7% of the time, Pallas kernels for 17%

profile of v4, /device:TPU:1, one launch (start us, length us, event | category | flops | bytes accessed | tf_op | source)
XLA Modules:
  0.0 301.6 jit_solution(14195557206857687372)
XLA Ops:
  6.5 0.7 all-gather.3.cloned.1.call-update
  8.6 7.6 %all-to-all-start = ((f32[8,12,128]{2,1,0:T(8,128)}), f32[8,12,128]{2,1,0:T(8,128)S(1)}, u32[]{:S(2)}, u32[]{:S(2)}) async-start(f32[8,12,128]{2,1,0:T(8,128)} %broadcast_in_dim.102), calls=%async_computation | async-start | bytes 131072 | tf_op jit(solution)/shard_map/all_to_all | solution.py:331
  16.2 0.9 copy.71
  17.8 0.7 fusion.11
  19.1 0.8 maximum_bitcast_fusion
  20.2 3.3 %all-to-all-done = f32[8,12,128]{2,1,0:T(8,128)S(1)} async-done(((f32[8,12,128]{2,1,0:T(8,128)}), f32[8,12,128]{2,1,0:T(8,128)S(1)}, u32[]{:S(2)}, u32[]{:S(2)}) %all-to-all-start) | async-done | bytes 49184 | tf_op jit(solution)/shard_map/all_to_all | solution.py:331
  24.1 10.0 %all-to-all-start.1 = ((f32[8,24,128]{2,1,0:T(8,128)}), f32[8,24,128]{2,1,0:T(8,128)S(1)}, u32[]{:S(2)}, u32[]{:S(2)}) async-start(f32[8,24,128]{2,1,0:T(8,128)} %broadcast_in_dim.103), calls=%async_computation.1 | async-start | bytes 196608 | tf_op jit(solution)/shard_map/all_to_all | solution.py:331
  34.2 8.7 %all-to-all-done.1 = f32[8,24,128]{2,1,0:T(8,128)S(1)} async-done(((f32[8,24,128]{2,1,0:T(8,128)}), f32[8,24,128]{2,1,0:T(8,128)S(1)}, u32[]{:S(2)}, u32[]{:S(2)}) %all-to-all-start.1) | async-done | bytes 98336 | tf_op jit(solution)/shard_map/all_to_all | solution.py:331
  43.0 0.9 broadcast_in_dim.105
  44.0 7.8 %all-to-all-start.2 = ((f32[8,200,128]{2,1,0:T(8,128)}), f32[8,200,128]{2,1,0:T(8,128)S(1)}, u32[]{:S(2)}, u32[]{:S(2)}) async-start(f32[8,200,128]{2,1,0:T(8,128)} %broadcast_in_dim.105), calls=%async_computation.2 | async-start | bytes 1638400 | tf_op jit(solution)/shard_map/all_to_all | solution.py:331
  51.8 1.3 and_reduce_fusion
  53.3 0.7 reshape.208.listed
  55.1 1.0 copy.76
  56.1 8.2 %all-to-all-done.2 = f32[8,200,128]{2,1,0:T(8,128)S(1)} async-done(((f32[8,200,128]{2,1,0:T(8,128)}), f32[8,200,128]{2,1,0:T(8,128)S(1)}, u32[]{:S(2)}, u32[]{:S(2)}) %all-to-all-start.2) | async-done | bytes 819232 | tf_op jit(solution)/shard_map/all_to_all | solution.py:331
  64.3 0.9 copy-done
  65.3 18.5 %line_basis.1.basis = bf16[8,512,2048]{2,1,0:T(8,128)(2,1)} custom-call(s32[128]{0:T(128)} %get-tuple-element.36.rows_at, s32[512]{0:T(512)} %reshape.208.listed, f32[1600,128]{1,0:T(8,128)} %bitcast.39, f32[8,128,12]{2,1,0:T(8,128)} %bitcast.43), custom_call_target="tpu_custom_call" | custom-call | flops 419430400 | tf_op jit(solution)/shard_map/line_basis/pallas_call | solution.py:70
  83.7 0.8 slice_bitcast_fusion
  84.5 10.2 %all-gather.3.cloned.1.call-done = bf16[24576,128]{1,0:T(8,128)(2,1)} async-done(((bf16[3072,128]{1,0:T(8,128)(2,1)}), bf16[24576,128]{1,0:T(8,128)(2,1)}) %all-gather.3.cloned.1.call-update) | async-done | bytes 6291472 | tf_op jit(solution)/shard_map/all_gather | solution.py:391
  94.7 12.3 %line_field.1 = f32[8,512,128]{2,1,0:T(8,128)} custom-call(s32[128]{0:T(128)} %get-tuple-element.37.tiles_at, bf16[192,128,128]{2,1,0:T(8,128)(2,1)} %bitcast.42, bf16[8,512,2048]{2,1,0:T(8,128)(2,1)} %line_basis.1.basis), custom_call_target="tpu_custom_call" | custom-call | flops 2147483648 | tf_op jit(solution)/shard_map/line_field/pallas_call | solution.py:100
  107.7 0.9 copy.77
  111.2 14.4 %pair_values.1.values = f32[4,128,2048]{2,1,0:T(8,128)} custom-call(s32[4,1,2048]{2,1,0:T(1,128)} %broadcast_in_dim.110.target, s32[4,1,2048]{2,1,0:T(1,128)} %broadcast_in_dim.111.source, bf16[16,1024]{1,0:T(8,128)(2,1)} %maximum_maximum_fusion.1.window, bf16[16,128]{1,0:T(8,128)(2,1)} %maximum_maximum_fusion.2.local, f32[4,128,3]{2,1,0:T(8,128)} %bitcast.44), custom_call_target="tpu_custom_call" | custom-call | flops 419430400 | tf_op jit(solution)/shard_map/pair_values/pallas_call | solution.py:167
  125.6 20.3 %reduce-scatter.2.cloned.1.call-done = f32[512,128]{1,0:T(8,128)} async-done(((f32[4096,128]{1,0:T(8,128)}), f32[512,128]{1,0:T(8,128)}) %reduce-scatter.2.cloned.1.call-update) | async-done | bytes 262160 | tf_op jit(solution)/shard_map/reduce_scatter | solution.py:450
  145.9 9.8 %potential_parts.1 = (f32[8,4,128,128]{3,2,1,0:T(8,128)}, f32[4,8,128]{2,1,0:T(8,128)}) custom-call(f32[4,128,128]{2,1,0:T(8,128)} %bitcast.60, f32[4,128,2048]{2,1,0:T(8,128)} %pair_values.1.values, s32[4,1,2048]{2,1,0:T(1,128)} %broadcast_in_dim.110.target, s32[4,1,2048]{2,1,0:T(1,128)} %broadcast_in_dim.111.source), custom_call_target="tpu_custom_call" | custom-call | flops 2147483648 | tf_op jit(solution)/shard_map/potential_parts/pallas_call | solution.py:211
  155.7 0.8 exponential_reduce_fusion
  156.7 2.0 multiply_convert_fusion
  159.2 25.9 %all_to_all.20 = f16[8,4,144,128]{3,2,1,0:T(8,128)(2,1)S(1)} all-to-all(f16[8,4,144,128]{3,2,1,0:T(8,128)(2,1)S(1)} %pad_maximum_fusion), channel_id=1, replica_groups=mesh['y'=8,'z'=8,'col'=8] {'col'}, dimensions={0} | all-to-all | bytes 2359296 | tf_op jit(solution)/shard_map/all_to_all | solution.py:351
  185.7 0.8 fusion
  187.5 0.7 reshape.207.listed
  189.8 1.7 copy.69
  191.4 19.5 %basis_at_owner.1.basis = bf16[64,256,512]{2,1,0:T(8,128)(2,1)} custom-call(s32[128]{0:T(128)} %select_n.59.pick, s32[512]{0:T(512)} %reshape.207.listed, s32[64]{0:T(128)} %add.90.points_at, f32[3072,4]{1,0:T(8,128)} %bitcast.41, f32[1600,128]{1,0:T(8,128)} %bitcast.40), custom_call_target="tpu_custom_call" | custom-call | flops 419430400 | tf_op jit(solution)/shard_map/basis_at_owner/pallas_call | solution.py:274
  210.9 72.0 %all-gather.5.cloned.1.call-done = bf16[32768,128]{1,0:T(8,128)(2,1)} async-done(((bf16[512,128]{1,0:T(8,128)(2,1)}), bf16[32768,128]{1,0:T(8,128)(2,1)}) %all-gather.5.cloned.1.call-update) | async-done | bytes 8388624 | tf_op jit(solution)/shard_map/all_gather | solution.py:458
  282.9 12.1 %fock_at_owner.1 = f32[24,128,128]{2,1,0:T(8,128)} custom-call(s32[128]{0:T(128)} %select_n.59.pick, bf16[64,256,512]{2,1,0:T(8,128)(2,1)} %basis_at_owner.1.basis, bf16[64,512,128]{2,1,0:T(8,128)(2,1)} %bitcast.37), custom_call_target="tpu_custom_call" | custom-call | flops 2147483648 | tf_op jit(solution)/shard_map/fock_at_owner/pallas_call | solution.py:312
  (89 shorter events, 11.9 us)
Async XLA Ops:
  6.5 36.4 %copy-start.9 = (f32[128]{0:T(128)S(1)}, f32[128]{0:T(128)}, u32[]{:S(2)}) copy-start(f32[128]{0:T(128)} %param.14) | copy-start | bytes 1540
  6.5 36.4 %copy-start.7 = (f32[3,128]{1,0:T(4,128)S(1)}, f32[3,128]{1,0:T(4,128)}, u32[]{:S(2)}) copy-start(f32[3,128]{1,0:T(4,128)} %param.13) | copy-start | bytes 4612
  6.5 88.2 %all-gather.3.cloned.1.call-start = ((), (), s32[]{:S(2)}) async-start(), calls=%async_computation.5 | async-start | bytes 7077888 | tf_op jit(solution)/shard_map/all_gather | solution.py:391
  8.6 14.9 %all-to-all-start = ((f32[8,12,128]{2,1,0:T(8,128)}), f32[8,12,128]{2,1,0:T(8,128)S(1)}, u32[]{:S(2)}, u32[]{:S(2)}) async-start(f32[8,12,128]{2,1,0:T(8,128)} %broadcast_in_dim.102), calls=%async_computation | async-start | bytes 131072 | tf_op jit(solution)/shard_map/all_to_all | solution.py:331
  24.1 18.8 %all-to-all-start.1 = ((f32[8,24,128]{2,1,0:T(8,128)}), f32[8,24,128]{2,1,0:T(8,128)S(1)}, u32[]{:S(2)}, u32[]{:S(2)}) async-start(f32[8,24,128]{2,1,0:T(8,128)} %broadcast_in_dim.103), calls=%async_computation.1 | async-start | bytes 196608 | tf_op jit(solution)/shard_map/all_to_all | solution.py:331
  44.0 20.3 %all-to-all-start.2 = ((f32[8,200,128]{2,1,0:T(8,128)}), f32[8,200,128]{2,1,0:T(8,128)S(1)}, u32[]{:S(2)}, u32[]{:S(2)}) async-start(f32[8,200,128]{2,1,0:T(8,128)} %broadcast_in_dim.105), calls=%async_computation.2 | async-start | bytes 1638400 | tf_op jit(solution)/shard_map/all_to_all | solution.py:331
  51.8 94.1 %reduce-scatter.2.cloned.1.call-start = ((), (), s32[]{:S(2)}) async-start(), calls=%async_computation.6 | async-start | bytes 2359296 | tf_op jit(solution)/shard_map/reduce_scatter | solution.py:450
  64.3 0.9 copy-start
  107.0 0.7 copy-start.6
  107.0 1.6 copy-start.4
  107.0 2.2 copy-start.5
  107.0 175.9 %all-gather.5.cloned.1.call-start = ((), (), s32[]{:S(2)}) async-start(), calls=%async_computation.7 | async-start | bytes 8519680 | tf_op jit(solution)/shard_map/all_gather | solution.py:458
  159.1 26.6 %copy-start.8 = (f32[4,128]{1,0:T(4,128)S(1)}, f32[4,128]{1,0:T(4,128)}, u32[]{:S(2)}) copy-start(f32[4,128]{1,0:T(4,128)} %param.16) | copy-start | bytes 6148
  159.1 27.4 %copy-start.2 = (s32[256,32]{0,1:T(8,128)S(1)}, s32[256,32]{0,1:T(8,128)}, u32[]{:S(2)}) copy-start(s32[256,32]{0,1:T(8,128)} %param.17) | copy-start | bytes 98308
  159.1 30.6 %copy-start.1 = (f32[3,3072]{1,0:T(4,128)S(1)}, f32[3,3072]{1,0:T(4,128)}, u32[]{:S(2)}) copy-start(f32[3,3072]{1,0:T(4,128)} %param.11) | copy-start | bytes 110596
  159.1 30.6 %copy-start.3 = (f32[3072]{0:T(1024)S(1)}, f32[3072]{0:T(1024)}, u32[]{:S(2)}) copy-start(f32[3072]{0:T(1024)} %param.12) | copy-start | bytes 36868
Sparse Core Ops, SparseCore 0:
  9.4 85.2 all-gather.2
  107.1 38.7 reduce-scatter.1
  186.6 96.2 all-gather.4

commit v5 on v4

--- a/solution.py
+++ b/solution.py
@@ -17,6 +17,7 @@
 SCALE_ROWS = 16
 STEP_GATHERED = 16
 STEP_PLACES = 2
+PARTS = 2
 GRID = ("y", "z")
 quad_nodes = 8
 F32 = jnp.float32
@@ -233,7 +234,10 @@
     )(field, values, target, source)
 
 
-def owner_basis_kernel(pick, listed, points_at, params, gathered, out, spread_params, *, batches):
+def owner_basis_kernel(pick, listed, points_at, params, gathered, *refs, batches):
+    outs, spread_params = refs[:-1], refs[-1]
+    together = batches // len(outs)
+
     @pl.when(pl.program_id(0) == 0)
     def _():
         for block in range(spread_params.shape[0]):
@@ -247,11 +251,12 @@
         for slot in range(CAPB):
             block = pick[place * CAPB + slot]
             for batch in range(batches):
-                here = (owner, slice(slot * BLK, (slot + 1) * BLK), slice(batch * BLK, (batch + 1) * BLK))
+                out, lane = outs[batch // together], batch % together * BLK
+                here = (owner, slice(slot * BLK, (slot + 1) * BLK), slice(lane, lane + BLK))
                 keep = listed[(place * CAPB + slot) * batches + batch]
 
                 @pl.when(keep > 0)
-                def _():
+                def _(out=out, here=here):
                     squared = None
                     for axis in range(3):
                         row = points_at[place] + axis * batches + batch
@@ -260,7 +265,7 @@
                     out[here] = jnp.exp(-spread_params[block, 3] * squared).astype(BF16)
 
                 @pl.when(keep == 0)
-                def _():
+                def _(out=out, here=here):
                     out[here] = jnp.zeros((BLK, BLK), BF16)
 
         return carry
@@ -271,6 +276,7 @@
 def basis_at_owner(pick, listed, points_at, params_t, gathered, batches, pts):
     owners = points_at.shape[0]
     held = params_t.shape[0] // BLK
+    points = batches * pts // PARTS
     return call(
         functools.partial(owner_basis_kernel, batches=batches),
         "basis_at_owner",
@@ -282,10 +288,13 @@
                 pl.BlockSpec(params_t.shape, lambda i, *_: (0, 0)),
                 pl.BlockSpec(gathered.shape, lambda i, *_: (0, 0)),
             ],
-            out_specs=pl.BlockSpec((STEP_OWNERS, CAPB * BLK, batches * pts), lambda i, *_: (i, 0, 0)),
+            out_specs=[
+                pl.BlockSpec((STEP_OWNERS, CAPB * BLK, points), lambda i, *_: (i, 0, 0))
+            ]
+            * PARTS,
             scratch_shapes=[pltpu.VMEM((held, PARAMS, BLK, BLK), F32)],
         ),
-        out_shape=jax.ShapeDtypeStruct((owners, CAPB * BLK, batches * pts), BF16),
+        out_shape=[jax.ShapeDtypeStruct((owners, CAPB * BLK, points), BF16)] * PARTS,
     )(pick, listed, points_at, params_t, gathered)
 
 
@@ -295,23 +304,24 @@
         out[block] = out[block] + rows[slot * BLK : (slot + 1) * BLK]
 
 
-def fock_kernel(pick, basis, weighted, out):
+def fock_kernel(pick, basis, weighted, before, out):
     @pl.when(pl.program_id(0) == 0)
     def _():
-        out[...] = jnp.zeros_like(out)
+        out[...] = before[...]
 
     for owner in range(basis.shape[0]):
         place = pl.program_id(0) * basis.shape[0] + owner
         add_rows(out, pick, place, jnp.dot(basis[owner], weighted[owner], preferred_element_type=F32))
 
 
-def fock_at_owner(pick, basis, weighted, held):
+def fock_from_gather(pick, basis, weighted, before):
     owners, rows, points = basis.shape
     width = weighted.shape[2]
     step = min(STEP_GATHERED, owners)
+    whole = pl.BlockSpec(before.shape, lambda i, *_: (0, 0, 0))
     return call(
         fock_kernel,
-        "fock_at_owner",
+        "fock_from_gather",
         flops=2 * owners * rows * points * width,
         grid_spec=pltpu.PrefetchScalarGridSpec(
             num_scalar_prefetch=1,
@@ -319,11 +329,59 @@
             in_specs=[
                 pl.BlockSpec((step, rows, points), lambda i, *_: (i, 0, 0)),
                 pl.BlockSpec((step, points, width), lambda i, *_: (i, 0, 0)),
-            ],
-            out_specs=pl.BlockSpec((held, BLK, width), lambda i, *_: (0, 0, 0)),
+                whole,
+            ],
+            out_specs=whole,
+        ),
+        out_shape=jax.ShapeDtypeStruct(before.shape, F32),
+        input_output_aliases={3: 0},
+    )(pick, basis, weighted, before)
+
+
+def fock_line_kernel(pick, lines, *refs, first, count, side, fresh):
+    basis, weighted, out = refs[:count], refs[count : 2 * count], refs[-1]
+
+    @pl.when(pl.program_id(0) == 0)
+    def _():
+        out[...] = jnp.zeros_like(out) if fresh else refs[2 * count][...]
+
+    here = weighted[0].shape[0]
+    for line in range(count):
+        for owner in range(here):
+            place = lines[first + line] * side + pl.program_id(0) * here + owner
+            rows = jnp.dot(basis[line][owner], weighted[line][owner], preferred_element_type=F32)
+            add_rows(out, pick, place, rows)
+
+
+def fock_from_lines(pick, lines, first, basis, weighted, before, held):
+    _, rows, points = basis.shape
+    count = len(weighted)
+    side, _, width = weighted[0].shape
+    step = side // 2
+    whole = pl.BlockSpec((held, BLK, width), lambda i, *_: (0, 0, 0))
+
+    def line_spec(line):
+        return pl.BlockSpec(
+            (step, rows, points), lambda i, _, lines: (lines[first + line] * 2 + i, 0, 0)
+        )
+
+    return call(
+        functools.partial(
+            fock_line_kernel, first=first, count=count, side=side, fresh=before is None
+        ),
+        "fock_from_lines",
+        flops=2 * count * side * rows * points * width,
+        grid_spec=pltpu.PrefetchScalarGridSpec(
+            num_scalar_prefetch=2,
+            grid=(2,),
+            in_specs=[line_spec(line) for line in range(count)]
+            + [pl.BlockSpec((step, points, width), lambda i, *_: (i, 0, 0))] * count
+            + ([] if before is None else [whole]),
+            out_specs=whole,
         ),
         out_shape=jax.ShapeDtypeStruct((held, BLK, width), F32),
-    )(pick, basis, weighted)
+        input_output_aliases={} if before is None else {2 + 2 * count: 0},
+    )(pick, lines, *[basis] * count, *weighted, *([] if before is None else [before]))
 
 
 def to_everyone(value, axis):
@@ -444,23 +502,41 @@
         batches,
     )
     share = line_field(tiles_at.reshape(-1), tiles, basis)
-    share, local_window, whole_window = lax.optimization_barrier(
-        (share, local_window, whole_window)
+    share, local_window, whole_window, gathered = lax.optimization_barrier(
+        (share, local_window, whole_window, gathered)
     )
     field = lax.psum_scatter(share.reshape(-1, width), "y", scatter_dimension=0, tiled=True)
     values = pair_values(target, source, in_parts(whole_window), in_parts(local_window), points_t)
+    own_basis = basis_at_owner(pick, listed, points_at, own_params.T, gathered, batches, pts)
+    values, own_basis = lax.optimization_barrier((values, own_basis))
     parts, largest = potential_parts(
         field.reshape(batches, pts, width), values, target, source, columns
     )
     potential = sum_at_column(parts, largest[:, 0, 0])
     weighted = (weights[:, :, None] * potential).astype(BF16).reshape(batches * pts, width)
 
-    all_weighted = lax.all_gather(weighted, GRID, axis=0, tiled=True)
-    gathered, weighted = lax.optimization_barrier((gathered, weighted))
-    own_basis = basis_at_owner(pick, listed, points_at, own_params.T, gathered, batches, pts)
-    fock = fock_at_owner(
-        pick, own_basis, all_weighted.reshape(owners, batches * pts, width), held
-    )
+    half = batches * pts // PARTS
+    all_weighted = lax.all_gather(weighted[:half], GRID, axis=0, tiled=True)
+    came = [to_everyone(weighted[half:], "z")]
+    offsets = [0]
+    for step in range(1, lines // 2 + 1):
+        offsets += [lines - step, step]
+    order = (line + jnp.array(offsets[:lines], jnp.int32)) & (lines - 1)
+    ahead = [(i, (i + 1) % lines) for i in range(lines)]
+    behind = [(i, (i - 1) % lines) for i in range(lines)]
+    up = down = came[0]
+    fock = None
+    for step in range(1, lines // 2 + 1):
+        up = lax.ppermute(up, "y", ahead)
+        if step < lines - step:
+            down = lax.ppermute(down, "y", behind)
+        fock = fock_from_lines(pick, order, max(0, 2 * step - 3), own_basis[1], came, fock, held)
+        if step < lines - step:
+            up, down, fock = lax.optimization_barrier((up, down, fock))
+            came = [up, down]
+        else:
+            fock = fock_from_lines(pick, order, 2 * step - 1, own_basis[1], [up], fock, held)
+    fock = fock_from_gather(pick, own_basis[0], all_weighted.reshape(owners, half, width), fock)
     return fock.reshape(held * BLK, width)
 
 

time: 303 us -> 310 us (1.023)
  the two profiles are of different devices: /device:TPU:1 before, /device:TPU:2 now
where the time goes in v5:
time: 310 us; the launch traced here: 308 us
  Pallas kernels  106 us (34%)
  waiting for transfers between devices  68.6 us (22%)
  starting transfers between devices  46.4 us (15%)
  blocking collectives  45.9 us (15%)
  local copies, waits for them, and re-layouts  18.1 us (6%)
  between operations  13.5 us (4%)
  other arithmetic  9.68 us (3%)
    ppermute x4, waiting for transfers between devices, on_device(): up = lax.ppermute(up, 'y', ahead)  25.4 us
    all_to_all x1, blocking collectives, to_everyone(): lax.all_to_all(jnp.broadcast_to(value[None], (devices, *value.shape)), ax...  24.9 us
    pallas_call x5, Pallas kernels, fock_from_lines(): call(functools.partial(fock_line_kernel, first=first, count=count, side=s...  22.7 us
    all_to_all x3, waiting for transfers between devices, to_everyone(): lax.all_to_all(jnp.broadcast_to(value[None], (devices, *value.shape)), ax...  22.3 us
    all_to_all x3, starting transfers between devices, to_everyone(): lax.all_to_all(jnp.broadcast_to(value[None], (devices, *value.shape)), ax...  22.2 us
    all_to_all x1, blocking collectives, sum_at_column(): lax.all_to_all(jnp.concatenate([scaled, tail], axis=2), 'col', split_axis...  21 us
    pallas_call x1, Pallas kernels, basis_at_owner(): call(functools.partial(owner_basis_kernel, batches=batches), 'basis_at_ow...  19.3 us
    pallas_call x1, Pallas kernels, line_basis(): call(functools.partial(line_basis_kernel, batches=batches, slots=slots),...  18 us
  transfers between devices with their start and end apart: 13, of which 11 were waited for; matrix products, arithmetic and copies ran while one was open for 7% of the time, Pallas kernels for 24%

profile of v5, /device:TPU:2, one launch (start us, length us, event | category | flops | bytes accessed | tf_op | source)
XLA Modules:
  0.0 308.1 jit_solution(5049566981599241411)
XLA Ops:
  8.6 7.1 %all-to-all-start = ((f32[8,12,128]{2,1,0:T(8,128)}), f32[8,12,128]{2,1,0:T(8,128)S(1)}, u32[]{:S(2)}, u32[]{:S(2)}) async-start(f32[8,12,128]{2,1,0:T(8,128)} %broadcast_in_dim.115), calls=%async_computation | async-start | bytes 131072 | tf_op jit(solution)/shard_map/all_to_all | solution.py:389
  19.4 4.7 %all-to-all-done = f32[8,12,128]{2,1,0:T(8,128)S(1)} async-done(((f32[8,12,128]{2,1,0:T(8,128)}), f32[8,12,128]{2,1,0:T(8,128)S(1)}, u32[]{:S(2)}, u32[]{:S(2)}) %all-to-all-start) | async-done | bytes 49184 | tf_op jit(solution)/shard_map/all_to_all | solution.py:389
  24.7 10.3 %all-to-all-start.1 = ((f32[8,24,128]{2,1,0:T(8,128)}), f32[8,24,128]{2,1,0:T(8,128)S(1)}, u32[]{:S(2)}, u32[]{:S(2)}) async-start(f32[8,24,128]{2,1,0:T(8,128)} %broadcast_in_dim.116), calls=%async_computation.1 | async-start | bytes 196608 | tf_op jit(solution)/shard_map/all_to_all | solution.py:389
  35.1 9.8 %all-to-all-done.1 = f32[8,24,128]{2,1,0:T(8,128)S(1)} async-done(((f32[8,24,128]{2,1,0:T(8,128)}), f32[8,24,128]{2,1,0:T(8,128)S(1)}, u32[]{:S(2)}, u32[]{:S(2)}) %all-to-all-start.1) | async-done | bytes 98336 | tf_op jit(solution)/shard_map/all_to_all | solution.py:389
  46.0 4.8 %all-to-all-start.2 = ((f32[8,200,128]{2,1,0:T(8,128)}), f32[8,200,128]{2,1,0:T(8,128)S(1)}, u32[]{:S(2)}, u32[]{:S(2)}) async-start(f32[8,200,128]{2,1,0:T(8,128)} %broadcast_in_dim.118), calls=%async_computation.2 | async-start | bytes 1638400 | tf_op jit(solution)/shard_map/all_to_all | solution.py:389
  55.1 7.8 %all-to-all-done.2 = f32[8,200,128]{2,1,0:T(8,128)S(1)} async-done(((f32[8,200,128]{2,1,0:T(8,128)}), f32[8,200,128]{2,1,0:T(8,128)S(1)}, u32[]{:S(2)}, u32[]{:S(2)}) %all-to-all-start.2) | async-done | bytes 819232 | tf_op jit(solution)/shard_map/all_to_all | solution.py:389
  63.9 18.0 %line_basis.1.basis = bf16[8,512,2048]{2,1,0:T(8,128)(2,1)} custom-call(s32[128]{0:T(128)} %get-tuple-element.68.rows_at, s32[512]{0:T(512)} %reshape.208.listed, f32[1600,128]{1,0:T(8,128)} %bitcast.35, f32[8,128,12]{2,1,0:T(8,128)} %bitcast.40), custom_call_target="tpu_custom_call" | custom-call | flops 419430400 | tf_op jit(solution)/shard_map/line_basis/pallas_call | solution.py:71
  82.6 11.5 %all-gather.3.cloned.1.call-done = bf16[24576,128]{1,0:T(8,128)(2,1)} async-done(((bf16[3072,128]{1,0:T(8,128)(2,1)}), bf16[24576,128]{1,0:T(8,128)(2,1)}) %all-gather.3.cloned.1.call-update) | async-done | bytes 6291472 | tf_op jit(solution)/shard_map/all_gather | solution.py:449
  94.0 12.3 %line_field.1 = f32[8,512,128]{2,1,0:T(8,128)} custom-call(s32[128]{0:T(128)} %get-tuple-element.69.tiles_at, bf16[192,128,128]{2,1,0:T(8,128)(2,1)} %bitcast.38, bf16[8,512,2048]{2,1,0:T(8,128)(2,1)} %line_basis.1.basis), custom_call_target="tpu_custom_call" | custom-call | flops 2147483648 | tf_op jit(solution)/shard_map/line_field/pallas_call | solution.py:101
  114.1 19.3 %basis_at_owner.1 = (bf16[64,256,256]{2,1,0:T(8,128)(2,1)}, bf16[64,256,256]{2,1,0:T(8,128)(2,1)}) custom-call(s32[128]{0:T(128)} %select_n.59.pick, s32[512]{0:T(512)} %reshape.209.listed, s32[64]{0:T(128)} %add.106.points_at, f32[3072,4]{1,0:T(8,128)} %bitcast.37, f32[1600,128]{1,0:T(8,128)} %bitcast.36), custom_call_target="tpu_custom_call" | custom-call | flops 419430400 | tf_op jit(solution)/shard_map/basis_at_owner/pallas_call | solution.py:280
  134.8 14.4 %pair_values.1.values = f32[4,128,2048]{2,1,0:T(8,128)} custom-call(s32[4,1,2048]{2,1,0:T(1,128)} %broadcast_in_dim.63.target, s32[4,1,2048]{2,1,0:T(1,128)} %broadcast_in_dim.64.source, bf16[16,1024]{1,0:T(8,128)(2,1)} %maximum_maximum_fusion.1.window, bf16[16,128]{1,0:T(8,128)(2,1)} %maximum_maximum_fusion.2.local, f32[4,128,3]{2,1,0:T(8,128)} %bitcast.41), custom_call_target="tpu_custom_call" | custom-call | flops 419430400 | tf_op jit(solution)/shard_map/pair_values/pallas_call | solution.py:168
  149.4 9.8 %potential_parts.1 = (f32[8,4,128,128]{3,2,1,0:T(8,128)}, f32[4,8,128]{2,1,0:T(8,128)}) custom-call(f32[4,128,128]{2,1,0:T(8,128)} %bitcast.58, f32[4,128,2048]{2,1,0:T(8,128)} %pair_values.1.values, s32[4,1,2048]{2,1,0:T(1,128)} %broadcast_in_dim.63.target, s32[4,1,2048]{2,1,0:T(1,128)} %broadcast_in_dim.64.source), custom_call_target="tpu_custom_call" | custom-call | flops 2147483648 | tf_op jit(solution)/shard_map/potential_parts/pallas_call | solution.py:212
  162.6 21.0 %all_to_all.25 = f16[8,4,144,128]{3,2,1,0:T(8,128)(2,1)S(1)} all-to-all(f16[8,4,144,128]{3,2,1,0:T(8,128)(2,1)S(1)} %pad_maximum_fusion), channel_id=1, replica_groups=mesh['y'=8,'z'=8,'col'=8] {'col'}, dimensions={0} | all-to-all | bytes 2359296 | tf_op jit(solution)/shard_map/all_to_all | solution.py:409
  185.1 24.9 %all_to_all.26.refs_1_ = bf16[8,256,128]{2,1,0:T(8,128)(2,1)S(1)} all-to-all(bf16[8,256,128]{2,1,0:T(8,128)(2,1)S(1)} %broadcast_in_dim.123), channel_id=1, replica_groups=mesh['y'=8,'z'=8,'col'=8] {'z'}, dimensions={0} | all-to-all | bytes 1048576 | tf_op jit(solution)/shard_map/all_to_all | solution.py:389
  210.0 3.4 %collective-permute-start = (bf16[8,256,128]{2,1,0:T(8,128)(2,1)S(1)}, bf16[8,256,128]{2,1,0:T(8,128)(2,1)S(1)}, u32[]{:S(2)}, u32[]{:S(2)}) collective-permute-start(bf16[8,256,128]{2,1,0:T(8,128)(2,1)S(1)} %all_to_all.26.refs_1_), channel_id=1, source_target_pairs={{0,64},{64,128},{128,192},{192,256},{256,320},{320,384},{384,448},... | collective-permute-start | bytes 1572872 | tf_op jit(solution)/shard_map/ppermute | solution.py:530
  213.4 3.7 %collective-permute-start.1 = (bf16[8,256,128]{2,1,0:T(8,128)(2,1)S(1)}, bf16[8,256,128]{2,1,0:T(8,128)(2,1)S(1)}, u32[]{:S(2)}, u32[]{:S(2)}) collective-permute-start(bf16[8,256,128]{2,1,0:T(8,128)(2,1)S(1)} %all_to_all.26.refs_1_), channel_id=1, source_target_pairs={{0,448},{64,0},{128,64},{192,128},{256,192},{320,256},{384,320},{4... | collective-permute-start | bytes 1572872 | tf_op jit(solution)/shard_map/ppermute | solution.py:532
  217.6 3.7 %fock_from_lines.5.refs_4_ = f32[24,128,128]{2,1,0:T(8,128)} custom-call(s32[128]{0:T(128)} %select_n.59.pick, s32[8]{0:T(128)} %add_and_fusion.lines, bf16[64,256,256]{2,1,0:T(8,128)(2,1)} %get-tuple-element.35.refs_0_.refs_1_, bf16[8,256,128]{2,1,0:T(8,128)(2,1)} %copy-done.1), custom_call_target="tpu_custom_call" | custom-call | flops 134217728 | tf_op jit(solution)/shard_map/fock_from_lines/pallas_call | solution.py:368
  221.3 4.7 %collective-permute-done.refs_2_ = bf16[8,256,128]{2,1,0:T(8,128)(2,1)S(1)} collective-permute-done((bf16[8,256,128]{2,1,0:T(8,128)(2,1)S(1)}, bf16[8,256,128]{2,1,0:T(8,128)(2,1)S(1)}, u32[]{:S(2)}, u32[]{:S(2)}) %collective-permute-start) | collective-permute-done | bytes 524320 | tf_op jit(solution)/shard_map/ppermute | solution.py:530
  227.5 3.5 %collective-permute-start.2 = (bf16[8,256,128]{2,1,0:T(8,128)(2,1)S(1)}, bf16[8,256,128]{2,1,0:T(8,128)(2,1)S(1)}, u32[]{:S(2)}, u32[]{:S(2)}) collective-permute-start(bf16[8,256,128]{2,1,0:T(8,128)(2,1)S(1)} %collective-permute-done.refs_2_), channel_id=1, source_target_pairs={{0,64},{64,128},{128,192},{192,256},{256,320},{320,384},{384,448},... | collective-permute-start | bytes 1572872 | tf_op jit(solution)/shard_map/ppermute | solution.py:530
  230.9 3.8 %collective-permute-start.3 = (bf16[8,256,128]{2,1,0:T(8,128)(2,1)S(1)}, bf16[8,256,128]{2,1,0:T(8,128)(2,1)S(1)}, u32[]{:S(2)}, u32[]{:S(2)}) collective-permute-start(bf16[8,256,128]{2,1,0:T(8,128)(2,1)S(1)} %collective-permute-done.1.refs_3_), channel_id=1, source_target_pairs={{0,448},{64,0},{128,64},{192,128},{256,192},{320,256},{384,320},{4... | collective-permute-start | bytes 1572872 | tf_op jit(solution)/shard_map/ppermute | solution.py:532
  234.7 4.9 %fock_from_lines.6.refs_4_ = f32[24,128,128]{2,1,0:T(8,128)} custom-call(s32[128]{0:T(128)} %select_n.59.pick, s32[8]{0:T(128)} %add_and_fusion.lines, bf16[64,256,256]{2,1,0:T(8,128)(2,1)} %get-tuple-element.35.refs_0_.refs_1_, bf16[64,256,256]{2,1,0:T(8,128)(2,1)} %get-tuple-element.35.refs_0_.refs_1_, ...), custom_call_target="tpu_custom_call", output_to_operand_aliasing={{}: (6, {})} | custom-call | flops 268435456 | tf_op jit(solution)/shard_map/fock_from_lines/pallas_call | solution.py:368
  239.6 2.9 collective-permute-done.2.refs_2_
  242.5 7.0 %collective-permute-done.3.refs_3_ = bf16[8,256,128]{2,1,0:T(8,128)(2,1)S(1)} collective-permute-done((bf16[8,256,128]{2,1,0:T(8,128)(2,1)S(1)}, bf16[8,256,128]{2,1,0:T(8,128)(2,1)S(1)}, u32[]{:S(2)}, u32[]{:S(2)}) %collective-permute-start.3) | collective-permute-done | bytes 524320 | tf_op jit(solution)/shard_map/ppermute | solution.py:532
  249.5 2.3 collective-permute-start.4
  251.8 5.2 %collective-permute-start.5 = (bf16[8,256,128]{2,1,0:T(8,128)(2,1)S(1)}, bf16[8,256,128]{2,1,0:T(8,128)(2,1)S(1)}, u32[]{:S(2)}, u32[]{:S(2)}) collective-permute-start(bf16[8,256,128]{2,1,0:T(8,128)(2,1)S(1)} %collective-permute-done.3.refs_3_), channel_id=1, source_target_pairs={{0,448},{64,0},{128,64},{192,128},{256,192},{320,256},{384,320},{4... | collective-permute-start | bytes 1572872 | tf_op jit(solution)/shard_map/ppermute | solution.py:532
  257.0 5.0 %fock_from_lines.7.refs_4_ = f32[24,128,128]{2,1,0:T(8,128)} custom-call(s32[128]{0:T(128)} %select_n.59.pick, s32[8]{0:T(128)} %add_and_fusion.lines, bf16[64,256,256]{2,1,0:T(8,128)(2,1)} %get-tuple-element.35.refs_0_.refs_1_, bf16[64,256,256]{2,1,0:T(8,128)(2,1)} %get-tuple-element.35.refs_0_.refs_1_, ...), custom_call_target="tpu_custom_call", output_to_operand_aliasing={{}: (6, {})} | custom-call | flops 268435456 | tf_op jit(solution)/shard_map/fock_from_lines/pallas_call | solution.py:368
  262.0 12.9 %collective-permute-done.4.refs_2_ = bf16[8,256,128]{2,1,0:T(8,128)(2,1)S(1)} collective-permute-done((bf16[8,256,128]{2,1,0:T(8,128)(2,1)S(1)}, bf16[8,256,128]{2,1,0:T(8,128)(2,1)S(1)}, u32[]{:S(2)}, u32[]{:S(2)}) %collective-permute-start.4) | collective-permute-done | bytes 524320 | tf_op jit(solution)/shard_map/ppermute | solution.py:530
  274.9 2.4 collective-permute-start.6
  277.3 4.9 %fock_from_lines.8.refs_2_ = f32[24,128,128]{2,1,0:T(8,128)} custom-call(s32[128]{0:T(128)} %select_n.59.pick, s32[8]{0:T(128)} %add_and_fusion.lines, bf16[64,256,256]{2,1,0:T(8,128)(2,1)} %get-tuple-element.35.refs_0_.refs_1_, bf16[64,256,256]{2,1,0:T(8,128)(2,1)} %get-tuple-element.35.refs_0_.refs_1_, ...), custom_call_target="tpu_custom_call", output_to_operand_aliasing={{}: (6, {})} | custom-call | flops 268435456 | tf_op jit(solution)/shard_map/fock_from_lines/pallas_call | solution.py:368
  282.2 5.0 %collective-permute-done.6.refs_1_ = bf16[8,256,128]{2,1,0:T(8,128)(2,1)S(1)} collective-permute-done((bf16[8,256,128]{2,1,0:T(8,128)(2,1)S(1)}, bf16[8,256,128]{2,1,0:T(8,128)(2,1)S(1)}, u32[]{:S(2)}, u32[]{:S(2)}) %collective-permute-start.6) | collective-permute-done | bytes 524320 | tf_op jit(solution)/shard_map/ppermute | solution.py:530
  288.0 4.2 %fock_from_lines.9.before = f32[24,128,128]{2,1,0:T(8,128)} custom-call(s32[128]{0:T(128)} %select_n.59.pick, s32[8]{0:T(128)} %add_and_fusion.lines, bf16[64,256,256]{2,1,0:T(8,128)(2,1)} %get-tuple-element.35.refs_0_.refs_1_, bf16[8,256,128]{2,1,0:T(8,128)(2,1)} %copy-done.2, f32[24,128,128]{2,1,0:T(8,128)} %fock_from_lines.8.refs_2_), custom_call_target="tpu_custom_call", output_to_operand_aliasing={{}: (4, {})} | custom-call | flops 134217728 | tf_op jit(solution)/shard_map/fock_from_lines/pallas_call | solution.py:368
  292.2 9.3 %fock_from_gather.1 = f32[24,128,128]{2,1,0:T(8,128)} custom-call(s32[128]{0:T(128)} %select_n.59.pick, bf16[64,256,256]{2,1,0:T(8,128)(2,1)} %get-tuple-element.30.basis, bf16[64,256,128]{2,1,0:T(8,128)(2,1)} %bitcast.39, f32[24,128,128]{2,1,0:T(8,128)} %fock_from_lines.9.before), custom_call_target="tpu_custom_call", output_to_operand_aliasing={{}: (3, {})} | custom-call | flops 1073741824 | tf_op jit(solution)/shard_map/fock_from_gather/pallas_call | solution.py:322
  (130 shorter events, 30.3 us)
Async XLA Ops:
  6.5 38.4 %copy-start.17 = (f32[128]{0:T(128)S(1)}, f32[128]{0:T(128)}, u32[]{:S(2)}) copy-start(f32[128]{0:T(128)} %param.15) | copy-start | bytes 1540
  6.5 38.4 %copy-start.15 = (f32[3,128]{1,0:T(4,128)S(1)}, f32[3,128]{1,0:T(4,128)}, u32[]{:S(2)}) copy-start(f32[3,128]{1,0:T(4,128)} %param.14) | copy-start | bytes 4612
  6.5 87.5 %all-gather.3.cloned.1.call-start = ((), (), s32[]{:S(2)}) async-start(), calls=%async_computation.6 | async-start | bytes 7077888 | tf_op jit(solution)/shard_map/all_gather | solution.py:449
  8.6 15.5 %all-to-all-start = ((f32[8,12,128]{2,1,0:T(8,128)}), f32[8,12,128]{2,1,0:T(8,128)S(1)}, u32[]{:S(2)}, u32[]{:S(2)}) async-start(f32[8,12,128]{2,1,0:T(8,128)} %broadcast_in_dim.115), calls=%async_computation | async-start | bytes 131072 | tf_op jit(solution)/shard_map/all_to_all | solution.py:389
  24.7 20.2 %all-to-all-start.1 = ((f32[8,24,128]{2,1,0:T(8,128)}), f32[8,24,128]{2,1,0:T(8,128)S(1)}, u32[]{:S(2)}, u32[]{:S(2)}) async-start(f32[8,24,128]{2,1,0:T(8,128)} %broadcast_in_dim.116), calls=%async_computation.1 | async-start | bytes 196608 | tf_op jit(solution)/shard_map/all_to_all | solution.py:389
  46.0 16.8 %all-to-all-start.2 = ((f32[8,200,128]{2,1,0:T(8,128)}), f32[8,200,128]{2,1,0:T(8,128)S(1)}, u32[]{:S(2)}, u32[]{:S(2)}) async-start(f32[8,200,128]{2,1,0:T(8,128)} %broadcast_in_dim.118), calls=%async_computation.2 | async-start | bytes 1638400 | tf_op jit(solution)/shard_map/all_to_all | solution.py:389
  50.9 98.6 %reduce-scatter.2.cloned.1.call-start = ((), (), s32[]{:S(2)}) async-start(), calls=%async_computation.7 | async-start | bytes 2359296 | tf_op jit(solution)/shard_map/reduce_scatter | solution.py:508
  62.9 1.0 copy-start
  106.3 0.7 copy-start.14
  106.3 1.5 copy-start.10
  106.3 4.8 %copy-start.9 = (f32[3,3072]{1,0:T(4,128)S(1)}, f32[3,3072]{1,0:T(4,128)}, u32[]{:S(2)}) copy-start(f32[3,3072]{1,0:T(4,128)} %param.12) | copy-start | bytes 110596
  106.3 4.8 %copy-start.11 = (f32[3072]{0:T(1024)S(1)}, f32[3072]{0:T(1024)}, u32[]{:S(2)}) copy-start(f32[3072]{0:T(1024)} %param.13) | copy-start | bytes 36868
  106.3 6.4 %copy-start.12 = (s32[4,2048]{1,0:T(4,128)S(1)}, s32[4,2048]{1,0:T(4,128)}, u32[]{:S(2)}) copy-start(s32[4,2048]{1,0:T(4,128)} %param.19) | copy-start | bytes 98308
  106.4 7.0 %copy-start.13 = (s32[4,2048]{1,0:T(4,128)S(1)}, s32[4,2048]{1,0:T(4,128)}, u32[]{:S(2)}) copy-start(s32[4,2048]{1,0:T(4,128)} %param.20) | copy-start | bytes 98308
  106.4 185.8 %all-gather.5.cloned.1.call-start = ((), (), s32[]{:S(2)}) async-start(), calls=%async_computation.8 | async-start | bytes 4259840 | tf_op jit(solution)/shard_map/all_gather | solution.py:519
  162.6 21.6 %copy-start.16 = (f32[4,128]{1,0:T(4,128)S(1)}, f32[4,128]{1,0:T(4,128)}, u32[]{:S(2)}) copy-start(f32[4,128]{1,0:T(4,128)} %param.17) | copy-start | bytes 6148
  183.6 33.5 %copy-start.18 = (s32[8]{0:T(128)S(1)}, s32[8]{0:T(128)}, u32[]{:S(2)}) copy-start(s32[8]{0:T(128)} %constant.90.clone) | copy-start | bytes 100
  210.0 7.6 %copy-start.1 = (bf16[8,256,128]{2,1,0:T(8,128)(2,1)}, bf16[8,256,128]{2,1,0:T(8,128)(2,1)S(1)}, u32[]{:S(2)}) copy-start(bf16[8,256,128]{2,1,0:T(8,128)(2,1)S(1)} %all_to_all.26.refs_1_) | copy-start | bytes 1572868
  210.0 15.9 %collective-permute-start = (bf16[8,256,128]{2,1,0:T(8,128)(2,1)S(1)}, bf16[8,256,128]{2,1,0:T(8,128)(2,1)S(1)}, u32[]{:S(2)}, u32[]{:S(2)}) collective-permute-start(bf16[8,256,128]{2,1,0:T(8,128)(2,1)S(1)} %all_to_all.26.refs_1_), channel_id=1, source_target_pairs={{0,64},{64,128},{128,192},{192,256},{256,320},{320,384},{384,448},... | collective-permute-start | bytes 1572872 | tf_op jit(solution)/shard_map/ppermute | solution.py:530
  213.4 14.1 %collective-permute-start.1 = (bf16[8,256,128]{2,1,0:T(8,128)(2,1)S(1)}, bf16[8,256,128]{2,1,0:T(8,128)(2,1)S(1)}, u32[]{:S(2)}, u32[]{:S(2)}) collective-permute-start(bf16[8,256,128]{2,1,0:T(8,128)(2,1)S(1)} %all_to_all.26.refs_1_), channel_id=1, source_target_pairs={{0,448},{64,0},{128,64},{192,128},{256,192},{320,256},{384,320},{4... | collective-permute-start | bytes 1572872 | tf_op jit(solution)/shard_map/ppermute | solution.py:532
  225.9 8.8 %copy-start.3 = (bf16[8,256,128]{2,1,0:T(8,128)(2,1)}, bf16[8,256,128]{2,1,0:T(8,128)(2,1)S(1)}, u32[]{:S(2)}) copy-start(bf16[8,256,128]{2,1,0:T(8,128)(2,1)S(1)} %collective-permute-done.refs_2_) | copy-start | bytes 1572868
  227.5 7.3 %copy-start.4 = (bf16[8,256,128]{2,1,0:T(8,128)(2,1)}, bf16[8,256,128]{2,1,0:T(8,128)(2,1)S(1)}, u32[]{:S(2)}) copy-start(bf16[8,256,128]{2,1,0:T(8,128)(2,1)S(1)} %collective-permute-done.1.refs_3_) | copy-start | bytes 1572868
  227.5 15.0 %collective-permute-start.2 = (bf16[8,256,128]{2,1,0:T(8,128)(2,1)S(1)}, bf16[8,256,128]{2,1,0:T(8,128)(2,1)S(1)}, u32[]{:S(2)}, u32[]{:S(2)}) collective-permute-start(bf16[8,256,128]{2,1,0:T(8,128)(2,1)S(1)} %collective-permute-done.refs_2_), channel_id=1, source_target_pairs={{0,64},{64,128},{128,192},{192,256},{256,320},{320,384},{384,448},... | collective-permute-start | bytes 1572872 | tf_op jit(solution)/shard_map/ppermute | solution.py:530
  230.9 18.6 %collective-permute-start.3 = (bf16[8,256,128]{2,1,0:T(8,128)(2,1)S(1)}, bf16[8,256,128]{2,1,0:T(8,128)(2,1)S(1)}, u32[]{:S(2)}, u32[]{:S(2)}) collective-permute-start(bf16[8,256,128]{2,1,0:T(8,128)(2,1)S(1)} %collective-permute-done.1.refs_3_), channel_id=1, source_target_pairs={{0,448},{64,0},{128,64},{192,128},{256,192},{320,256},{384,320},{4... | collective-permute-start | bytes 1572872 | tf_op jit(solution)/shard_map/ppermute | solution.py:532
  242.5 14.5 %copy-start.5 = (bf16[8,256,128]{2,1,0:T(8,128)(2,1)}, bf16[8,256,128]{2,1,0:T(8,128)(2,1)S(1)}, u32[]{:S(2)}) copy-start(bf16[8,256,128]{2,1,0:T(8,128)(2,1)S(1)} %collective-permute-done.2.refs_2_) | copy-start | bytes 1572868
  249.5 7.5 %copy-start.6 = (bf16[8,256,128]{2,1,0:T(8,128)(2,1)}, bf16[8,256,128]{2,1,0:T(8,128)(2,1)S(1)}, u32[]{:S(2)}) copy-start(bf16[8,256,128]{2,1,0:T(8,128)(2,1)S(1)} %collective-permute-done.3.refs_3_) | copy-start | bytes 1572868
  249.5 25.4 %collective-permute-start.4 = (bf16[8,256,128]{2,1,0:T(8,128)(2,1)S(1)}, bf16[8,256,128]{2,1,0:T(8,128)(2,1)S(1)}, u32[]{:S(2)}, u32[]{:S(2)}) collective-permute-start(bf16[8,256,128]{2,1,0:T(8,128)(2,1)S(1)} %collective-permute-done.2.refs_2_), channel_id=1, source_target_pairs={{0,64},{64,128},{128,192},{192,256},{256,320},{320,384},{384,448},... | collective-permute-start | bytes 1572872 | tf_op jit(solution)/shard_map/ppermute | solution.py:530
  251.8 23.1 %collective-permute-start.5 = (bf16[8,256,128]{2,1,0:T(8,128)(2,1)S(1)}, bf16[8,256,128]{2,1,0:T(8,128)(2,1)S(1)}, u32[]{:S(2)}, u32[]{:S(2)}) collective-permute-start(bf16[8,256,128]{2,1,0:T(8,128)(2,1)S(1)} %collective-permute-done.3.refs_3_), channel_id=1, source_target_pairs={{0,448},{64,0},{128,64},{192,128},{256,192},{320,256},{384,320},{4... | collective-permute-start | bytes 1572872 | tf_op jit(solution)/shard_map/ppermute | solution.py:532
  274.9 2.4 copy-start.7
  274.9 2.4 copy-start.8
  274.9 12.3 %collective-permute-start.6 = (bf16[8,256,128]{2,1,0:T(8,128)(2,1)S(1)}, bf16[8,256,128]{2,1,0:T(8,128)(2,1)S(1)}, u32[]{:S(2)}, u32[]{:S(2)}) collective-permute-start(bf16[8,256,128]{2,1,0:T(8,128)(2,1)S(1)} %collective-permute-done.4.refs_2_), channel_id=1, source_target_pairs={{0,64},{64,128},{128,192},{192,256},{256,320},{320,384},{384,448},... | collective-permute-start | bytes 1572872 | tf_op jit(solution)/shard_map/ppermute | solution.py:530
  287.2 0.8 copy-start.2
Sparse Core Ops, SparseCore 0:
  9.4 84.5 all-gather.2
  106.5 42.8 reduce-scatter.1
  185.1 90.4 all-gather.4

commit v6 on v4

--- a/solution.py
+++ b/solution.py
@@ -14,7 +14,7 @@
 PARAMS = 4
 CHUNK = 512
 STEP_OWNERS = 4
-SCALE_ROWS = 16
+SCALE_ROWS = 8
 STEP_GATHERED = 16
 STEP_PLACES = 2
 GRID = ("y", "z")
@@ -185,7 +185,7 @@
     )(target, source, window, local, points_t)
 
 
-def potential_kernel(field, values, target, source, out, largest):
+def potential_kernel(field, values, target, source, out):
     columns, width = out.shape[0], out.shape[3]
     window_count = columns * width
     rounded = field[0].astype(BF16)
@@ -200,9 +200,13 @@
             (((1,), (1,)), ((), ())),
             preferred_element_type=F32,
         )
+    largest = jnp.max(jnp.abs(potential), keepdims=True)
+    power = jnp.clip(13.0 - jnp.ceil(jnp.log2(largest)), -100.0, 100.0)
+    scaled = potential * jnp.exp2(power)
+    pts = potential.shape[0]
     for column in range(columns):
-        out[column, 0] = potential[:, column * width : (column + 1) * width]
-    largest[0] = jnp.broadcast_to(jnp.max(jnp.abs(potential), keepdims=True), largest.shape[1:])
+        out[column, 0, :pts] = scaled[:, column * width : (column + 1) * width]
+        out[column, 0, pts:] = jnp.broadcast_to(power, (SCALE_ROWS, width))
 
 
 def potential_parts(field, values, target, source, columns):
@@ -221,15 +225,9 @@
                 pl.BlockSpec((1, 1, pairs), lambda b: (b, 0, 0)),
                 pl.BlockSpec((1, 1, pairs), lambda b: (b, 0, 0)),
             ],
-            out_specs=[
-                pl.BlockSpec((columns, 1, pts, width), lambda b: (0, b, 0, 0)),
-                pl.BlockSpec((1, 8, BLK), lambda b: (b, 0, 0)),
-            ],
-        ),
-        out_shape=[
-            jax.ShapeDtypeStruct((columns, batches, pts, width), F32),
-            jax.ShapeDtypeStruct((batches, 8, BLK), F32),
-        ],
+            out_specs=pl.BlockSpec((columns, 1, pts + SCALE_ROWS, width), lambda b: (0, b, 0, 0)),
+        ),
+        out_shape=jax.ShapeDtypeStruct((columns, batches, pts + SCALE_ROWS, width), F32),
     )(field, values, target, source)
 
 
@@ -341,15 +339,10 @@
     return parts.astype(BF16)
 
 
-def sum_at_column(parts, largest):
-    columns, batches, pts, width = parts.shape
-    power = jnp.clip(13.0 - jnp.ceil(jnp.log2(largest)), -100.0, 100.0)
-    scaled = (parts * jnp.exp2(power)[None, :, None, None]).astype(jnp.float16)
-    tail = jnp.broadcast_to(
-        power[None, :, None, None], (columns, batches, SCALE_ROWS, width)
-    ).astype(jnp.float16)
+def sum_at_column(parts):
+    pts = parts.shape[2] - SCALE_ROWS
     got = lax.all_to_all(
-        jnp.concatenate([scaled, tail], axis=2), "col", split_axis=0, concat_axis=0, tiled=True
+        parts.astype(jnp.float16), "col", split_axis=0, concat_axis=0, tiled=True
     )
     factor = jnp.exp2(-got[:, :, pts : pts + 1, 0:1].astype(F32))
     return jnp.sum(got[:, :, :pts].astype(F32) * factor, axis=0)
@@ -449,10 +442,10 @@
     )
     field = lax.psum_scatter(share.reshape(-1, width), "y", scatter_dimension=0, tiled=True)
     values = pair_values(target, source, in_parts(whole_window), in_parts(local_window), points_t)
-    parts, largest = potential_parts(
+    parts = potential_parts(
         field.reshape(batches, pts, width), values, target, source, columns
     )
-    potential = sum_at_column(parts, largest[:, 0, 0])
+    potential = sum_at_column(parts)
     weighted = (weights[:, :, None] * potential).astype(BF16).reshape(batches * pts, width)
 
     all_weighted = lax.all_gather(weighted, GRID, axis=0, tiled=True)

time: 303 us -> 301 us (level)
  no operation moved by 1% of the time
where the time goes in v6:
time: 301 us; the launch traced here: 299 us
  waiting for transfers between devices  124 us (41%)
  Pallas kernels  86.7 us (29%)
  starting transfers between devices  25.6 us (9%)
  blocking collectives  25.4 us (8%)
  local copies, waits for them, and re-layouts  16.7 us (6%)
  between operations  13.4 us (4%)
  other arithmetic  8.3 us (3%)
    all_gather x1, waiting for transfers between devices, on_device(): all_weighted = lax.all_gather(weighted, GRID, axis=0, tiled=True)  71.9 us
    all_to_all x3, starting transfers between devices, to_everyone(): lax.all_to_all(jnp.broadcast_to(value[None], (devices, *value.shape)), ax...  25.5 us
    all_to_all x1, blocking collectives, sum_at_column(): lax.all_to_all(parts.astype(jnp.float16), 'col', split_axis=0, concat_axi...  25.4 us
    all_to_all x3, waiting for transfers between devices, to_everyone(): lax.all_to_all(jnp.broadcast_to(value[None], (devices, *value.shape)), ax...  20.4 us
    reduce_scatter x1, waiting for transfers between devices, on_device(): lax.psum_scatter(share.reshape(-1, width), 'y', scatter_dimension=0, tile...  20.3 us
    pallas_call x1, Pallas kernels, basis_at_owner(): call(functools.partial(owner_basis_kernel, batches=batches), 'basis_at_ow...  19.4 us
    pallas_call x1, Pallas kernels, line_basis(): call(functools.partial(line_basis_kernel, batches=batches, slots=slots),...  18.4 us
    pallas_call x1, Pallas kernels, pair_values(): call(pair_kernel, 'pair_values', flops=batches * pairs * pts * 400, grid_...  14.4 us
  transfers between devices with their start and end apart: 6, of which 6 were waited for; matrix products, arithmetic and copies ran while one was open for 7% of the time, Pallas kernels for 17%

profile of v6, /device:TPU:1, one launch (start us, length us, event | category | flops | bytes accessed | tf_op | source)
XLA Modules:
  0.0 299.5 jit_solution(2687146561682242592)
XLA Ops:
  6.5 0.7 all-gather.3.cloned.1.call-update
  7.3 0.7 broadcast_in_dim.94
  8.6 7.6 %all-to-all-start = ((f32[8,12,128]{2,1,0:T(8,128)}), f32[8,12,128]{2,1,0:T(8,128)S(1)}, u32[]{:S(2)}, u32[]{:S(2)}) async-start(f32[8,12,128]{2,1,0:T(8,128)} %broadcast_in_dim.95), calls=%async_computation | async-start | bytes 131072 | tf_op jit(solution)/shard_map/all_to_all | solution.py:329
  16.2 0.9 copy.71
  18.9 0.8 maximum_bitcast_fusion
  20.1 3.4 %all-to-all-done = f32[8,12,128]{2,1,0:T(8,128)S(1)} async-done(((f32[8,12,128]{2,1,0:T(8,128)}), f32[8,12,128]{2,1,0:T(8,128)S(1)}, u32[]{:S(2)}, u32[]{:S(2)}) %all-to-all-start) | async-done | bytes 49184 | tf_op jit(solution)/shard_map/all_to_all | solution.py:329
  24.1 10.0 %all-to-all-start.1 = ((f32[8,24,128]{2,1,0:T(8,128)}), f32[8,24,128]{2,1,0:T(8,128)S(1)}, u32[]{:S(2)}, u32[]{:S(2)}) async-start(f32[8,24,128]{2,1,0:T(8,128)} %broadcast_in_dim.96), calls=%async_computation.1 | async-start | bytes 196608 | tf_op jit(solution)/shard_map/all_to_all | solution.py:329
  34.2 8.7 %all-to-all-done.1 = f32[8,24,128]{2,1,0:T(8,128)S(1)} async-done(((f32[8,24,128]{2,1,0:T(8,128)}), f32[8,24,128]{2,1,0:T(8,128)S(1)}, u32[]{:S(2)}, u32[]{:S(2)}) %all-to-all-start.1) | async-done | bytes 98336 | tf_op jit(solution)/shard_map/all_to_all | solution.py:329
  43.0 0.9 broadcast_in_dim.98
  44.0 7.8 %all-to-all-start.2 = ((f32[8,200,128]{2,1,0:T(8,128)}), f32[8,200,128]{2,1,0:T(8,128)S(1)}, u32[]{:S(2)}, u32[]{:S(2)}) async-start(f32[8,200,128]{2,1,0:T(8,128)} %broadcast_in_dim.98), calls=%async_computation.2 | async-start | bytes 1638400 | tf_op jit(solution)/shard_map/all_to_all | solution.py:329
  51.8 1.3 and_reduce_fusion
  53.3 0.7 reshape.188.listed
  55.0 1.0 copy.76
  56.0 8.3 %all-to-all-done.2 = f32[8,200,128]{2,1,0:T(8,128)S(1)} async-done(((f32[8,200,128]{2,1,0:T(8,128)}), f32[8,200,128]{2,1,0:T(8,128)S(1)}, u32[]{:S(2)}, u32[]{:S(2)}) %all-to-all-start.2) | async-done | bytes 819232 | tf_op jit(solution)/shard_map/all_to_all | solution.py:329
  64.3 0.9 copy-done
  65.3 18.4 %line_basis.1.basis = bf16[8,512,2048]{2,1,0:T(8,128)(2,1)} custom-call(s32[128]{0:T(128)} %get-tuple-element.30.rows_at, s32[512]{0:T(512)} %reshape.188.listed, f32[1600,128]{1,0:T(8,128)} %bitcast.39, f32[8,128,12]{2,1,0:T(8,128)} %bitcast.43), custom_call_target="tpu_custom_call" | custom-call | flops 419430400 | tf_op jit(solution)/shard_map/line_basis/pallas_call | solution.py:70
  83.7 0.8 slice_bitcast_fusion
  84.4 10.3 %all-gather.3.cloned.1.call-done = bf16[24576,128]{1,0:T(8,128)(2,1)} async-done(((bf16[3072,128]{1,0:T(8,128)(2,1)}), bf16[24576,128]{1,0:T(8,128)(2,1)}) %all-gather.3.cloned.1.call-update) | async-done | bytes 6291472 | tf_op jit(solution)/shard_map/all_gather | solution.py:384
  94.7 12.3 %line_field.1 = f32[8,512,128]{2,1,0:T(8,128)} custom-call(s32[128]{0:T(128)} %get-tuple-element.31.tiles_at, bf16[192,128,128]{2,1,0:T(8,128)(2,1)} %bitcast.42, bf16[8,512,2048]{2,1,0:T(8,128)(2,1)} %line_basis.1.basis), custom_call_target="tpu_custom_call" | custom-call | flops 2147483648 | tf_op jit(solution)/shard_map/line_field/pallas_call | solution.py:100
  107.7 0.9 copy.77
  111.2 14.4 %pair_values.1.values = f32[4,128,2048]{2,1,0:T(8,128)} custom-call(s32[4,1,2048]{2,1,0:T(1,128)} %broadcast_in_dim.103.target, s32[4,1,2048]{2,1,0:T(1,128)} %broadcast_in_dim.104.source, bf16[16,1024]{1,0:T(8,128)(2,1)} %maximum_maximum_fusion.1.window, bf16[16,128]{1,0:T(8,128)(2,1)} %maximum_maximum_fusion.2.local, f32[4,128,3]{2,1,0:T(8,128)} %bitcast.44), custom_call_target="tpu_custom_call" | custom-call | flops 419430400 | tf_op jit(solution)/shard_map/pair_values/pallas_call | solution.py:167
  125.7 20.3 %reduce-scatter.2.cloned.1.call-done = f32[512,128]{1,0:T(8,128)} async-done(((f32[4096,128]{1,0:T(8,128)}), f32[512,128]{1,0:T(8,128)}) %reduce-scatter.2.cloned.1.call-update) | async-done | bytes 262160 | tf_op jit(solution)/shard_map/reduce_scatter | solution.py:443
  145.9 10.0 %potential_parts.1 = f32[8,4,136,128]{3,2,1,0:T(8,128)} custom-call(f32[4,128,128]{2,1,0:T(8,128)} %bitcast.60, f32[4,128,2048]{2,1,0:T(8,128)} %pair_values.1.values, s32[4,1,2048]{2,1,0:T(1,128)} %broadcast_in_dim.103.target, s32[4,1,2048]{2,1,0:T(1,128)} %broadcast_in_dim.104.source), custom_call_target="tpu_custom_call" | custom-call | flops 2147483648 | tf_op jit(solution)/shard_map/potential_parts/pallas_call | solution.py:215
  155.9 1.8 convert_element_type.33
  157.8 25.4 %all_to_all.20 = f16[8,4,136,128]{3,2,1,0:T(8,128)(2,1)S(1)} all-to-all(f16[8,4,136,128]{3,2,1,0:T(8,128)(2,1)S(1)} %convert_element_type.33), channel_id=1, replica_groups=mesh['y'=8,'z'=8,'col'=8] {'col'}, dimensions={0} | all-to-all | bytes 2228224 | tf_op jit(solution)/shard_map/all_to_all | solution.py:344
  183.7 0.8 fusion
  185.5 0.7 reshape.187.listed
  186.4 0.7 select_n.59.pick
  187.9 1.7 copy.69
  189.5 19.4 %basis_at_owner.1.basis = bf16[64,256,512]{2,1,0:T(8,128)(2,1)} custom-call(s32[128]{0:T(128)} %select_n.59.pick, s32[512]{0:T(512)} %reshape.187.listed, s32[64]{0:T(128)} %add.90.points_at, f32[3072,4]{1,0:T(8,128)} %bitcast.41, f32[1600,128]{1,0:T(8,128)} %bitcast.40), custom_call_target="tpu_custom_call" | custom-call | flops 419430400 | tf_op jit(solution)/shard_map/basis_at_owner/pallas_call | solution.py:272
  209.0 71.9 %all-gather.5.cloned.1.call-done = bf16[32768,128]{1,0:T(8,128)(2,1)} async-done(((bf16[512,128]{1,0:T(8,128)(2,1)}), bf16[32768,128]{1,0:T(8,128)(2,1)}) %all-gather.5.cloned.1.call-update) | async-done | bytes 8388624 | tf_op jit(solution)/shard_map/all_gather | solution.py:451
  280.8 12.1 %fock_at_owner.1 = f32[24,128,128]{2,1,0:T(8,128)} custom-call(s32[128]{0:T(128)} %select_n.59.pick, bf16[64,256,512]{2,1,0:T(8,128)(2,1)} %basis_at_owner.1.basis, bf16[64,512,128]{2,1,0:T(8,128)(2,1)} %bitcast.37), custom_call_target="tpu_custom_call" | custom-call | flops 2147483648 | tf_op jit(solution)/shard_map/fock_at_owner/pallas_call | solution.py:310
  (85 shorter events, 10.5 us)
Async XLA Ops:
  6.5 36.4 %copy-start.9 = (f32[128]{0:T(128)S(1)}, f32[128]{0:T(128)}, u32[]{:S(2)}) copy-start(f32[128]{0:T(128)} %param.14) | copy-start | bytes 1540
  6.5 36.4 %copy-start.7 = (f32[3,128]{1,0:T(4,128)S(1)}, f32[3,128]{1,0:T(4,128)}, u32[]{:S(2)}) copy-start(f32[3,128]{1,0:T(4,128)} %param.13) | copy-start | bytes 4612
  6.5 88.2 %all-gather.3.cloned.1.call-start = ((), (), s32[]{:S(2)}) async-start(), calls=%async_computation.5 | async-start | bytes 7077888 | tf_op jit(solution)/shard_map/all_gather | solution.py:384
  8.6 14.9 %all-to-all-start = ((f32[8,12,128]{2,1,0:T(8,128)}), f32[8,12,128]{2,1,0:T(8,128)S(1)}, u32[]{:S(2)}, u32[]{:S(2)}) async-start(f32[8,12,128]{2,1,0:T(8,128)} %broadcast_in_dim.95), calls=%async_computation | async-start | bytes 131072 | tf_op jit(solution)/shard_map/all_to_all | solution.py:329
  24.1 18.8 %all-to-all-start.1 = ((f32[8,24,128]{2,1,0:T(8,128)}), f32[8,24,128]{2,1,0:T(8,128)S(1)}, u32[]{:S(2)}, u32[]{:S(2)}) async-start(f32[8,24,128]{2,1,0:T(8,128)} %broadcast_in_dim.96), calls=%async_computation.1 | async-start | bytes 196608 | tf_op jit(solution)/shard_map/all_to_all | solution.py:329
  44.0 20.3 %all-to-all-start.2 = ((f32[8,200,128]{2,1,0:T(8,128)}), f32[8,200,128]{2,1,0:T(8,128)S(1)}, u32[]{:S(2)}, u32[]{:S(2)}) async-start(f32[8,200,128]{2,1,0:T(8,128)} %broadcast_in_dim.98), calls=%async_computation.2 | async-start | bytes 1638400 | tf_op jit(solution)/shard_map/all_to_all | solution.py:329
  51.8 94.1 %reduce-scatter.2.cloned.1.call-start = ((), (), s32[]{:S(2)}) async-start(), calls=%async_computation.6 | async-start | bytes 2359296 | tf_op jit(solution)/shard_map/reduce_scatter | solution.py:443
  64.3 0.9 copy-start
  107.0 0.7 copy-start.6
  107.0 1.6 copy-start.4
  107.0 2.2 copy-start.5
  107.0 173.8 %all-gather.5.cloned.1.call-start = ((), (), s32[]{:S(2)}) async-start(), calls=%async_computation.7 | async-start | bytes 8519680 | tf_op jit(solution)/shard_map/all_gather | solution.py:451
  157.7 26.0 %copy-start.8 = (f32[4,128]{1,0:T(4,128)S(1)}, f32[4,128]{1,0:T(4,128)}, u32[]{:S(2)}) copy-start(f32[4,128]{1,0:T(4,128)} %param.16) | copy-start | bytes 6148
  157.7 26.8 %copy-start.2 = (s32[256,32]{0,1:T(8,128)S(1)}, s32[256,32]{0,1:T(8,128)}, u32[]{:S(2)}) copy-start(s32[256,32]{0,1:T(8,128)} %param.17) | copy-start | bytes 98308
  157.7 30.1 %copy-start.1 = (f32[3,3072]{1,0:T(4,128)S(1)}, f32[3,3072]{1,0:T(4,128)}, u32[]{:S(2)}) copy-start(f32[3,3072]{1,0:T(4,128)} %param.11) | copy-start | bytes 110596
  157.8 30.1 %copy-start.3 = (f32[3072]{0:T(1024)S(1)}, f32[3072]{0:T(1024)}, u32[]{:S(2)}) copy-start(f32[3072]{0:T(1024)} %param.12) | copy-start | bytes 36868
Sparse Core Ops, SparseCore 0:
  9.4 85.2 all-gather.2
  107.2 38.7 reduce-scatter.1
  184.7 96.1 all-gather.4
